TPU v7x, 32 devices: a whole 2x2x4 slice. The times are simulated.
32 devices in a mesh: level: 4 (over x, core), tile: 8 (over z, y).
Axes of the slice: x: 2, y: 2, z: 4, core: 2. Of those that a mesh axis runs over, the one named last changes fastest.
Arguments:
- queue_init: bfloat16 [4, 4, 4, 32, 128], P('level', None, None, 'tile'), may hold values from -6 to 6
- noise_frames: bfloat16 [2, 4, 4, 32, 128], P(None, None, None, 'tile'), may hold values from -6 to 6
- conv_first: bfloat16 [3, 3, 320, 4], replicated, may hold values from -1 to 1
- conv_second: bfloat16 [3, 3, 320, 320], replicated, may hold values from -0.109375 to 0.109375
- time_weight: bfloat16 [3, 320, 320], replicated, may hold values from -0.1875 to 0.1875
- out_proj: bfloat16 [4, 320], replicated, may hold values from -0.3125 to 0.3125
- keep_coef: float32 [2, 4, 4], replicated, may hold values from 0.6 to 1
- noise_coef: float32 [2, 4, 4], replicated, may hold values from 0.1 to 0.5
Outputs:
- queue_final: bfloat16 [4, 4, 4, 32, 128], P('level', None, None, 'tile')
All inputs are finite; a program needn't handle non-finite values.
Results may differ from a plain program's by a relative error of at most 0.0048.
Values may be sent and summed in bfloat16 or wider, within the bound.
No kernel may reach another device: no remote copies, remote signals or barrier semaphores. Data moves between devices by JAX's collectives and lax.ppermute only.
A program may use at most 64 MiB of HBM per device.

v0:
```python
import jax
import jax.numpy as jnp
from jax import lax
from jax.sharding import PartitionSpec as P

STEPS = 2


def with_halo(block, sides, width):
    for axis, dim in sides:
        count = lax.axis_size(axis)
        forward = [(i, i + 1) for i in range(count - 1)]
        backward = [(target, source) for source, target in forward]
        low = lax.ppermute(
            lax.slice_in_dim(block, block.shape[dim] - width, None, axis=dim), axis, forward
        )
        high = lax.ppermute(lax.slice_in_dim(block, 0, width, axis=dim), axis, backward)
        block = jnp.concatenate([low, block, high], axis=dim)
    return block


def shifted(value, axis, steps):
    count = lax.axis_size(axis)
    leading, last = (max(0, -steps), min(count, count - steps))
    return lax.ppermute(value, axis, [(source, source + steps) for source in range(leading, last)])


def conv_rows(extended, weight, row_count):
    padded = jnp.pad(extended, ((0, 0), (0, 0), (0, 0), (1, 1)))
    col_count = extended.shape[3]
    running = jnp.zeros((extended.shape[0], weight.shape[2], row_count, col_count), jnp.float32)
    for row_tap in range(3):
        for col_tap in range(3):
            window = padded[:, :, row_tap : row_tap + row_count, col_tap : col_tap + col_count]
            running = running + jnp.einsum(
                "oc,fchw->fohw",
                weight[row_tap, col_tap],
                window,
                preferred_element_type=jnp.float32,
            )
    return running


def time_terms(active, time_weight):
    extended = with_halo(active, (("level", 0),), 1)
    frame_count = active.shape[0]
    running = jnp.einsum(
        "oc,fchw->fohw", time_weight[0], extended[0:frame_count], preferred_element_type=jnp.float32
    )
    running = running + jnp.einsum(
        "oc,fchw->fohw",
        time_weight[1],
        extended[1 : frame_count + 1],
        preferred_element_type=jnp.float32,
    )
    running = running + jnp.einsum(
        "oc,fchw->fohw",
        time_weight[2],
        extended[2 : frame_count + 2],
        preferred_element_type=jnp.float32,
    )
    return running


def per_device(
    queue_init, noise_frames, conv_first, conv_second, time_weight, out_proj, keep_coef, noise_coef
):
    queued = queue_init[0]
    row_count = queued.shape[2]
    position = lax.axis_index("level")
    for step_index in range(STEPS):
        queued = shifted(queued, "level", 1)
        queued = jnp.where(position == 0, noise_frames[step_index], queued)
        extended = with_halo(queued, (("tile", 2),), 2)
        first_act = jax.nn.silu(conv_rows(extended, conv_first, row_count + 2))
        global_rows = (
            lax.axis_index("tile") * row_count + jnp.arange(row_count + 2, dtype=jnp.int32) - 1
        )
        inside = (global_rows >= 0) & (global_rows < row_count * lax.axis_size("tile"))
        first_act = jnp.where(inside[None, None, :, None], first_act, 0.0).astype(jnp.bfloat16)
        second = conv_rows(first_act, conv_second, row_count)
        active = jax.nn.silu(second).astype(jnp.bfloat16)
        predicted = (second + time_terms(active, time_weight)).astype(jnp.bfloat16)
        projected = jnp.einsum(
            "oc,fchw->fohw", out_proj, predicted, preferred_element_type=jnp.float32
        )
        keep_rate = lax.dynamic_index_in_dim(keep_coef[step_index], position, 0, keepdims=False)
        noise_rate = lax.dynamic_index_in_dim(noise_coef[step_index], position, 0, keepdims=False)
        queued = (
            keep_rate[:, None, None, None] * queued.astype(jnp.float32)
            - noise_rate[:, None, None, None] * projected
        ).astype(jnp.bfloat16)
    return queued[None]


def solution(mesh):
    return jax.shard_map(
        per_device,
        mesh=mesh,
        in_specs=(
            P("level", None, None, "tile", None),
            P(None, None, None, "tile", None),
            P(),
            P(),
            P(),
            P(),
            P(),
            P(),
        ),
        out_specs=P("level", None, None, "tile", None),
        check_vma=False,
    )
```

profile of v0, /device:TPU:1, one launch (start us, length us, event | category | flops | bytes accessed | tf_op | source)
XLA Modules:
  0.0 129.3 jit_solution(8777187381080837384)
XLA Ops:
  0.0 0.7 copy.44
  0.8 4.5 %collective-permute-start = (bf16[4,4,4,128]{3,1,2,0:T(4,128)(2,1)S(1)}, bf16[4,4,4,128]{3,1,2,0:T(4,128)(2,1)S(1)}, u32[]{:S(2)}, u32[]{:S(2)}) collective-permute-start(bf16[4,4,4,128]{3,1,2,0:T(4,128)(2,1)S(1)} %bitcast.335), channel_id=1, source_target_pairs={{0,8},{8,16},{16,24},{1,9},{9,17},{17,25},{2,10},{10,18},{18,26},{... | collective-permute-start | bytes 49160 | tf_op jit(solution)/shard_map/ppermute | solution.py:25
  5.3 1.4 %fusion.225 = (bf16[1,4,4,4,128]{4,3,2,1,0:T(4,128)(2,1)}, bf16[1,4,4,4,128]{4,3,2,1,0:T(4,128)(2,1)S(1)}) fusion(bf16[2,4,4,4,128]{4,3,2,1,0:T(4,128)(2,1)} %param.9), kind=kLoop, calls=%fused_computation.267 | loop fusion | bytes 65536 | tf_op jit(solution)/shard_map/slice | solution.py:73
  6.6 0.7 fusion.228
  7.3 0.7 fusion.229
  8.0 0.5 fusion.186
  8.6 3.1 %collective-permute-start.1 = (bf16[4,4,2,128]{3,1,2,0:T(4,128)(2,1)S(1)}, bf16[4,4,2,128]{3,1,2,0:T(4,128)(2,1)S(1)}, u32[]{:S(2)}, u32[]{:S(2)}) collective-permute-start(bf16[4,4,2,128]{3,1,2,0:T(4,128)(2,1)S(1)} %get-tuple-element.13), channel_id=1, source_target_pairs={{0,1},{1,2},{2,3},{3,4},{4,5},{5,6},{6,7},{8,9},{9,10},{10,11},{11... | collective-permute-start | bytes 24584 | tf_op jit(solution)/shard_map/ppermute | solution.py:14
  11.7 1.3 collective-permute-start.2
  13.1 3.1 %collective-permute-done.2 = bf16[4,4,2,128]{3,1,2,0:T(4,128)(2,1)S(1)} collective-permute-done((bf16[4,4,2,128]{3,1,2,0:T(4,128)(2,1)S(1)}, bf16[4,4,2,128]{3,1,2,0:T(4,128)(2,1)S(1)}, u32[]{:S(2)}, u32[]{:S(2)}) %collective-permute-start.2) | collective-permute-done | bytes 8224 | tf_op jit(solution)/shard_map/ppermute | solution.py:17
  16.2 1.4 %fusion.110 = f32[4,6,128,320]{2,3,1,0:T(8,128)S(1)} fusion(bf16[4,4,8,128]{3,1,2,0:T(4,128)(2,1)S(1)} %pad_maximum_fusion.24, bf16[3,3,320,4]{2,3,1,0:T(4,128)(2,1)} %param.10), kind=kOutput, calls=%fused_computation.150 | convolution fusion | flops 7864320 | bytes 3968000 | tf_op jit(solution)/shard_map/oc,fchw->fohw/dot_general | solution.py:35
  17.6 0.7 fusion.111
  18.3 0.7 fusion.112
  19.0 0.7 fusion.113
  19.8 2.6 %fusion.114 = f32[4,6,128,320]{2,3,1,0:T(8,128)} fusion(bf16[4,4,8,128]{3,1,2,0:T(4,128)(2,1)S(1)} %pad_maximum_fusion.24, bf16[3,3,320,4]{2,3,1,0:T(4,128)(2,1)S(1)} %copy-done.5), kind=kOutput, calls=%fused_computation.154 | convolution fusion | flops 7864320 | bytes 3968000 | tf_op jit(solution)/shard_map/oc,fchw->fohw/dot_general | solution.py:35
  22.4 2.6 %fusion.157 = f32[4,6,128,320]{2,3,1,0:T(8,128)} fusion(bf16[3,3,320,4]{2,3,1,0:T(4,128)(2,1)S(1)} %copy-done.5, bf16[4,4,2,128]{3,1,2,0:T(4,128)(2,1)S(1)} %collective-permute-done.2, bf16[4,4,4,128]{3,1,2,0:T(4,128)(2,1)S(1)} %fusion.139, bf16[4,4,2,128]{3,1,2,0:T(4,128)(2,1)S(1)} %collective-permute-done.1), kind=kOutput, calls=%fused_computation.196 | convolution fusion | flops 7962624 | bytes 3968000 | tf_op jit(solution)/shard_map/oc,fchw->fohw/dot_general | solution.py:35
  25.0 2.6 %fusion.122 = f32[4,6,128,320]{2,3,1,0:T(8,128)} fusion(bf16[4,4,4,128]{3,1,2,0:T(4,128)(2,1)S(1)} %fusion.139, bf16[4,4,2,128]{3,1,2,0:T(4,128)(2,1)S(1)} %collective-permute-done.1, bf16[3,3,320,4]{2,3,1,0:T(4,128)(2,1)S(1)} %copy-done.5), kind=kOutput, calls=%fused_computation.162 | convolution fusion | flops 7913472 | bytes 3959808 | tf_op jit(solution)/shard_map/oc,fchw->fohw/dot_general | solution.py:35
  27.6 2.6 %fusion.126 = f32[4,6,128,320]{2,3,1,0:T(8,128)} fusion(bf16[4,4,2,128]{3,1,2,0:T(4,128)(2,1)S(1)} %collective-permute-done.2, bf16[4,4,4,128]{3,1,2,0:T(4,128)(2,1)S(1)} %fusion.139, bf16[3,3,320,4]{2,3,1,0:T(4,128)(2,1)S(1)} %copy-done.5), kind=kOutput, calls=%fused_computation.166 | convolution fusion | flops 7913472 | bytes 3959808 | tf_op jit(solution)/shard_map/oc,fchw->fohw/dot_general | solution.py:35
  30.2 6.9 %fusion.8 = bf16[4,320,6,128]{3,1,2,0:T(8,128)(2,1)S(1)} fusion(f32[4,6,128,320]{2,3,1,0:T(8,128)} %fusion.126, f32[4,6,128,320]{2,3,1,0:T(8,128)} %fusion.114, f32[4,6,128,320]{2,3,1,0:T(8,128)S(1)} %fusion.113, f32[4,6,128,320]{2,3,1,0:T(8,128)} %fusion.157, f32[4,6,128,320]{2,3,1,0:T(8,128)S(1)} %fusion.112, f32[4,6,128,320]{2,3,1,0:T(8,128)S(1)} %fusion.111, ...), kind=kOutput, calls=%fused_computation.24 | convolution fusion | flops 21626880 | bytes 33459712 | tf_op jit(solution)/shard_map/oc,fchw->fohw/dot_general | solution.py:35
  37.1 2.0 %fusion.20 = f32[4,4,128,320]{2,3,1,0:T(8,128)S(1)} fusion(bf16[4,320,6,128]{3,1,2,0:T(8,128)(2,1)S(1)} %fusion.8, bf16[3,3,320,320]{3,2,1,0:T(8,128)(2,1)} %param.11), kind=kOutput, calls=%fused_computation.44 | convolution fusion | flops 419430400 | bytes 4833280 | tf_op jit(solution)/shard_map/oc,fchw->fohw/dot_general | solution.py:35
  39.2 0.9 fusion.21
  40.2 1.0 fusion.22
  41.1 0.9 fusion.23
  42.1 1.0 fusion.24
  43.0 0.8 fusion.44
  43.9 0.8 fusion.46
  44.7 0.8 fusion.48
  45.6 3.8 %fusion.18 = (bf16[4,320,4,128]{3,1,2,0:T(8,128)(2,1)S(1)}, f32[4,4,128,320]{2,3,1,0:T(8,128)}) fusion(bf16[4,320,6,128]{3,1,2,0:T(8,128)(2,1)S(1)} %fusion.8, bf16[3,3,320,320]{3,2,1,0:T(8,128)(2,1)S(1)} %copy-done.1, f32[4,4,128,320]{2,3,1,0:T(8,128)S(1)} %fusion.44, f32[4,4,128,320]{2,3,1,0:T(8,128)S(1)} %fusion.24, f32[4,4,128,320]{2,3,1,0:T(8,128)S(1)} %fusion.23, ...), kind=kOutput, calls=%fused_computation.42 | convolution fusion | flops 427950080 | bytes 27115520 | tf_op jit(solution)/shard_map/oc,fchw->fohw/dot_general | solution.py:35
  49.5 3.4 %collective-permute-start.3 = (bf16[1,320,4,128]{3,1,2,0:T(8,128)(2,1)S(1)}, bf16[1,320,4,128]{3,1,2,0:T(8,128)(2,1)S(1)}, u32[]{:S(2)}, u32[]{:S(2)}) collective-permute-start(bf16[1,320,4,128]{3,1,2,0:T(8,128)(2,1)S(1)} %get-tuple-element.8), channel_id=1, source_target_pairs={{0,8},{8,16},{16,24},{1,9},{9,17},{17,25},{2,10},{10,18},{18,26},{... | collective-permute-start | bytes 983048 | tf_op jit(solution)/shard_map/ppermute | solution.py:14
  52.8 1.9 %collective-permute-start.4 = (bf16[1,320,4,128]{3,1,2,0:T(8,128)(2,1)S(1)}, bf16[1,320,4,128]{3,1,2,0:T(8,128)(2,1)S(1)}, u32[]{:S(2)}, u32[]{:S(2)}) collective-permute-start(bf16[1,320,4,128]{3,1,2,0:T(8,128)(2,1)S(1)} %get-tuple-element.7), channel_id=1, source_target_pairs={{8,0},{16,8},{24,16},{9,1},{17,9},{25,17},{10,2},{18,10},{26,18},{... | collective-permute-start | bytes 983048 | tf_op jit(solution)/shard_map/ppermute | solution.py:17
  54.8 2.3 %fusion.60 = f32[4,4,128,320]{2,3,1,0:T(8,128)} fusion(bf16[4,320,4,128]{3,1,2,0:T(8,128)(2,1)S(1)} %get-tuple-element.19, bf16[3,320,320]{2,1,0:T(8,128)(2,1)S(1)} %copy-done.3), kind=kOutput, calls=%fused_computation.86 | convolution fusion | flops 419430400 | bytes 4177920 | tf_op jit(solution)/shard_map/oc,fchw->fohw/dot_general | solution.py:50
  57.1 2.4 %fusion.42 = f32[4,4,128,320]{2,3,1,0:T(8,128)} fusion(bf16[4,320,4,128]{3,1,2,0:T(8,128)(2,1)S(1)} %get-tuple-element.19, bf16[1,320,4,128]{3,1,2,0:T(8,128)(2,1)S(1)} %collective-permute-done.3, bf16[3,320,320]{2,1,0:T(8,128)(2,1)S(1)} %copy-done.3), kind=kOutput, calls=%fused_computation.70 | convolution fusion | flops 422051840 | bytes 4505600 | tf_op jit(solution)/shard_map/oc,fchw->fohw/dot_general | solution.py:47
  59.5 1.7 %collective-permute-done.4 = bf16[1,320,4,128]{3,1,2,0:T(8,128)(2,1)S(1)} collective-permute-done((bf16[1,320,4,128]{3,1,2,0:T(8,128)(2,1)S(1)}, bf16[1,320,4,128]{3,1,2,0:T(8,128)(2,1)S(1)}, u32[]{:S(2)}, u32[]{:S(2)}) %collective-permute-start.4) | collective-permute-done | bytes 327712 | tf_op jit(solution)/shard_map/ppermute | solution.py:17
  61.3 4.5 %subtract_convert_fusion.1 = bf16[4,4,4,128]{3,1,2,0:T(4,128)(2,1)S(1)} fusion(bf16[4,4,4,128]{3,1,2,0:T(4,128)(2,1)S(1)} %fusion.139, f32[4,4,128,320]{2,3,1,0:T(8,128)} %get-tuple-element.20, f32[4,4,128,320]{2,3,1,0:T(8,128)} %fusion.42, f32[4,4,128,320]{2,3,1,0:T(8,128)} %fusion.60, bf16[1,320,4,128]{3,1,2,0:T(8,128)(2,1)S(1)} %collective-permute-done.4, ...), kind=kOutput, calls=%fused_computation.149 | convolution fusion | flops 429957120 | bytes 9783840 | tf_op jit(solution)/shard_map/oc,fchw->fohw/dot_general | solution.py:84
  65.8 2.4 %collective-permute-start.5 = (bf16[4,4,4,128]{3,1,2,0:T(4,128)(2,1)S(1)}, bf16[4,4,4,128]{3,1,2,0:T(4,128)(2,1)S(1)}, u32[]{:S(2)}, u32[]{:S(2)}) collective-permute-start(bf16[4,4,4,128]{3,1,2,0:T(4,128)(2,1)S(1)} %subtract_convert_fusion.1), channel_id=1, source_target_pairs={{0,8},{8,16},{16,24},{1,9},{9,17},{17,25},{2,10},{10,18},{18,26},{... | collective-permute-start | bytes 49160 | tf_op jit(solution)/shard_map/ppermute | solution.py:25
  68.2 0.8 collective-permute-done.5
  69.1 4.0 %collective-permute-start.6 = (bf16[4,4,2,128]{3,1,2,0:T(4,128)(2,1)S(1)}, bf16[4,4,2,128]{3,1,2,0:T(4,128)(2,1)S(1)}, u32[]{:S(2)}, u32[]{:S(2)}) collective-permute-start(bf16[4,4,2,128]{3,1,2,0:T(4,128)(2,1)S(1)} %get-tuple-element.11), channel_id=1, source_target_pairs={{0,1},{1,2},{2,3},{3,4},{4,5},{5,6},{6,7},{8,9},{9,10},{10,11},{11... | collective-permute-start | bytes 24584 | tf_op jit(solution)/shard_map/ppermute | solution.py:14
  73.1 1.5 %collective-permute-start.7 = (bf16[4,4,2,128]{3,1,2,0:T(4,128)(2,1)S(1)}, bf16[4,4,2,128]{3,1,2,0:T(4,128)(2,1)S(1)}, u32[]{:S(2)}, u32[]{:S(2)}) collective-permute-start(bf16[4,4,2,128]{3,1,2,0:T(4,128)(2,1)S(1)} %get-tuple-element.12), channel_id=1, source_target_pairs={{1,0},{2,1},{3,2},{4,3},{5,4},{6,5},{7,6},{9,8},{10,9},{11,10},{12... | collective-permute-start | bytes 24584 | tf_op jit(solution)/shard_map/ppermute | solution.py:17
  74.6 0.5 fusion.185
  75.2 2.3 %collective-permute-done.7 = bf16[4,4,2,128]{3,1,2,0:T(4,128)(2,1)S(1)} collective-permute-done((bf16[4,4,2,128]{3,1,2,0:T(4,128)(2,1)S(1)}, bf16[4,4,2,128]{3,1,2,0:T(4,128)(2,1)S(1)}, u32[]{:S(2)}, u32[]{:S(2)}) %collective-permute-start.7) | collective-permute-done | bytes 8224 | tf_op jit(solution)/shard_map/ppermute | solution.py:17
  77.5 0.7 fusion.116
  78.3 0.7 fusion.117
  79.0 0.7 fusion.118
  79.7 0.7 fusion.119
  80.4 2.6 %fusion.120 = f32[4,6,128,320]{2,3,1,0:T(8,128)} fusion(bf16[4,4,8,128]{3,1,2,0:T(4,128)(2,1)S(1)} %pad_maximum_fusion.25, bf16[3,3,320,4]{2,3,1,0:T(4,128)(2,1)S(1)} %copy-done.6), kind=kOutput, calls=%fused_computation.160 | convolution fusion | flops 7864320 | bytes 3968000 | tf_op jit(solution)/shard_map/oc,fchw->fohw/dot_general | solution.py:35
  83.0 2.6 %fusion.130 = f32[4,6,128,320]{2,3,1,0:T(8,128)} fusion(bf16[4,4,4,128]{3,1,2,0:T(4,128)(2,1)S(1)} %fusion.140, bf16[4,4,2,128]{3,1,2,0:T(4,128)(2,1)S(1)} %collective-permute-done.6, bf16[3,3,320,4]{2,3,1,0:T(4,128)(2,1)S(1)} %copy-done.6), kind=kOutput, calls=%fused_computation.170 | convolution fusion | flops 7913472 | bytes 3959808 | tf_op jit(solution)/shard_map/oc,fchw->fohw/dot_general | solution.py:35
  85.6 2.6 %fusion.155 = f32[4,6,128,320]{2,3,1,0:T(8,128)} fusion(bf16[3,3,320,4]{2,3,1,0:T(4,128)(2,1)S(1)} %copy-done.6, bf16[4,4,2,128]{3,1,2,0:T(4,128)(2,1)S(1)} %collective-permute-done.7, bf16[4,4,4,128]{3,1,2,0:T(4,128)(2,1)S(1)} %fusion.140, bf16[4,4,2,128]{3,1,2,0:T(4,128)(2,1)S(1)} %collective-permute-done.6), kind=kOutput, calls=%fused_computation.194 | convolution fusion | flops 7962624 | bytes 3968000 | tf_op jit(solution)/shard_map/oc,fchw->fohw/dot_general | solution.py:35
  88.3 2.6 %fusion.134 = f32[4,6,128,320]{2,3,1,0:T(8,128)} fusion(bf16[4,4,2,128]{3,1,2,0:T(4,128)(2,1)S(1)} %collective-permute-done.7, bf16[4,4,4,128]{3,1,2,0:T(4,128)(2,1)S(1)} %fusion.140, bf16[3,3,320,4]{2,3,1,0:T(4,128)(2,1)S(1)} %copy-done.6), kind=kOutput, calls=%fused_computation.174 | convolution fusion | flops 7913472 | bytes 3959808 | tf_op jit(solution)/shard_map/oc,fchw->fohw/dot_general | solution.py:35
  90.9 6.9 %fusion.9 = bf16[4,320,6,128]{3,1,2,0:T(8,128)(2,1)S(1)} fusion(f32[4,6,128,320]{2,3,1,0:T(8,128)} %fusion.134, f32[4,6,128,320]{2,3,1,0:T(8,128)} %fusion.120, f32[4,6,128,320]{2,3,1,0:T(8,128)S(1)} %fusion.119, f32[4,6,128,320]{2,3,1,0:T(8,128)} %fusion.155, f32[4,6,128,320]{2,3,1,0:T(8,128)S(1)} %fusion.118, f32[4,6,128,320]{2,3,1,0:T(8,128)S(1)} %fusion.117, ...), kind=kOutput, calls=%fused_computation.25 | convolution fusion | flops 21626880 | bytes 33459712 | tf_op jit(solution)/shard_map/oc,fchw->fohw/dot_general | solution.py:35
  97.8 2.0 %fusion.25 = f32[4,4,128,320]{2,3,1,0:T(8,128)S(1)} fusion(bf16[4,320,6,128]{3,1,2,0:T(8,128)(2,1)S(1)} %fusion.9, bf16[3,3,320,320]{3,2,1,0:T(8,128)(2,1)} %param.11), kind=kOutput, calls=%fused_computation.49 | convolution fusion | flops 419430400 | bytes 4833280 | tf_op jit(solution)/shard_map/oc,fchw->fohw/dot_general | solution.py:35
  99.9 0.9 fusion.26
  100.8 1.0 fusion.27
  101.8 0.9 fusion.28
  102.7 1.0 fusion.29
  103.7 0.8 fusion.34
  104.5 0.8 fusion.36
  105.4 0.8 fusion.38
  106.3 3.8 %fusion.19 = (bf16[4,320,4,128]{3,1,2,0:T(8,128)(2,1)S(1)}, f32[4,4,128,320]{2,3,1,0:T(8,128)}) fusion(bf16[4,320,6,128]{3,1,2,0:T(8,128)(2,1)S(1)} %fusion.9, bf16[3,3,320,320]{3,2,1,0:T(8,128)(2,1)S(1)} %copy-done.2, f32[4,4,128,320]{2,3,1,0:T(8,128)S(1)} %fusion.34, f32[4,4,128,320]{2,3,1,0:T(8,128)S(1)} %fusion.29, f32[4,4,128,320]{2,3,1,0:T(8,128)S(1)} %fusion.28, ...), kind=kOutput, calls=%fused_computation.43 | convolution fusion | flops 427950080 | bytes 27115520 | tf_op jit(solution)/shard_map/oc,fchw->fohw/dot_general | solution.py:35
  110.1 5.6 %collective-permute-start.8 = (bf16[1,320,4,128]{3,1,2,0:T(8,128)(2,1)S(1)}, bf16[1,320,4,128]{3,1,2,0:T(8,128)(2,1)S(1)}, u32[]{:S(2)}, u32[]{:S(2)}) collective-permute-start(bf16[1,320,4,128]{3,1,2,0:T(8,128)(2,1)S(1)} %get-tuple-element.6), channel_id=1, source_target_pairs={{0,8},{8,16},{16,24},{1,9},{9,17},{17,25},{2,10},{10,18},{18,26},{... | collective-permute-start | bytes 983048 | tf_op jit(solution)/shard_map/ppermute | solution.py:14
  115.8 1.9 %collective-permute-start.9 = (bf16[1,320,4,128]{3,1,2,0:T(8,128)(2,1)S(1)}, bf16[1,320,4,128]{3,1,2,0:T(8,128)(2,1)S(1)}, u32[]{:S(2)}, u32[]{:S(2)}) collective-permute-start(bf16[1,320,4,128]{3,1,2,0:T(8,128)(2,1)S(1)} %get-tuple-element.5), channel_id=1, source_target_pairs={{8,0},{16,8},{24,16},{9,1},{17,9},{25,17},{10,2},{18,10},{26,18},{... | collective-permute-start | bytes 983048 | tf_op jit(solution)/shard_map/ppermute | solution.py:17
  117.7 2.3 %fusion.62 = f32[4,4,128,320]{2,3,1,0:T(8,128)} fusion(bf16[4,320,4,128]{3,1,2,0:T(8,128)(2,1)S(1)} %get-tuple-element.21, bf16[3,320,320]{2,1,0:T(8,128)(2,1)S(1)} %copy-done.4), kind=kOutput, calls=%fused_computation.88 | convolution fusion | flops 419430400 | bytes 4177920 | tf_op jit(solution)/shard_map/oc,fchw->fohw/dot_general | solution.py:50
  120.1 2.4 %fusion.32 = f32[4,4,128,320]{2,3,1,0:T(8,128)} fusion(bf16[4,320,4,128]{3,1,2,0:T(8,128)(2,1)S(1)} %get-tuple-element.21, bf16[1,320,4,128]{3,1,2,0:T(8,128)(2,1)S(1)} %collective-permute-done.8, bf16[3,320,320]{2,1,0:T(8,128)(2,1)S(1)} %copy-done.4), kind=kOutput, calls=%fused_computation.58 | convolution fusion | flops 422051840 | bytes 4505600 | tf_op jit(solution)/shard_map/oc,fchw->fohw/dot_general | solution.py:47
  122.5 1.7 %collective-permute-done.9 = bf16[1,320,4,128]{3,1,2,0:T(8,128)(2,1)S(1)} collective-permute-done((bf16[1,320,4,128]{3,1,2,0:T(8,128)(2,1)S(1)}, bf16[1,320,4,128]{3,1,2,0:T(8,128)(2,1)S(1)}, u32[]{:S(2)}, u32[]{:S(2)}) %collective-permute-start.9) | collective-permute-done | bytes 327712 | tf_op jit(solution)/shard_map/ppermute | solution.py:17
  124.2 4.5 %fusion.138 = bf16[1,4,4,4,128]{4,2,3,1,0:T(4,128)(2,1)S(1)} fusion(bf16[4,4,4,128]{3,1,2,0:T(4,128)(2,1)S(1)} %fusion.140, f32[4,4,128,320]{2,3,1,0:T(8,128)} %get-tuple-element.22, f32[4,4,128,320]{2,3,1,0:T(8,128)} %fusion.32, f32[4,4,128,320]{2,3,1,0:T(8,128)} %fusion.62, bf16[1,320,4,128]{3,1,2,0:T(8,128)(2,1)S(1)} %collective-permute-done.9, ...), kind=kOutput, calls=%fused_computation.178 | convolution fusion | flops 429957120 | bytes 9783840 | tf_op jit(solution)/shard_map/oc,fchw->fohw/dot_general | solution.py:84
  128.7 0.6 copy.12
  (38 shorter events, 0.3 us)
Async XLA Ops:
  0.0 61.2 %copy-start = (bf16[4,320]{1,0:T(4,128)(2,1)S(1)}, bf16[4,320]{1,0:T(4,128)(2,1)}, u32[]{:S(2)}) copy-start(bf16[4,320]{1,0:T(4,128)(2,1)} %param.13) | copy-start | bytes 7684
  0.0 17.6 %copy-start.5 = (bf16[3,3,320,4]{2,3,1,0:T(4,128)(2,1)S(1)}, bf16[3,3,320,4]{2,3,1,0:T(4,128)(2,1)}, u32[]{:S(2)}) copy-start(bf16[3,3,320,4]{2,3,1,0:T(4,128)(2,1)} %param.10) | copy-start | bytes 69124
  0.8 7.8 %collective-permute-start = (bf16[4,4,4,128]{3,1,2,0:T(4,128)(2,1)S(1)}, bf16[4,4,4,128]{3,1,2,0:T(4,128)(2,1)S(1)}, u32[]{:S(2)}, u32[]{:S(2)}) collective-permute-start(bf16[4,4,4,128]{3,1,2,0:T(4,128)(2,1)S(1)} %bitcast.335), channel_id=1, source_target_pairs={{0,8},{8,16},{16,24},{1,9},{9,17},{17,25},{2,10},{10,18},{18,26},{... | collective-permute-start | bytes 49160 | tf_op jit(solution)/shard_map/ppermute | solution.py:25
  8.6 4.5 %collective-permute-start.1 = (bf16[4,4,2,128]{3,1,2,0:T(4,128)(2,1)S(1)}, bf16[4,4,2,128]{3,1,2,0:T(4,128)(2,1)S(1)}, u32[]{:S(2)}, u32[]{:S(2)}) collective-permute-start(bf16[4,4,2,128]{3,1,2,0:T(4,128)(2,1)S(1)} %get-tuple-element.13), channel_id=1, source_target_pairs={{0,1},{1,2},{2,3},{3,4},{4,5},{5,6},{6,7},{8,9},{9,10},{10,11},{11... | collective-permute-start | bytes 24584 | tf_op jit(solution)/shard_map/ppermute | solution.py:14
  11.7 4.4 %collective-permute-start.2 = (bf16[4,4,2,128]{3,1,2,0:T(4,128)(2,1)S(1)}, bf16[4,4,2,128]{3,1,2,0:T(4,128)(2,1)S(1)}, u32[]{:S(2)}, u32[]{:S(2)}) collective-permute-start(bf16[4,4,2,128]{3,1,2,0:T(4,128)(2,1)S(1)} %get-tuple-element.14), channel_id=1, source_target_pairs={{1,0},{2,1},{3,2},{4,3},{5,4},{6,5},{7,6},{9,8},{10,9},{11,10},{12... | collective-permute-start | bytes 24584 | tf_op jit(solution)/shard_map/ppermute | solution.py:17
  37.1 2.1 %copy-start.1 = (bf16[3,3,320,320]{3,2,1,0:T(8,128)(2,1)S(1)}, bf16[3,3,320,320]{3,2,1,0:T(8,128)(2,1)}, u32[]{:S(2)}) copy-start(bf16[3,3,320,320]{3,2,1,0:T(8,128)(2,1)} %param.11) | copy-start | bytes 5529604
  45.6 9.2 %copy-start.3 = (bf16[3,320,320]{2,1,0:T(8,128)(2,1)S(1)}, bf16[3,320,320]{2,1,0:T(8,128)(2,1)}, u32[]{:S(2)}) copy-start(bf16[3,320,320]{2,1,0:T(8,128)(2,1)} %param.12) | copy-start | bytes 1843204
  49.5 7.7 %collective-permute-start.3 = (bf16[1,320,4,128]{3,1,2,0:T(8,128)(2,1)S(1)}, bf16[1,320,4,128]{3,1,2,0:T(8,128)(2,1)S(1)}, u32[]{:S(2)}, u32[]{:S(2)}) collective-permute-start(bf16[1,320,4,128]{3,1,2,0:T(8,128)(2,1)S(1)} %get-tuple-element.8), channel_id=1, source_target_pairs={{0,8},{8,16},{16,24},{1,9},{9,17},{17,25},{2,10},{10,18},{18,26},{... | collective-permute-start | bytes 983048 | tf_op jit(solution)/shard_map/ppermute | solution.py:14
  52.8 8.4 %collective-permute-start.4 = (bf16[1,320,4,128]{3,1,2,0:T(8,128)(2,1)S(1)}, bf16[1,320,4,128]{3,1,2,0:T(8,128)(2,1)S(1)}, u32[]{:S(2)}, u32[]{:S(2)}) collective-permute-start(bf16[1,320,4,128]{3,1,2,0:T(8,128)(2,1)S(1)} %get-tuple-element.7), channel_id=1, source_target_pairs={{8,0},{16,8},{24,16},{9,1},{17,9},{25,17},{10,2},{18,10},{26,18},{... | collective-permute-start | bytes 983048 | tf_op jit(solution)/shard_map/ppermute | solution.py:17
  57.1 4.1 %copy-start.8 = (f32[4]{0:T(128)S(1)}, f32[4]{0:T(128)}, u32[]{:S(2)}) copy-start(f32[4]{0:T(128)} %get-tuple-element.25) | copy-start | bytes 52
  57.1 4.1 %copy-start.9 = (f32[4]{0:T(128)S(1)}, f32[4]{0:T(128)}, u32[]{:S(2)}) copy-start(f32[4]{0:T(128)} %get-tuple-element.26) | copy-start | bytes 52
  61.2 7.8 %copy-start.7 = (bf16[1,4,4,4,128]{4,3,2,1,0:T(4,128)(2,1)S(1)}, bf16[1,4,4,4,128]{4,3,2,1,0:T(4,128)(2,1)}, u32[]{:S(2)}) copy-start(bf16[1,4,4,4,128]{4,3,2,1,0:T(4,128)(2,1)} %get-tuple-element.9) | copy-start | bytes 49156
  61.3 16.3 %copy-start.6 = (bf16[3,3,320,4]{2,3,1,0:T(4,128)(2,1)S(1)}, bf16[3,3,320,4]{2,3,1,0:T(4,128)(2,1)}, u32[]{:S(2)}) copy-start(bf16[3,3,320,4]{2,3,1,0:T(4,128)(2,1)} %param.10) | copy-start | bytes 69124
  65.8 3.3 %collective-permute-start.5 = (bf16[4,4,4,128]{3,1,2,0:T(4,128)(2,1)S(1)}, bf16[4,4,4,128]{3,1,2,0:T(4,128)(2,1)S(1)}, u32[]{:S(2)}, u32[]{:S(2)}) collective-permute-start(bf16[4,4,4,128]{3,1,2,0:T(4,128)(2,1)S(1)} %subtract_convert_fusion.1), channel_id=1, source_target_pairs={{0,8},{8,16},{16,24},{1,9},{9,17},{17,25},{2,10},{10,18},{18,26},{... | collective-permute-start | bytes 49160 | tf_op jit(solution)/shard_map/ppermute | solution.py:25
  69.1 6.1 %collective-permute-start.6 = (bf16[4,4,2,128]{3,1,2,0:T(4,128)(2,1)S(1)}, bf16[4,4,2,128]{3,1,2,0:T(4,128)(2,1)S(1)}, u32[]{:S(2)}, u32[]{:S(2)}) collective-permute-start(bf16[4,4,2,128]{3,1,2,0:T(4,128)(2,1)S(1)} %get-tuple-element.11), channel_id=1, source_target_pairs={{0,1},{1,2},{2,3},{3,4},{4,5},{5,6},{6,7},{8,9},{9,10},{10,11},{11... | collective-permute-start | bytes 24584 | tf_op jit(solution)/shard_map/ppermute | solution.py:14
  73.1 4.4 %collective-permute-start.7 = (bf16[4,4,2,128]{3,1,2,0:T(4,128)(2,1)S(1)}, bf16[4,4,2,128]{3,1,2,0:T(4,128)(2,1)S(1)}, u32[]{:S(2)}, u32[]{:S(2)}) collective-permute-start(bf16[4,4,2,128]{3,1,2,0:T(4,128)(2,1)S(1)} %get-tuple-element.12), channel_id=1, source_target_pairs={{1,0},{2,1},{3,2},{4,3},{5,4},{6,5},{7,6},{9,8},{10,9},{11,10},{12... | collective-permute-start | bytes 24584 | tf_op jit(solution)/shard_map/ppermute | solution.py:17
  97.8 2.1 %copy-start.2 = (bf16[3,3,320,320]{3,2,1,0:T(8,128)(2,1)S(1)}, bf16[3,3,320,320]{3,2,1,0:T(8,128)(2,1)}, u32[]{:S(2)}) copy-start(bf16[3,3,320,320]{3,2,1,0:T(8,128)(2,1)} %param.11) | copy-start | bytes 5529604
  106.2 11.5 %copy-start.4 = (bf16[3,320,320]{2,1,0:T(8,128)(2,1)S(1)}, bf16[3,320,320]{2,1,0:T(8,128)(2,1)}, u32[]{:S(2)}) copy-start(bf16[3,320,320]{2,1,0:T(8,128)(2,1)} %param.12) | copy-start | bytes 1843204
  110.1 9.9 %collective-permute-start.8 = (bf16[1,320,4,128]{3,1,2,0:T(8,128)(2,1)S(1)}, bf16[1,320,4,128]{3,1,2,0:T(8,128)(2,1)S(1)}, u32[]{:S(2)}, u32[]{:S(2)}) collective-permute-start(bf16[1,320,4,128]{3,1,2,0:T(8,128)(2,1)S(1)} %get-tuple-element.6), channel_id=1, source_target_pairs={{0,8},{8,16},{16,24},{1,9},{9,17},{17,25},{2,10},{10,18},{18,26},{... | collective-permute-start | bytes 983048 | tf_op jit(solution)/shard_map/ppermute | solution.py:14
  115.8 8.4 %collective-permute-start.9 = (bf16[1,320,4,128]{3,1,2,0:T(8,128)(2,1)S(1)}, bf16[1,320,4,128]{3,1,2,0:T(8,128)(2,1)S(1)}, u32[]{:S(2)}, u32[]{:S(2)}) collective-permute-start(bf16[1,320,4,128]{3,1,2,0:T(8,128)(2,1)S(1)} %get-tuple-element.5), channel_id=1, source_target_pairs={{8,0},{16,8},{24,16},{9,1},{17,9},{25,17},{10,2},{18,10},{26,18},{... | collective-permute-start | bytes 983048 | tf_op jit(solution)/shard_map/ppermute | solution.py:17
  120.1 4.1 %copy-start.10 = (f32[4]{0:T(128)S(1)}, f32[4]{0:T(128)}, u32[]{:S(2)}) copy-start(f32[4]{0:T(128)} %get-tuple-element.23) | copy-start | bytes 52
  120.1 4.1 %copy-start.11 = (f32[4]{0:T(128)S(1)}, f32[4]{0:T(128)}, u32[]{:S(2)}) copy-start(f32[4]{0:T(128)} %get-tuple-element.24) | copy-start | bytes 52
where the time goes:
time: 130 us; the launch traced here: 129 us
  matrix products  84 us (65%)
  starting transfers between devices  29.7 us (23%)
  waiting for transfers between devices  9.7 us (7%)
  local copies, waits for them, and re-layouts  5.35 us (4%)
    dot_general x36, matrix products, conv_rows(): jnp.einsum('oc,fchw->fohw', weight[row_tap, col_tap], window, preferred_e...  65.5 us
    ppermute x4, starting transfers between devices, with_halo(): lax.ppermute(lax.slice_in_dim(block, block.shape[dim] - width, None, axis...  16.2 us
    dot_general x2, matrix products, per_device(): jnp.einsum('oc,fchw->fohw', out_proj, predicted, preferred_element_type=j...  8.98 us
    ppermute x4, waiting for transfers between devices, with_halo(): lax.ppermute(lax.slice_in_dim(block, 0, width, axis=dim), axis, backward)  8.84 us
    ppermute x2, starting transfers between devices, shifted(): lax.ppermute(value, axis, [(source, source + steps) for source in range(l...  6.88 us
    ppermute x4, starting transfers between devices, with_halo(): lax.ppermute(lax.slice_in_dim(block, 0, width, axis=dim), axis, backward)  6.65 us
    dot_general x2, matrix products, time_terms(): jnp.einsum('oc,fchw->fohw', time_weight[0], extended[0:frame_count], pref...  4.79 us
    dot_general x2, matrix products, time_terms(): jnp.einsum('oc,fchw->fohw', time_weight[1], extended[1:frame_count + 1],...  4.69 us
  transfers between devices with their start and end apart: 10, of which 5 were waited for; matrix products, arithmetic and copies ran while one was open for 10% of the time, Pallas kernels for 0%

commit v1 on v0

v1 whole, which is shorter than its diff:
```python
import functools

import jax
import jax.numpy as jnp
from jax import lax
from jax.experimental import pallas as pl
from jax.experimental.pallas import tpu as pltpu
from jax.sharding import PartitionSpec as P

BF16 = jnp.bfloat16
F32 = jnp.float32


def silu(v):
    half = 0.5 * v
    return half * jnp.tanh(half) + half


def step_kernel(
    dims, edge_ref, keep_ref, noise_ref, prev_ref, own_ref, next_ref, w1_ref, w2_ref, wz_ref,
    upd_ref, fwd_ref, bwd_ref, s_ref, z_ref,
):
    frames, latent, rows, width, channels = dims
    n_out = rows * width
    n_mid = (rows + 2) * width
    n_in = (rows + 4) * width
    slot = w1_ref.shape[1] // 3

    def shift_cols(v, by):
        lane = lax.broadcasted_iota(jnp.int32, v.shape, 1) % width
        if by > 0:
            return jnp.where(lane == 0, jnp.zeros_like(v), pltpu.roll(v, 1, 1))
        return jnp.where(lane == width - 1, jnp.zeros_like(v), pltpu.roll(v, v.shape[1] - 1, 1))

    def conv1(f):
        lo, hi = f * latent, (f + 1) * latent
        a = jnp.concatenate(
            [prev_ref[lo:hi, :], own_ref[lo:hi, :], next_ref[lo:hi, :]], axis=1
        ).astype(F32)
        parts = [shift_cols(a, 1), a, shift_cols(a, -1)]
        if slot > 3 * latent:
            parts.append(jnp.zeros((slot - 3 * latent, n_in), F32))
        b = jnp.concatenate(parts, axis=0).astype(BF16)
        x = jnp.concatenate([b[:, k * width:k * width + n_mid] for k in range(3)], axis=0)
        v = silu(jnp.dot(w1_ref[...], x, preferred_element_type=F32))
        row = lax.broadcasted_iota(jnp.int32, v.shape, 1) // width
        outside = ((row == 0) & (edge_ref[0] == 1)) | ((row == rows + 1) & (edge_ref[1] == 1))
        v = jnp.where(outside, 0.0, v)
        s_ref[f % 2, 0:channels, :] = shift_cols(v, 1).astype(BF16)
        s_ref[f % 2, channels:2 * channels, :] = v.astype(BF16)
        s_ref[f % 2, 2 * channels:, :] = shift_cols(v, -1).astype(BF16)

    def conv2(f):
        total = None
        for k in range(3):
            part = jnp.dot(
                w2_ref[k], s_ref[f % 2, :, k * width:k * width + n_out],
                preferred_element_type=F32,
            )
            total = part if total is None else total + part
        return total

    def project(f, second):
        x = jnp.concatenate([second.astype(BF16), silu(second).astype(BF16)], axis=0)
        z_ref[f] = jnp.dot(wz_ref[...], x, preferred_element_type=F32)

    conv1(0)
    for f in range(frames):
        if f + 1 < frames:
            conv1(f + 1)
        project(f, conv2(f))
    for f in range(frames):
        z = z_ref[f, 0:latent, :]
        if f > 0:
            z = z + z_ref[f - 1, latent:2 * latent, :]
        if f + 1 < frames:
            z = z + z_ref[f + 1, 2 * latent:3 * latent, :]
        lo, hi = f * latent, (f + 1) * latent
        upd_ref[lo:hi, :] = keep_ref[f] * own_ref[lo:hi, :].astype(F32) - noise_ref[f] * z
    fwd_ref[...] = z_ref[frames - 1, latent:2 * latent, :]
    bwd_ref[...] = z_ref[0, 2 * latent:3 * latent, :]


def per_device(
    queue_init, noise_frames, conv_first, conv_second, time_weight, out_proj, keep_coef, noise_coef
):
    steps = noise_frames.shape[0]
    _, frames, latent, rows, width = queue_init.shape
    channels = conv_second.shape[2]
    levels, tiles = lax.axis_size("level"), lax.axis_size("tile")
    level, tile = lax.axis_index("level"), lax.axis_index("tile")
    flat = frames * latent
    n_out = rows * width
    dims = (frames, latent, rows, width, channels)
    half = 2 * width

    slot = -(-3 * latent // 16) * 16
    w1 = jnp.transpose(conv_first, (2, 0, 1, 3)).reshape(channels, 3, 3 * latent)
    w1 = jnp.pad(w1, ((0, 0), (0, 0), (0, slot - 3 * latent))).reshape(channels, 3 * slot)
    w2 = jnp.transpose(conv_second, (0, 2, 1, 3)).reshape(3, channels, 3 * channels)
    pt = jnp.einsum("lo,koi->kli", out_proj, time_weight, preferred_element_type=F32).astype(BF16)
    left = jnp.zeros((4 * latent, channels), BF16).at[0:latent].set(out_proj)
    right = jnp.concatenate([pt[1], pt[0], pt[2], jnp.zeros((latent, channels), BF16)], axis=0)
    wz = jnp.concatenate([left, right], axis=1)
    edge = jnp.stack([tile == 0, tile == tiles - 1]).astype(jnp.int32)

    def permute(x, dl, dt):
        pairs = [
            (l * tiles + t, ((l + dl) % levels) * tiles + t + dt)
            for l in range(levels) for t in range(tiles) if 0 <= t + dt < tiles
        ]
        return lax.ppermute(x, ("level", "tile"), pairs)

    def level_chain(x, by, skip):
        pairs = [(l, (l + by) % levels) for l in range(levels) if l != skip]
        return lax.ppermute(x, "level", pairs)

    queue = queue_init[0].reshape(flat, n_out)
    noise = noise_frames.reshape(steps, flat, n_out)
    send = jnp.where(level == levels - 1, noise[0], queue)
    own = permute(send, steps, 0)
    prev = permute(send[:, n_out - half:], steps, 1)
    nxt = permute(send[:, :half], steps, -1)

    smem = pl.BlockSpec(memory_space=pltpu.SMEM)
    vmem = pl.BlockSpec(memory_space=pltpu.VMEM)
    flops = 2 * frames * n_out * channels * (9 * channels + 9 * latent * 2 + 8 * latent)
    call = pl.pallas_call(
        functools.partial(step_kernel, dims),
        out_shape=(
            jax.ShapeDtypeStruct((flat, n_out), F32),
            jax.ShapeDtypeStruct((latent, n_out), F32),
            jax.ShapeDtypeStruct((latent, n_out), F32),
        ),
        in_specs=[smem] * 3 + [vmem] * 6,
        out_specs=(vmem,) * 3,
        scratch_shapes=[
            pltpu.VMEM((2, 3 * channels, (rows + 2) * width), BF16),
            pltpu.VMEM((frames, 4 * latent, n_out), F32),
        ],
        compiler_params=pltpu.CompilerParams(vmem_limit_bytes=32 * 1024 * 1024),
        cost_estimate=pl.CostEstimate(
            flops=flops, bytes_accessed=2 * 9 * channels * channels, transcendentals=0
        ),
    )

    for s in range(steps):
        offset = steps - 1 - s
        position = (level + levels - offset % levels) % levels
        keep = lax.dynamic_index_in_dim(keep_coef[s], position, 0, keepdims=False)
        rate = lax.dynamic_index_in_dim(noise_coef[s], position, 0, keepdims=False)
        upd, fwd, bwd = call(edge, keep, rate, prev, own, nxt, w1, w2, wz)
        last = (levels - 1 + offset) % levels
        before = level_chain(fwd, 1, last)
        after = level_chain(bwd, -1, (last + 1) % levels)
        gap = jnp.zeros((flat - 2 * latent, n_out), F32)
        corr = jnp.concatenate([rate[0] * before, gap, rate[frames - 1] * after], axis=0)
        queue = (upd - corr).astype(BF16)
        if s + 1 < steps:
            queue = jnp.where(position == levels - 1, noise[s + 1], queue)
            own = queue
            prev = permute(queue[:, n_out - half:], 0, 1)
            nxt = permute(queue[:, :half], 0, -1)
    return queue.reshape(1, frames, latent, rows, width)


def solution(mesh):
    return jax.shard_map(
        per_device,
        mesh=mesh,
        in_specs=(
            P("level", None, None, "tile", None),
            P(None, None, None, "tile", None),
            P(),
            P(),
            P(),
            P(),
            P(),
            P(),
        ),
        out_specs=P("level", None, None, "tile", None),
        check_vma=False,
    )
```

time: 130 us -> 63 us (0.48)
  the two profiles are of different devices: /device:TPU:1 before, /device:TPU:21 now
where the time goes in v1:
time: 63 us; the launch traced here: 62.4 us
  starting transfers between devices  23.7 us (38%)
  Pallas kernels  14.1 us (22%)
  local copies, waits for them, and re-layouts  10.5 us (17%)
  waiting for transfers between devices  8.58 us (14%)
  other arithmetic  4.29 us (7%)
  matrix products  0.89 us (1%)
    pallas_call x2, Pallas kernels, per_device(): upd, fwd, bwd = call(edge, keep, rate, prev, own, nxt, w1, w2, wz)  14.1 us
    ppermute x5, starting transfers between devices, permute(): return lax.ppermute(x, ('level', 'tile'), pairs)  13.6 us
    ppermute x4, starting transfers between devices, level_chain(): return lax.ppermute(x, 'level', pairs)  10.1 us
    ppermute x4, waiting for transfers between devices, level_chain(): return lax.ppermute(x, 'level', pairs)  5.42 us
    transpose x1, local copies, waits for them, and re-layouts, per_device(): jnp.transpose(conv_second, (0, 2, 1, 3)).reshape(3, channels, 3 * channels)  4.19 us
    ppermute x5, waiting for transfers between devices, permute(): return lax.ppermute(x, ('level', 'tile'), pairs)  3.17 us
    reshape x1, local copies, waits for them, and re-layouts, per_device(): jnp.transpose(conv_second, (0, 2, 1, 3)).reshape(3, channels, 3 * channels)  2.77 us
    mul x2, other arithmetic, per_device(): rate[0] * before  1.26 us
  transfers between devices with their start and end apart: 9, of which 3 were waited for; matrix products, arithmetic and copies ran while one was open for 21% of the time, Pallas kernels for 0%

profile of v1, /device:TPU:21, one launch (start us, length us, event | category | flops | bytes accessed | tf_op | source)
XLA Modules:
  0.0 62.4 jit_solution(3448012430991192608)
XLA Ops:
  0.0 0.0 copy-start
  0.0 0.8 %fusion.9 = (bf16[1,4,4,4,128]{4,3,2,1,0:T(4,128)(2,1)S(1)}, bf16[1,4,4,4,128]{4,3,2,1,0:T(4,128)(2,1)S(1)}) fusion(bf16[2,4,4,4,128]{4,3,2,1,0:T(4,128)(2,1)} %param.11, bf16[1,4,4,4,128]{4,3,2,1,0:T(4,128)(2,1)} %param.10, pred[]{:T(512)S(6)} %eq.18), kind=kLoop, calls=%fused_computation.27 | loop fusion | flops 8192 | bytes 81921 | tf_op jit(solution)/shard_map/slice | solution.py:160
  0.9 1.3 %collective-permute-start.1 = (bf16[16,512]{1,0:T(8,128)(2,1)S(1)}, bf16[16,512]{1,0:T(8,128)(2,1)S(1)}, u32[]{:S(2)}, u32[]{:S(2)}) collective-permute-start(bf16[16,512]{1,0:T(8,128)(2,1)S(1)} %bitcast.46), channel_id=1, source_target_pairs={{0,16},{1,17},{2,18},{3,19},{4,20},{5,21},{6,22},{7,23},{8,24},{9,... | collective-permute-start | bytes 49160 | tf_op jit(solution)/shard_map/ppermute | solution.py:112
  2.1 3.1 %collective-permute-start = (bf16[16,256]{1,0:T(8,128)(2,1)S(1)}, bf16[16,256]{1,0:T(8,128)(2,1)S(1)}, u32[]{:S(2)}, u32[]{:S(2)}) collective-permute-start(bf16[16,256]{1,0:T(8,128)(2,1)S(1)} %get-tuple-element.34), channel_id=1, source_target_pairs={{0,17},{1,18},{2,19},{3,20},{4,21},{5,22},{6,23},{8,25},{9,26},{10... | collective-permute-start | bytes 24584 | tf_op jit(solution)/shard_map/ppermute | solution.py:112
  5.3 3.0 %collective-permute-start.2 = (bf16[16,256]{1,0:T(8,128)(2,1)S(1)}, bf16[16,256]{1,0:T(8,128)(2,1)S(1)}, u32[]{:S(2)}, u32[]{:S(2)}) collective-permute-start(bf16[16,256]{1,0:T(8,128)(2,1)S(1)} %get-tuple-element.33), channel_id=1, source_target_pairs={{1,16},{2,17},{3,18},{4,19},{5,20},{6,21},{7,22},{9,24},{10,25},{1... | collective-permute-start | bytes 24584 | tf_op jit(solution)/shard_map/ppermute | solution.py:112
  8.3 0.7 %fusion.12 = (f32[1,4,4]{2,1,0:T(4,128)S(1)}, f32[1,4,4]{2,1,0:T(4,128)S(1)}) fusion(f32[2,4,4]{2,1,0:T(4,128)} %param.17), kind=kLoop, calls=%fused_computation.30 | loop fusion | bytes 256 | tf_op jit(solution)/shard_map/slice | solution.py:151
  9.1 0.7 %fusion.13 = (f32[1,4,4]{2,1,0:T(4,128)S(1)}, f32[1,4,4]{2,1,0:T(4,128)S(1)}) fusion(f32[2,4,4]{2,1,0:T(4,128)} %param.16), kind=kLoop, calls=%fused_computation.31 | loop fusion | bytes 256 | tf_op jit(solution)/shard_map/slice | solution.py:150
  9.8 0.0 copy-done
  9.8 0.9 %fusion = bf16[3,4,320]{2,1,0:T(4,128)(2,1)S(1)} fusion(bf16[3,320,320]{2,1,0:T(8,128)(2,1)S(1)} %copy-done, bf16[4,320]{1,0:T(4,128)(2,1)} %param.15), kind=kOutput, calls=%fused_computation.1 | convolution fusion | flops 2461440 | bytes 624640 | tf_op jit(solution)/shard_map/lo,koi->kli/dot_general | solution.py:101
  10.7 0.6 fusion.15
  11.3 0.1 add_convert_fusion.edge_ref
  11.4 0.8 %fusion.4.wz_ref = bf16[16,640]{1,0:T(8,128)(2,1)S(1)} fusion(bf16[4,320]{1,0:T(4,128)(2,1)} %param.15, bf16[4,320]{1,0:T(4,128)(2,1)S(1)} %broadcast.29, bf16[4,320]{1,0:T(4,128)(2,1)S(1)} %get-tuple-element.36, bf16[4,320]{1,0:T(4,128)(2,1)S(1)} %get-tuple-element.37, bf16[4,320]{1,0:T(4,128)(2,1)S(1)} %get-tuple-element.35), kind=kLoop, calls=%fused_computation.8 | loop fusion | flops 122880 | bytes 33280 | tf_op jit(solution)/shard_map/concatenate | solution.py:104
  12.2 4.2 %copy.11 = bf16[3,320,3,320]{1,3,2,0:T(8,128)(2,1)} copy(bf16[3,320,3,320]{3,1,2,0:T(8,128)(2,1)} %bitcast.42) | data formatting | bytes 3686400 | tf_op jit(solution)/shard_map/transpose | solution.py:100
  16.3 0.0 copy-start.1
  16.4 2.8 %copy.13.w2_ref = bf16[3,320,960]{2,1,0:T(8,128)(2,1)S(1)} copy(bf16[3,320,960]{1,2,0:T(8,128)(2,1)} %bitcast.41) | data formatting | bytes 3686400 | tf_op jit(solution)/shard_map/reshape | solution.py:100
  19.1 0.0 copy-done.1
  19.2 0.1 copy.12.w1_ref
  19.3 0.0 collective-permute-done.prev_ref
  19.3 0.0 collective-permute-done.2.next_ref
  19.3 0.0 collective-permute-done.1.own_ref
  19.3 7.1 %shard_map.82 = (f32[16,512]{1,0:T(8,128)S(1)}, f32[4,512]{1,0:T(4,128)S(1)}, f32[4,512]{1,0:T(4,128)S(1)}) custom-call(s32[2]{0:T(128)S(1)} %add_convert_fusion.edge_ref, f32[4]{0:T(128)S(1)} %fusion.8.keep_ref, f32[4]{0:T(128)S(1)} %fusion.17.noise_ref, bf16[16,256]{1,0:T(8,128)(2,1)S(1)} %collective-permute-done.prev_ref, ...), custom_call_target="tpu_custom_call" | custom-call | flops 3911188480 | bytes 1843200 | tf_op jit(solution)/shard_map/pallas_call | solution.py:152
  26.4 3.6 %collective-permute-start.3 = (f32[4,512]{1,0:T(4,128)S(1)}, f32[4,512]{1,0:T(4,128)S(1)}, u32[]{:S(2)}, u32[]{:S(2)}) collective-permute-start(f32[4,512]{1,0:T(4,128)S(1)} %get-tuple-element.24), channel_id=1, source_target_pairs={{8,16},{16,24},{24,0},{9,17},{17,25},{25,1},{10,18},{18,26},{26,2}... | collective-permute-start | bytes 24584 | tf_op jit(solution)/shard_map/ppermute | solution.py:116
  30.0 0.1 pad.12.clone
  30.1 1.3 %collective-permute-start.4 = (f32[4,512]{1,0:T(4,128)S(1)}, f32[4,512]{1,0:T(4,128)S(1)}, u32[]{:S(2)}, u32[]{:S(2)}) collective-permute-start(f32[4,512]{1,0:T(4,128)S(1)} %get-tuple-element.25), channel_id=1, source_target_pairs={{0,24},{16,8},{24,16},{1,25},{17,9},{25,17},{2,26},{18,10},{26,18}... | collective-permute-start | bytes 24584 | tf_op jit(solution)/shard_map/ppermute | solution.py:116
  31.4 0.0 collective-permute-done.3
  31.4 0.6 broadcast_multiply_fusion.3
  32.0 3.0 %collective-permute-done.4 = f32[4,512]{1,0:T(4,128)S(1)} collective-permute-done((f32[4,512]{1,0:T(4,128)S(1)}, f32[4,512]{1,0:T(4,128)S(1)}, u32[]{:S(2)}, u32[]{:S(2)}) %collective-permute-start.4) | collective-permute-done | bytes 8224 | tf_op jit(solution)/shard_map/ppermute | solution.py:116
  35.1 0.6 %broadcast_multiply_fusion.2 = f32[4,512]{1,0:T(4,128)S(1)} fusion(f32[4,512]{1,0:T(4,128)S(1)} %collective-permute-done.4, f32[]{:T(128)} %bitcast.16), kind=kLoop, calls=%fused_computation.14 | loop fusion | flops 2048 | bytes 16388 | tf_op jit(solution)/shard_map/mul | solution.py:157
  35.7 0.1 fusion.5.own_ref
  35.8 4.0 %collective-permute-start.5 = (bf16[16,256]{1,0:T(8,128)(2,1)S(1)}, bf16[16,256]{1,0:T(8,128)(2,1)S(1)}, u32[]{:S(2)}, u32[]{:S(2)}) collective-permute-start(bf16[16,256]{1,0:T(8,128)(2,1)S(1)} %get-tuple-element.32), channel_id=1, source_target_pairs={{0,1},{1,2},{2,3},{3,4},{4,5},{5,6},{6,7},{8,9},{9,10},{10,11},{11... | collective-permute-start | bytes 24584 | tf_op jit(solution)/shard_map/ppermute | solution.py:112
  39.8 2.1 %collective-permute-start.6 = (bf16[16,256]{1,0:T(8,128)(2,1)S(1)}, bf16[16,256]{1,0:T(8,128)(2,1)S(1)}, u32[]{:S(2)}, u32[]{:S(2)}) collective-permute-start(bf16[16,256]{1,0:T(8,128)(2,1)S(1)} %get-tuple-element.31), channel_id=1, source_target_pairs={{1,0},{2,1},{3,2},{4,3},{5,4},{6,5},{7,6},{9,8},{10,9},{11,10},{12... | collective-permute-start | bytes 24584 | tf_op jit(solution)/shard_map/ppermute | solution.py:112
  42.0 0.0 collective-permute-done.5.prev_ref
  42.0 3.2 %collective-permute-done.6.next_ref = bf16[16,256]{1,0:T(8,128)(2,1)S(1)} collective-permute-done((bf16[16,256]{1,0:T(8,128)(2,1)S(1)}, bf16[16,256]{1,0:T(8,128)(2,1)S(1)}, u32[]{:S(2)}, u32[]{:S(2)}) %collective-permute-start.6) | collective-permute-done | bytes 8224 | tf_op jit(solution)/shard_map/ppermute | solution.py:112
  45.1 7.1 %shard_map.83 = (f32[16,512]{1,0:T(8,128)S(1)}, f32[4,512]{1,0:T(4,128)S(1)}, f32[4,512]{1,0:T(4,128)S(1)}) custom-call(s32[2]{0:T(128)S(1)} %add_convert_fusion.edge_ref, f32[4]{0:T(128)S(1)} %fusion.7.keep_ref, f32[4]{0:T(128)S(1)} %fusion.18.noise_ref, bf16[16,256]{1,0:T(8,128)(2,1)S(1)} %collective-permute-done.5.prev_ref, ...), custom_call_target="tpu_custom_call" | custom-call | flops 3911188480 | bytes 1843200 | tf_op jit(solution)/shard_map/pallas_call | solution.py:152
  52.2 3.4 %collective-permute-start.7 = (f32[4,512]{1,0:T(4,128)S(1)}, f32[4,512]{1,0:T(4,128)S(1)}, u32[]{:S(2)}, u32[]{:S(2)}) collective-permute-start(f32[4,512]{1,0:T(4,128)S(1)} %get-tuple-element.27), channel_id=1, source_target_pairs={{0,8},{8,16},{16,24},{1,9},{9,17},{17,25},{2,10},{10,18},{18,26},{... | collective-permute-start | bytes 24584 | tf_op jit(solution)/shard_map/ppermute | solution.py:116
  55.6 0.6 fusion.14
  56.2 1.9 %collective-permute-start.8 = (f32[4,512]{1,0:T(4,128)S(1)}, f32[4,512]{1,0:T(4,128)S(1)}, u32[]{:S(2)}, u32[]{:S(2)}) collective-permute-start(f32[4,512]{1,0:T(4,128)S(1)} %get-tuple-element.28), channel_id=1, source_target_pairs={{8,0},{16,8},{24,16},{9,1},{17,9},{25,17},{10,2},{18,10},{26,18},{... | collective-permute-start | bytes 24584 | tf_op jit(solution)/shard_map/ppermute | solution.py:116
  58.1 0.0 collective-permute-done.7
  58.1 0.7 %broadcast_multiply_fusion.1 = f32[4,512]{1,0:T(4,128)S(1)} fusion(f32[4,512]{1,0:T(4,128)S(1)} %collective-permute-done.7, f32[]{:T(128)} %bitcast.17), kind=kLoop, calls=%fused_computation.13 | loop fusion | flops 2048 | bytes 16388 | tf_op jit(solution)/shard_map/mul | solution.py:157
  58.8 2.4 %collective-permute-done.8 = f32[4,512]{1,0:T(4,128)S(1)} collective-permute-done((f32[4,512]{1,0:T(4,128)S(1)}, f32[4,512]{1,0:T(4,128)S(1)}, u32[]{:S(2)}, u32[]{:S(2)}) %collective-permute-start.8) | collective-permute-done | bytes 8224 | tf_op jit(solution)/shard_map/ppermute | solution.py:116
  61.1 0.6 broadcast_multiply_fusion
  61.7 0.1 fusion.3
  61.8 0.6 reshape.64
  (14 shorter events, 0.1 us)
Async XLA Ops:
  0.0 9.8 %copy-start = (bf16[3,320,320]{2,1,0:T(8,128)(2,1)S(1)}, bf16[3,320,320]{2,1,0:T(8,128)(2,1)}, u32[]{:S(2)}) copy-start(bf16[3,320,320]{2,1,0:T(8,128)(2,1)} %param.14) | copy-start | bytes 1843204
  0.9 18.5 %collective-permute-start.1 = (bf16[16,512]{1,0:T(8,128)(2,1)S(1)}, bf16[16,512]{1,0:T(8,128)(2,1)S(1)}, u32[]{:S(2)}, u32[]{:S(2)}) collective-permute-start(bf16[16,512]{1,0:T(8,128)(2,1)S(1)} %bitcast.46), channel_id=1, source_target_pairs={{0,16},{1,17},{2,18},{3,19},{4,20},{5,21},{6,22},{7,23},{8,24},{9,... | collective-permute-start | bytes 49160 | tf_op jit(solution)/shard_map/ppermute | solution.py:112
  2.1 17.2 %collective-permute-start = (bf16[16,256]{1,0:T(8,128)(2,1)S(1)}, bf16[16,256]{1,0:T(8,128)(2,1)S(1)}, u32[]{:S(2)}, u32[]{:S(2)}) collective-permute-start(bf16[16,256]{1,0:T(8,128)(2,1)S(1)} %get-tuple-element.34), channel_id=1, source_target_pairs={{0,17},{1,18},{2,19},{3,20},{4,21},{5,22},{6,23},{8,25},{9,26},{10... | collective-permute-start | bytes 24584 | tf_op jit(solution)/shard_map/ppermute | solution.py:112
  5.3 14.1 %collective-permute-start.2 = (bf16[16,256]{1,0:T(8,128)(2,1)S(1)}, bf16[16,256]{1,0:T(8,128)(2,1)S(1)}, u32[]{:S(2)}, u32[]{:S(2)}) collective-permute-start(bf16[16,256]{1,0:T(8,128)(2,1)S(1)} %get-tuple-element.33), channel_id=1, source_target_pairs={{1,16},{2,17},{3,18},{4,19},{5,20},{6,21},{7,22},{9,24},{10,25},{1... | collective-permute-start | bytes 24584 | tf_op jit(solution)/shard_map/ppermute | solution.py:112
  16.3 2.8 %copy-start.1 = (bf16[3,3,320,4]{2,3,1,0:T(4,128)(2,1)S(1)}, bf16[3,3,320,4]{2,3,1,0:T(4,128)(2,1)}, u32[]{:S(2)}) copy-start(bf16[3,3,320,4]{2,3,1,0:T(4,128)(2,1)} %param.12) | copy-start | bytes 69124
  26.4 5.0 %collective-permute-start.3 = (f32[4,512]{1,0:T(4,128)S(1)}, f32[4,512]{1,0:T(4,128)S(1)}, u32[]{:S(2)}, u32[]{:S(2)}) collective-permute-start(f32[4,512]{1,0:T(4,128)S(1)} %get-tuple-element.24), channel_id=1, source_target_pairs={{8,16},{16,24},{24,0},{9,17},{17,25},{25,1},{10,18},{18,26},{26,2}... | collective-permute-start | bytes 24584 | tf_op jit(solution)/shard_map/ppermute | solution.py:116
  30.1 5.0 %collective-permute-start.4 = (f32[4,512]{1,0:T(4,128)S(1)}, f32[4,512]{1,0:T(4,128)S(1)}, u32[]{:S(2)}, u32[]{:S(2)}) collective-permute-start(f32[4,512]{1,0:T(4,128)S(1)} %get-tuple-element.25), channel_id=1, source_target_pairs={{0,24},{16,8},{24,16},{1,25},{17,9},{25,17},{2,26},{18,10},{26,18}... | collective-permute-start | bytes 24584 | tf_op jit(solution)/shard_map/ppermute | solution.py:116
  35.8 6.2 %collective-permute-start.5 = (bf16[16,256]{1,0:T(8,128)(2,1)S(1)}, bf16[16,256]{1,0:T(8,128)(2,1)S(1)}, u32[]{:S(2)}, u32[]{:S(2)}) collective-permute-start(bf16[16,256]{1,0:T(8,128)(2,1)S(1)} %get-tuple-element.32), channel_id=1, source_target_pairs={{0,1},{1,2},{2,3},{3,4},{4,5},{5,6},{6,7},{8,9},{9,10},{10,11},{11... | collective-permute-start | bytes 24584 | tf_op jit(solution)/shard_map/ppermute | solution.py:112
  39.8 5.3 %collective-permute-start.6 = (bf16[16,256]{1,0:T(8,128)(2,1)S(1)}, bf16[16,256]{1,0:T(8,128)(2,1)S(1)}, u32[]{:S(2)}, u32[]{:S(2)}) collective-permute-start(bf16[16,256]{1,0:T(8,128)(2,1)S(1)} %get-tuple-element.31), channel_id=1, source_target_pairs={{1,0},{2,1},{3,2},{4,3},{5,4},{6,5},{7,6},{9,8},{10,9},{11,10},{12... | collective-permute-start | bytes 24584 | tf_op jit(solution)/shard_map/ppermute | solution.py:112
  52.2 5.9 %collective-permute-start.7 = (f32[4,512]{1,0:T(4,128)S(1)}, f32[4,512]{1,0:T(4,128)S(1)}, u32[]{:S(2)}, u32[]{:S(2)}) collective-permute-start(f32[4,512]{1,0:T(4,128)S(1)} %get-tuple-element.27), channel_id=1, source_target_pairs={{0,8},{8,16},{16,24},{1,9},{9,17},{17,25},{2,10},{10,18},{18,26},{... | collective-permute-start | bytes 24584 | tf_op jit(solution)/shard_map/ppermute | solution.py:116
  56.2 5.0 %collective-permute-start.8 = (f32[4,512]{1,0:T(4,128)S(1)}, f32[4,512]{1,0:T(4,128)S(1)}, u32[]{:S(2)}, u32[]{:S(2)}) collective-permute-start(f32[4,512]{1,0:T(4,128)S(1)} %get-tuple-element.28), channel_id=1, source_target_pairs={{8,0},{16,8},{24,16},{9,1},{17,9},{25,17},{10,2},{18,10},{26,18},{... | collective-permute-start | bytes 24584 | tf_op jit(solution)/shard_map/ppermute | solution.py:116

commit v2 on v0

v2 whole, which is shorter than its diff:
```python
import functools

import jax
import jax.numpy as jnp
from jax import lax
from jax.experimental import pallas as pl
from jax.experimental.pallas import tpu as pltpu
from jax.sharding import PartitionSpec as P

BF16 = jnp.bfloat16
F32 = jnp.float32
MIB = 1024 * 1024


def silu(v):
    half = 0.5 * v
    return half * jnp.tanh(half) + half


def dot(a, b):
    return jnp.dot(a, b, preferred_element_type=F32)


def slot_of(latent):
    return -(-3 * latent // 16) * 16


def lanes(n):
    return -(-n // 128) * 128


def prep_kernel(first_ref, second_ref, time_ref, proj_ref, w1_ref, w2_ref, wz_ref):
    taps, channels, latent = first_ref.shape
    slot = slot_of(latent)
    row = lax.broadcasted_iota(jnp.int32, (latent, w1_ref.shape[1]), 0)
    col = lax.broadcasted_iota(jnp.int32, (latent, w1_ref.shape[1]), 1)
    w1 = jnp.zeros(w1_ref.shape, F32)
    for tap in range(taps):
        base = tap // 3 * slot + tap % 3 * latent
        place = jnp.where(col == row + base, 1.0, 0.0).astype(BF16)
        w1 = w1 + dot(first_ref[tap], place)
    w1_ref[...] = w1.astype(BF16)
    for b in range(3):
        g = [second_ref[3 * a + b].astype(F32) for a in range(3)]
        outer = 0.5 * (g[0] + g[2])
        forms = [g[0], -outer - 0.5 * g[1], outer - 0.5 * g[1], -g[2]]
        for k in range(4):
            w2_ref[k, :, b * channels:(b + 1) * channels] = forms[k].astype(BF16)
    spare = w2_ref.shape[2] - 3 * channels
    if spare:
        w2_ref[:, :, 3 * channels:] = jnp.zeros((4, channels, spare), BF16)
    proj = proj_ref[...]
    zero = jnp.zeros((latent, channels), F32)
    pt = [dot(proj, time_ref[k]) for k in range(3)]
    left = jnp.concatenate([proj.astype(F32), zero, zero, zero], axis=0)
    right = jnp.concatenate([pt[1], pt[0], pt[2], zero], axis=0)
    wz_ref[:, 0:channels] = left.astype(BF16)
    wz_ref[:, channels:] = right.astype(BF16)


def convolve(batches, latents, dims, rows, tile, tiles, w1_ref, w2_ref, wz_ref, s_ref, store):
    latent, local_rows, width, channels = dims
    slot = slot_of(latent)
    pairs = rows // 2
    n_mid = (rows + 2) * width
    extra = (rows - local_rows) // 2
    span = pairs * width

    def shift_cols(v, by):
        lane = lax.broadcasted_iota(jnp.int32, v.shape, 1) % width
        if by > 0:
            return jnp.where(lane == 0, jnp.zeros_like(v), pltpu.roll(v, 1, 1))
        return jnp.where(lane == width - 1, jnp.zeros_like(v), pltpu.roll(v, v.shape[1] - 1, 1))

    def conv1(i, frames):
        for j, f in enumerate(frames):
            a = latents(f)
            parts = [shift_cols(a, 1), a, shift_cols(a, -1)]
            if slot > 3 * latent:
                parts.append(jnp.zeros((slot - 3 * latent, a.shape[1]), F32))
            b = jnp.concatenate(parts, axis=0).astype(BF16)
            x = jnp.concatenate([b[:, k * width:k * width + n_mid] for k in range(3)], axis=0)
            v = silu(dot(w1_ref[:, 0:3 * slot], x))
            row = lax.broadcasted_iota(jnp.int32, v.shape, 1) // width
            low = jnp.where(tile == 0, extra + 1, 0)
            high = jnp.where(tile == tiles - 1, extra + 1 + local_rows, rows + 2)
            v = jnp.where((row < low) | (row >= high), 0.0, v).astype(BF16).astype(F32)
            d = [v[:, k * width:(k + 1) * width] for k in range(rows + 2)]
            at = slice(j * span, (j + 1) * span)
            for k in range(4):
                forms = []
                for p in range(pairs):
                    e = d[2 * p:2 * p + 4]
                    forms.append((e[0] - e[2], e[1] + e[2], e[2] - e[1], e[1] - e[3])[k])
                form = jnp.concatenate(forms, axis=1) if pairs > 1 else forms[0]
                s_ref[i % 2, k, 0:channels, at] = shift_cols(form, 1).astype(BF16)
                s_ref[i % 2, k, channels:2 * channels, at] = form.astype(BF16)
                s_ref[i % 2, k, 2 * channels:, at] = shift_cols(form, -1).astype(BF16)

    def conv2(i, frames):
        used = len(frames) * span
        m = [dot(w2_ref[k, :, 0:3 * channels], s_ref[i % 2, k, :, 0:used]) for k in range(4)]
        for parity, second in enumerate(((m[0] - m[1]) + m[2], (m[3] - m[1]) - m[2])):
            x = jnp.concatenate([second.astype(BF16), silu(second).astype(BF16)], axis=0)
            z = dot(wz_ref[...], x)
            for j, f in enumerate(frames):
                for p in range(pairs):
                    at = (j * pairs + p) * width
                    store(f, 2 * p + parity, z[:, at:at + width])

    conv1(0, batches[0])
    for i, frames in enumerate(batches):
        if i + 1 < len(batches):
            conv1(i + 1, batches[i + 1])
        conv2(i, frames)


def z_parts(z_ref, f, latent):
    return [z_ref[f, k * latent:(k + 1) * latent, :] for k in range(3)]


def step0_kernel(
    dims, frames, levels, tiles, keep_ref, noise_ref, prev_ref, own_ref, next_ref,
    w1_ref, w2_ref, wz_ref, upd_ref, fwd_ref, bwd_ref, s_ref, z_ref,
):
    latent, local_rows, width, channels = dims
    rows = local_rows + 4
    position = lax.rem(lax.axis_index("level") + levels - 1, levels)
    tile = lax.axis_index("tile")

    def latents(f):
        lo, hi = f * latent, (f + 1) * latent
        return jnp.concatenate(
            [
                prev_ref[lo:hi, (local_rows - 4) * width:], own_ref[lo:hi, :],
                next_ref[lo:hi, 0:4 * width],
            ],
            axis=1,
        ).astype(F32)

    def store(f, row, z):
        z_ref[f, :, row * width:(row + 1) * width] = z

    convolve(
        [(f,) for f in range(frames)], latents, dims, rows, tile, tiles,
        w1_ref, w2_ref, wz_ref, s_ref, store,
    )
    skip = 2 * width
    for f in range(frames):
        z = z_parts(z_ref, f, latent)[0]
        if f > 0:
            z = z + z_parts(z_ref, f - 1, latent)[1]
        if f + 1 < frames:
            z = z + z_parts(z_ref, f + 1, latent)[2]
        lo, hi = f * latent, (f + 1) * latent
        q = latents(f)[:, skip:skip + rows * width]
        upd = keep_ref[0, position, f] * q - noise_ref[0, position, f] * z
        upd_ref[lo:hi, :] = upd
        if f == 0:
            bwd_ref[0:latent, :] = z_parts(z_ref, 0, latent)[2]
            bwd_ref[latent:, :] = upd
        if f == frames - 1:
            fwd_ref[0:latent, :] = z_parts(z_ref, f, latent)[1]
            fwd_ref[latent:, :] = upd


def window(f, dims, frames, prev_ref, own_ref, next_ref):
    latent, local_rows, width, _ = dims
    lo, hi = (frames + f) * latent, (frames + f + 1) * latent
    return jnp.concatenate(
        [
            prev_ref[lo:hi, (local_rows - 2) * width:], own_ref[lo:hi, :],
            next_ref[lo:hi, 0:2 * width],
        ],
        axis=1,
    ).astype(F32)


def inside(v, dims, tile, tiles):
    local_rows, width = dims[1], dims[2]
    row = lax.broadcasted_iota(jnp.int32, v.shape, 1) // width
    low = jnp.where(tile == 0, 2, 0)
    high = jnp.where(tile == tiles - 1, 2 + local_rows, local_rows + 4)
    return jnp.where((row < low) | (row >= high), 0.0, v).astype(BF16).astype(F32)


def inner_kernel(
    dims, frames, levels, tiles, prev_ref, own_ref, next_ref, upd_ref,
    w1_ref, w2_ref, wz_ref, lat_ref, zin_ref, s_ref,
):
    latent, local_rows, width, channels = dims
    level, tile = lax.axis_index("level"), lax.axis_index("tile")

    def latents(f):
        fresh = window(f, dims, frames, prev_ref, own_ref, next_ref)
        v = jnp.where(level == 0, fresh, upd_ref[f * latent:(f + 1) * latent, :])
        v = inside(v, dims, tile, tiles)
        lat_ref[f - 1] = v[:, 2 * width:(2 + local_rows) * width]
        return v

    def store(f, row, z):
        zin_ref[f - 1, :, row * width:(row + 1) * width] = z

    inner = list(range(1, frames - 1))
    batches = [tuple(inner[k:k + 2]) for k in range(0, len(inner), 2)]
    convolve(
        batches, latents, dims, local_rows, tile, tiles, w1_ref, w2_ref, wz_ref, s_ref, store
    )


def outer_kernel(
    dims, frames, levels, tiles, keep_ref, noise_ref, prev_ref, own_ref, next_ref, upd_ref,
    fwd_ref, bwd_ref, fwd_in_ref, bwd_in_ref, lat_ref, zin_ref, w1_ref, w2_ref, wz_ref,
    out_ref, s_ref, z_ref, edge_ref,
):
    latent, local_rows, width, channels = dims
    level, tile = lax.axis_index("level"), lax.axis_index("tile")
    before = lax.rem(level + levels - 1, levels)
    last = frames - 1
    slots = {-1: 0, 0: 1, last: 2, frames: 3}

    def latents(f):
        fresh = window(min(max(f, 0), last) if f >= 0 else last,
                       dims, frames, prev_ref, own_ref, next_ref)
        if f == -1:
            earlier = lax.rem(level + levels - 2, levels)
            v = fwd_in_ref[latent:, :] - noise_ref[0, earlier, last] * bwd_ref[0:latent, :]
            v = jnp.where(level == 1, fresh, v)
            v = jnp.where(level == 0, 0.0, v)
        elif f == 0:
            rate = jnp.where(level == 1, 0.0, noise_ref[0, before, 0])
            v = upd_ref[0:latent, :] - rate * fwd_in_ref[0:latent, :]
            v = jnp.where(level == 0, fresh, v)
        elif f == last:
            v = upd_ref[last * latent:, :] - noise_ref[0, before, last] * bwd_in_ref[0:latent, :]
            v = jnp.where(level == 0, fresh, v)
        else:
            rate = jnp.where(level == 0, 0.0, noise_ref[0, level, 0])
            v = bwd_in_ref[latent:, :] - rate * fwd_ref[0:latent, :]
            v = jnp.where(level == levels - 1, 0.0, v)
        v = inside(v, dims, tile, tiles)
        edge_ref[slots[f]] = v[:, 2 * width:(2 + local_rows) * width]
        return v

    def store(f, row, z):
        z_ref[slots[f], :, row * width:(row + 1) * width] = z

    convolve(
        [(-1, 0), (last, frames)], latents, dims, local_rows, tile, tiles,
        w1_ref, w2_ref, wz_ref, s_ref, store,
    )

    def parts(f):
        if f in slots:
            return z_parts(z_ref, slots[f], latent)
        return z_parts(zin_ref, f - 1, latent)

    for f in range(frames):
        z = parts(f)[0] + parts(f - 1)[1] + parts(f + 1)[2]
        q = edge_ref[slots[f]] if f in slots else lat_ref[f - 1]
        out = keep_ref[1, level, f] * q - noise_ref[1, level, f] * z
        out_ref[f * latent:(f + 1) * latent, :] = out.astype(BF16)


def per_device(
    queue_init, noise_frames, conv_first, conv_second, time_weight, out_proj, keep_coef, noise_coef
):
    steps = noise_frames.shape[0]
    _, frames, latent, rows, width = queue_init.shape
    assert steps == 2 and rows >= 4 and rows % 2 == 0
    channels = conv_second.shape[2]
    levels, tiles = lax.axis_size("level"), lax.axis_size("tile")
    level = lax.axis_index("level")
    flat = frames * latent
    n_out, n_wide = rows * width, (rows + 4) * width
    dims = (latent, rows, width, channels)
    slot = slot_of(latent)

    smem = pl.BlockSpec(memory_space=pltpu.SMEM)
    vmem = pl.BlockSpec(memory_space=pltpu.VMEM)

    def shape(*dims_and_type):
        return jax.ShapeDtypeStruct(dims_and_type[:-1], dims_and_type[-1])

    def call(body, operands, scalars, outs, scratch, row_frames, grant):
        flops = 2 * row_frames * width * channels * 8 * channels
        return pl.pallas_call(
            body,
            out_shape=tuple(outs),
            in_specs=[smem] * scalars + [vmem] * (len(operands) - scalars),
            out_specs=(vmem,) * len(outs),
            scratch_shapes=scratch,
            compiler_params=pltpu.CompilerParams(vmem_limit_bytes=grant * MIB),
            cost_estimate=pl.CostEstimate(
                flops=flops, bytes_accessed=channels * channels * 24, transcendentals=0
            ),
        )(*operands)

    def permute(x, dl, dt):
        pairs = [
            (l * tiles + t, ((l + dl) % levels) * tiles + t + dt)
            for l in range(levels) for t in range(tiles) if 0 <= t + dt < tiles
        ]
        return lax.ppermute(x, ("level", "tile"), pairs)

    queue = queue_init[0].reshape(flat, n_out)
    noise = noise_frames.reshape(steps, flat, n_out)
    pack = jnp.concatenate([jnp.where(level == levels - 1, noise[0], queue), noise[1]], axis=0)
    own = permute(pack, 2, 0)
    prev = permute(pack, 2, 1)
    nxt = permute(pack, 2, -1)

    w1, w2, wz = call(
        prep_kernel,
        (
            conv_first.reshape(9, channels, latent), conv_second.reshape(9, channels, channels),
            time_weight, out_proj,
        ),
        0,
        [
            shape(channels, lanes(3 * slot), BF16), shape(4, channels, lanes(3 * channels), BF16),
            shape(4 * latent, 2 * channels, BF16),
        ],
        [], 4, 16,
    )
    weights = (w1, w2, wz)
    coefs = (keep_coef, noise_coef)
    around = (prev, own, nxt)

    def spare(pairs_of_rows):
        return pltpu.VMEM((2, 4, 3 * channels, pairs_of_rows * width), BF16)

    place = (dims, frames, levels, tiles)
    upd, fwd, bwd = call(
        functools.partial(step0_kernel, *place),
        coefs + around + weights, 2,
        [shape(flat, n_wide, F32)] + [shape(2 * latent, n_wide, F32)] * 2,
        [spare(rows // 2 + 2), pltpu.VMEM((frames, 4 * latent, n_wide), F32)],
        frames * (rows + 4), 32,
    )
    fwd_in = lax.ppermute(fwd, "level", [(l, l + 1) for l in range(1, levels - 1)])
    bwd_in = lax.ppermute(bwd, "level", [(l, (l - 1) % levels) for l in range(levels)])
    lat, zin = call(
        functools.partial(inner_kernel, *place),
        around + (upd,) + weights, 0,
        [shape(frames - 2, latent, n_out, F32), shape(frames - 2, 4 * latent, n_out, F32)],
        [spare(rows)], (frames - 2) * rows, 32,
    )
    (out,) = call(
        functools.partial(outer_kernel, *place),
        coefs + around + (upd, fwd, bwd, fwd_in, bwd_in, lat, zin) + weights, 2,
        [shape(flat, n_out, BF16)],
        [
            spare(rows), pltpu.VMEM((4, 4 * latent, n_out), F32),
            pltpu.VMEM((4, latent, n_out), F32),
        ],
        4 * rows, 32,
    )
    return out.reshape(1, frames, latent, rows, width)


def solution(mesh):
    return jax.shard_map(
        per_device,
        mesh=mesh,
        in_specs=(
            P("level", None, None, "tile", None),
            P(None, None, None, "tile", None),
            P(),
            P(),
            P(),
            P(),
            P(),
            P(),
        ),
        out_specs=P("level", None, None, "tile", None),
        check_vma=False,
    )
```

time: 130 us -> 40.3 us (0.31)
  the two profiles are of different devices: /device:TPU:1 before, /device:TPU:13 now
where the time goes in v2:
time: 40.3 us; the launch traced here: 39.9 us
  Pallas kernels  21 us (52%)
  starting transfers between devices  12.1 us (30%)
  local copies, waits for them, and re-layouts  5.23 us (13%)
  other arithmetic  0.79 us (2%)
  waiting for transfers between devices  0.62 us (2%)
    pallas_call x4, Pallas kernels, call(): pl.pallas_call(body, out_shape=tuple(outs), in_specs=[smem] * scalars + [...  21 us
    ppermute x3, starting transfers between devices, permute(): return lax.ppermute(x, ('level', 'tile'), pairs)  8.33 us
    unnamed x12, local copies, waits for them, and re-layouts  4.61 us
    ppermute x1, starting transfers between devices, per_device(): lax.ppermute(fwd, 'level', [(l, l + 1) for l in range(1, levels - 1)])  3.57 us
  transfers between devices with their start and end apart: 5, of which 1 were waited for; matrix products, arithmetic and copies ran while one was open for 3% of the time, Pallas kernels for 10%

profile of v2, /device:TPU:13, one launch (start us, length us, event | category | flops | bytes accessed | tf_op | source)
XLA Modules:
  0.0 39.9 jit_solution(5887980010498473361)
XLA Ops:
  0.0 0.0 copy-start.4
  0.0 0.0 copy-start.3
  0.0 0.8 %fusion = (bf16[1,4,4,4,128]{4,3,2,1,0:T(4,128)(2,1)S(1)}, bf16[1,4,4,4,128]{4,3,2,1,0:T(4,128)(2,1)S(1)}) fusion(bf16[2,4,4,4,128]{4,3,2,1,0:T(4,128)(2,1)} %param.9, bf16[1,4,4,4,128]{4,3,2,1,0:T(4,128)(2,1)} %param.8, pred[]{:T(512)S(6)} %eq.3), kind=kLoop, calls=%fused_computation.3 | loop fusion | flops 8192 | bytes 81921 | tf_op jit(solution)/shard_map/slice | solution.py:308
  0.8 3.0 %collective-permute-start.2 = (bf16[32,512]{1,0:T(8,128)(2,1)S(1)}, bf16[32,512]{1,0:T(8,128)(2,1)S(1)}, u32[]{:S(2)}, u32[]{:S(2)}) collective-permute-start(bf16[32,512]{1,0:T(8,128)(2,1)S(1)} %bitcast_dynamic-update-slice_fusion), channel_id=1, source_target_pairs={{1,16},{2,17},{3,18},{4,19},{5,20},{6,21},{7,22},{9,24},{10,25},{1... | collective-permute-start | bytes 98312 | tf_op jit(solution)/shard_map/ppermute | solution.py:304
  3.9 0.3 collective-permute-start.1
  4.2 4.9 %collective-permute-start = (bf16[32,512]{1,0:T(8,128)(2,1)S(1)}, bf16[32,512]{1,0:T(8,128)(2,1)S(1)}, u32[]{:S(2)}, u32[]{:S(2)}) collective-permute-start(bf16[32,512]{1,0:T(8,128)(2,1)S(1)} %bitcast_dynamic-update-slice_fusion), channel_id=1, source_target_pairs={{0,17},{1,18},{2,19},{3,20},{4,21},{5,22},{6,23},{8,25},{9,26},{10... | collective-permute-start | bytes 98312 | tf_op jit(solution)/shard_map/ppermute | solution.py:304
  9.2 1.2 %copy.9 = bf16[3,3,320,4]{3,2,1,0:T(8,128)(2,1)S(1)} copy(bf16[3,3,320,4]{2,3,1,0:T(4,128)(2,1)} %param.10) | data formatting | bytes 46080 | tf_op args[2]
  10.4 0.0 copy-start
  10.4 1.6 %copy-done = bf16[3,3,320,320]{3,2,1,0:T(8,128)(2,1)S(1)} copy-done((bf16[3,3,320,320]{3,2,1,0:T(8,128)(2,1)S(1)}, bf16[3,3,320,320]{3,2,1,0:T(8,128)(2,1)}, u32[]{:S(2)}) %copy-start) | copy-done | bytes 1843224
  12.0 0.0 copy-start.1
  12.0 1.1 %copy-done.1 = bf16[3,320,320]{2,1,0:T(8,128)(2,1)S(1)} copy-done((bf16[3,320,320]{2,1,0:T(8,128)(2,1)S(1)}, bf16[3,320,320]{2,1,0:T(8,128)(2,1)}, u32[]{:S(2)}) %copy-start.1) | copy-done | bytes 614424
  13.1 0.0 copy-start.2
  13.1 0.7 %copy-done.2 = bf16[4,320]{1,0:T(4,128)(2,1)S(1)} copy-done((bf16[4,320]{1,0:T(4,128)(2,1)S(1)}, bf16[4,320]{1,0:T(4,128)(2,1)}, u32[]{:S(2)}) %copy-start.2) | copy-done | bytes 2584
  13.8 1.4 %shard_map.82 = (bf16[320,128]{1,0:T(8,128)(2,1)S(1)}, bf16[4,320,1024]{2,1,0:T(8,128)(2,1)S(1)}, bf16[16,640]{1,0:T(8,128)(2,1)S(1)}) custom-call(bf16[9,320,4]{2,1,0:T(8,128)(2,1)S(1)} %bitcast.10, bf16[9,320,320]{2,1,0:T(8,128)(2,1)S(1)} %bitcast.11, bf16[3,320,320]{2,1,0:T(8,128)(2,1)S(1)} %copy-done.1, bf16[4,320]{1,0:T(4,128)(2,1)S(1)} %copy-done.2), custom_call_target="tpu_custom_call" | custom-call | flops 838860800 | bytes 2457600 | tf_op jit(solution)/shard_map/pallas_call | solution.py:287
  15.2 0.0 collective-permute-done.2.next_ref
  15.2 0.0 collective-permute-done.1.own_ref
  15.2 0.0 collective-permute-done.prev_ref
  15.2 0.0 copy-done.4
  15.2 0.0 copy-done.3
  15.2 11.0 %shard_map.83 = (f32[16,1024]{1,0:T(8,128)S(1)}, f32[8,1024]{1,0:T(8,128)S(1)}, f32[8,1024]{1,0:T(8,128)S(1)}) custom-call(f32[2,4,4]{2,1,0:T(4,128)S(1)} %copy-done.3, f32[2,4,4]{2,1,0:T(4,128)S(1)} %copy-done.4, bf16[32,512]{1,0:T(8,128)(2,1)S(1)} %collective-permute-done.prev_ref, bf16[32,512]{1,0:T(8,128)(2,1)S(1)} %collective-permute-done.1.own_ref, ...), custom_call_target="tpu_custom_call" | custom-call | flops 6710886400 | bytes 2457600 | tf_op jit(solution)/shard_map/pallas_call | solution.py:287
  26.2 3.6 %collective-permute-start.3 = (f32[8,1024]{1,0:T(8,128)S(1)}, f32[8,1024]{1,0:T(8,128)S(1)}, u32[]{:S(2)}, u32[]{:S(2)}) collective-permute-start(f32[8,1024]{1,0:T(8,128)S(1)} %get-tuple-element.17.fwd_ref), channel_id=1, source_target_pairs={{8,16},{16,24},{9,17},{17,25},{10,18},{18,26},{11,19},{19,27},{12,... | collective-permute-start | bytes 98312 | tf_op jit(solution)/shard_map/ppermute | solution.py:341
  29.8 0.2 collective-permute-start.4
  30.0 2.7 %shard_map.84 = (f32[2,4,512]{2,1,0:T(4,128)S(1)}, f32[2,16,512]{2,1,0:T(8,128)S(1)}) custom-call(bf16[32,512]{1,0:T(8,128)(2,1)S(1)} %collective-permute-done.prev_ref, bf16[32,512]{1,0:T(8,128)(2,1)S(1)} %collective-permute-done.1.own_ref, bf16[32,512]{1,0:T(8,128)(2,1)S(1)} %collective-permute-done.2.next_ref, f32[16,1024]{1,0:T(8,128)S(1)} %get-tuple-element.16.upd_ref, ...), custom_call_target="tpu_custom_call" | custom-call | flops 1677721600 | bytes 2457600 | tf_op jit(solution)/shard_map/pallas_call | solution.py:287
  32.7 0.0 collective-permute-done.3.fwd_in_ref
  32.7 0.6 %collective-permute-done.4.bwd_in_ref = f32[8,1024]{1,0:T(8,128)S(1)} collective-permute-done((f32[8,1024]{1,0:T(8,128)S(1)}, f32[8,1024]{1,0:T(8,128)S(1)}, u32[]{:S(2)}, u32[]{:S(2)}) %collective-permute-start.4) | collective-permute-done | bytes 32800 | tf_op jit(solution)/shard_map/ppermute | solution.py:342
  33.3 6.0 %shard_map.85 = bf16[16,512]{1,0:T(8,128)(2,1)S(1)} custom-call(f32[2,4,4]{2,1,0:T(4,128)S(1)} %copy-done.3, f32[2,4,4]{2,1,0:T(4,128)S(1)} %copy-done.4, bf16[32,512]{1,0:T(8,128)(2,1)S(1)} %collective-permute-done.prev_ref, bf16[32,512]{1,0:T(8,128)(2,1)S(1)} %collective-permute-done.1.own_ref, bf16[32,512]{1,0:T(8,128)(2,1)S(1)} %collective-permute-done.2.next_ref, ...), custom_call_target="tpu_custom_call" | custom-call | flops 3355443200 | bytes 2457600 | tf_op jit(solution)/shard_map/pallas_call | solution.py:287
  39.3 0.6 %reshape.18 = bf16[1,4,4,4,128]{4,3,2,1,0:T(4,128)(2,1)} reshape(bf16[16,512]{1,0:T(8,128)(2,1)S(1)} %shard_map.85) | data formatting | bytes 32768 | tf_op jit(solution)/shard_map/reshape | solution.py:359
  (2 shorter events, 0.0 us)
Async XLA Ops:
  0.0 15.2 %copy-start.4 = (f32[2,4,4]{2,1,0:T(4,128)S(1)}, f32[2,4,4]{2,1,0:T(4,128)}, u32[]{:S(2)}) copy-start(f32[2,4,4]{2,1,0:T(4,128)} %noise_ref.3) | copy-start | bytes 388
  0.0 15.2 %copy-start.3 = (f32[2,4,4]{2,1,0:T(4,128)S(1)}, f32[2,4,4]{2,1,0:T(4,128)}, u32[]{:S(2)}) copy-start(f32[2,4,4]{2,1,0:T(4,128)} %keep_ref.3) | copy-start | bytes 388
  0.8 14.3 %collective-permute-start.2 = (bf16[32,512]{1,0:T(8,128)(2,1)S(1)}, bf16[32,512]{1,0:T(8,128)(2,1)S(1)}, u32[]{:S(2)}, u32[]{:S(2)}) collective-permute-start(bf16[32,512]{1,0:T(8,128)(2,1)S(1)} %bitcast_dynamic-update-slice_fusion), channel_id=1, source_target_pairs={{1,16},{2,17},{3,18},{4,19},{5,20},{6,21},{7,22},{9,24},{10,25},{1... | collective-permute-start | bytes 98312 | tf_op jit(solution)/shard_map/ppermute | solution.py:304
  3.9 11.3 %collective-permute-start.1 = (bf16[32,512]{1,0:T(8,128)(2,1)S(1)}, bf16[32,512]{1,0:T(8,128)(2,1)S(1)}, u32[]{:S(2)}, u32[]{:S(2)}) collective-permute-start(bf16[32,512]{1,0:T(8,128)(2,1)S(1)} %bitcast_dynamic-update-slice_fusion), channel_id=1, source_target_pairs={{0,16},{1,17},{2,18},{3,19},{4,20},{5,21},{6,22},{7,23},{8,24},{9,... | collective-permute-start | bytes 98312 | tf_op jit(solution)/shard_map/ppermute | solution.py:304
  4.2 11.0 %collective-permute-start = (bf16[32,512]{1,0:T(8,128)(2,1)S(1)}, bf16[32,512]{1,0:T(8,128)(2,1)S(1)}, u32[]{:S(2)}, u32[]{:S(2)}) collective-permute-start(bf16[32,512]{1,0:T(8,128)(2,1)S(1)} %bitcast_dynamic-update-slice_fusion), channel_id=1, source_target_pairs={{0,17},{1,18},{2,19},{3,20},{4,21},{5,22},{6,23},{8,25},{9,26},{10... | collective-permute-start | bytes 98312 | tf_op jit(solution)/shard_map/ppermute | solution.py:304
  10.4 1.6 %copy-start = (bf16[3,3,320,320]{3,2,1,0:T(8,128)(2,1)S(1)}, bf16[3,3,320,320]{3,2,1,0:T(8,128)(2,1)}, u32[]{:S(2)}) copy-start(bf16[3,3,320,320]{3,2,1,0:T(8,128)(2,1)} %param.11) | copy-start | bytes 5529604
  12.0 1.1 %copy-start.1 = (bf16[3,320,320]{2,1,0:T(8,128)(2,1)S(1)}, bf16[3,320,320]{2,1,0:T(8,128)(2,1)}, u32[]{:S(2)}) copy-start(bf16[3,320,320]{2,1,0:T(8,128)(2,1)} %time_ref.1) | copy-start | bytes 1843204
  13.1 0.7 %copy-start.2 = (bf16[4,320]{1,0:T(4,128)(2,1)S(1)}, bf16[4,320]{1,0:T(4,128)(2,1)}, u32[]{:S(2)}) copy-start(bf16[4,320]{1,0:T(4,128)(2,1)} %proj_ref.1) | copy-start | bytes 7684
  26.2 6.5 %collective-permute-start.3 = (f32[8,1024]{1,0:T(8,128)S(1)}, f32[8,1024]{1,0:T(8,128)S(1)}, u32[]{:S(2)}, u32[]{:S(2)}) collective-permute-start(f32[8,1024]{1,0:T(8,128)S(1)} %get-tuple-element.17.fwd_ref), channel_id=1, source_target_pairs={{8,16},{16,24},{9,17},{17,25},{10,18},{18,26},{11,19},{19,27},{12,... | collective-permute-start | bytes 98312 | tf_op jit(solution)/shard_map/ppermute | solution.py:341
  29.8 3.6 %collective-permute-start.4 = (f32[8,1024]{1,0:T(8,128)S(1)}, f32[8,1024]{1,0:T(8,128)S(1)}, u32[]{:S(2)}, u32[]{:S(2)}) collective-permute-start(f32[8,1024]{1,0:T(8,128)S(1)} %get-tuple-element.18.bwd_ref), channel_id=1, source_target_pairs={{0,24},{8,0},{16,8},{24,16},{1,25},{9,1},{17,9},{25,17},{2,26},{10... | collective-permute-start | bytes 98312 | tf_op jit(solution)/shard_map/ppermute | solution.py:342

commit v3 on v2

--- a/solution.py
+++ b/solution.py
@@ -12,11 +12,6 @@
 MIB = 1024 * 1024
 
 
-def silu(v):
-    half = 0.5 * v
-    return half * jnp.tanh(half) + half
-
-
 def dot(a, b):
     return jnp.dot(a, b, preferred_element_type=F32)
 
@@ -29,79 +24,114 @@
     return -(-n // 128) * 128
 
 
-def prep_kernel(first_ref, second_ref, time_ref, proj_ref, w1_ref, w2_ref, wz_ref):
-    taps, channels, latent = first_ref.shape
+def prep_kernel(
+    first_hbm, second_hbm, time_hbm, proj_hbm, w1_ref, w2_ref, wz_ref,
+    first_ref, second_ref, time_ref, proj_ref, second_sem, sems,
+):
+    taps, latent, channels = first_hbm.shape
     slot = slot_of(latent)
-    row = lax.broadcasted_iota(jnp.int32, (latent, w1_ref.shape[1]), 0)
-    col = lax.broadcasted_iota(jnp.int32, (latent, w1_ref.shape[1]), 1)
-    w1 = jnp.zeros(w1_ref.shape, F32)
-    for tap in range(taps):
-        base = tap // 3 * slot + tap % 3 * latent
-        place = jnp.where(col == row + base, 1.0, 0.0).astype(BF16)
-        w1 = w1 + dot(first_ref[tap], place)
-    w1_ref[...] = w1.astype(BF16)
+    loads = [
+        pltpu.make_async_copy(src, dst, sems.at[k])
+        for k, (src, dst) in enumerate(
+            ((first_hbm, first_ref), (proj_hbm, proj_ref), (time_hbm, time_ref))
+        )
+    ]
+    slabs = [
+        pltpu.make_async_copy(second_hbm.at[k], second_ref.at[k], second_sem.at[k])
+        for k in range(taps)
+    ]
     for b in range(3):
-        g = [second_ref[3 * a + b].astype(F32) for a in range(3)]
-        outer = 0.5 * (g[0] + g[2])
-        forms = [g[0], -outer - 0.5 * g[1], outer - 0.5 * g[1], -g[2]]
-        for k in range(4):
-            w2_ref[k, :, b * channels:(b + 1) * channels] = forms[k].astype(BF16)
+        for a in range(3):
+            slabs[3 * a + b].start()
+    for load in loads:
+        load.start()
     spare = w2_ref.shape[2] - 3 * channels
     if spare:
         w2_ref[:, :, 3 * channels:] = jnp.zeros((4, channels, spare), BF16)
+    for b in range(3):
+        for a in range(3):
+            slabs[3 * a + b].wait()
+        g = [0.5 * second_ref[3 * a + b].astype(F32) for a in range(3)]
+        outer = 0.5 * (g[0] + g[2])
+        middle = 0.5 * g[1]
+        forms = [g[0], -outer - middle, outer - middle, -g[2]]
+        for k in range(4):
+            w2_ref[k, :, b * channels:(b + 1) * channels] = forms[k].astype(BF16)
+    for load in loads:
+        load.wait()
+    pad = jnp.zeros((slot - 3 * latent, channels), F32)
+    pieces = []
+    for a in range(3):
+        pieces += [first_ref[3 * a + b].astype(F32) for b in range(3)]
+        if slot > 3 * latent:
+            pieces.append(pad)
+    w1 = 0.5 * jnp.concatenate(pieces, axis=0)
+    w1 = jnp.pad(w1, ((0, w1_ref.shape[1] - 3 * slot), (0, lanes(channels) - channels)))
+    w1_ref[...] = w1.T[0:channels].astype(BF16)
     proj = proj_ref[...]
     zero = jnp.zeros((latent, channels), F32)
     pt = [dot(proj, time_ref[k]) for k in range(3)]
-    left = jnp.concatenate([proj.astype(F32), zero, zero, zero], axis=0)
+    left = jnp.concatenate([2.0 * proj.astype(F32), zero, zero, zero], axis=0)
     right = jnp.concatenate([pt[1], pt[0], pt[2], zero], axis=0)
     wz_ref[:, 0:channels] = left.astype(BF16)
     wz_ref[:, channels:] = right.astype(BF16)
+
+
+def gate(half):
+    return half * jnp.tanh(half) + half
 
 
 def convolve(batches, latents, dims, rows, tile, tiles, w1_ref, w2_ref, wz_ref, s_ref, store):
     latent, local_rows, width, channels = dims
     slot = slot_of(latent)
     pairs = rows // 2
-    n_mid = (rows + 2) * width
     extra = (rows - local_rows) // 2
     span = pairs * width
-
-    def shift_cols(v, by):
-        lane = lax.broadcasted_iota(jnp.int32, v.shape, 1) % width
-        if by > 0:
-            return jnp.where(lane == 0, jnp.zeros_like(v), pltpu.roll(v, 1, 1))
-        return jnp.where(lane == width - 1, jnp.zeros_like(v), pltpu.roll(v, v.shape[1] - 1, 1))
+    column = lax.broadcasted_iota(jnp.int32, (1, width), 1)
+    not_first = jnp.where(column == 0, 0.0, 1.0)
+    not_last = jnp.where(column == width - 1, 0.0, 1.0)
+    top = jnp.where(tile == 0, 0.0, 1.0)
+    bottom = jnp.where(tile == tiles - 1, 0.0, 1.0)
+
+    def from_left(v):
+        return pltpu.roll(v, 1, 1) * not_first.astype(v.dtype)
+
+    def from_right(v):
+        return pltpu.roll(v, width - 1, 1) * not_last.astype(v.dtype)
 
     def conv1(i, frames):
         for j, f in enumerate(frames):
             a = latents(f)
-            parts = [shift_cols(a, 1), a, shift_cols(a, -1)]
-            if slot > 3 * latent:
-                parts.append(jnp.zeros((slot - 3 * latent, a.shape[1]), F32))
-            b = jnp.concatenate(parts, axis=0).astype(BF16)
-            x = jnp.concatenate([b[:, k * width:k * width + n_mid] for k in range(3)], axis=0)
-            v = silu(dot(w1_ref[:, 0:3 * slot], x))
-            row = lax.broadcasted_iota(jnp.int32, v.shape, 1) // width
-            low = jnp.where(tile == 0, extra + 1, 0)
-            high = jnp.where(tile == tiles - 1, extra + 1 + local_rows, rows + 2)
-            v = jnp.where((row < low) | (row >= high), 0.0, v).astype(BF16).astype(F32)
-            d = [v[:, k * width:(k + 1) * width] for k in range(rows + 2)]
-            at = slice(j * span, (j + 1) * span)
-            for k in range(4):
-                forms = []
-                for p in range(pairs):
-                    e = d[2 * p:2 * p + 4]
-                    forms.append((e[0] - e[2], e[1] + e[2], e[2] - e[1], e[1] - e[3])[k])
-                form = jnp.concatenate(forms, axis=1) if pairs > 1 else forms[0]
-                s_ref[i % 2, k, 0:channels, at] = shift_cols(form, 1).astype(BF16)
-                s_ref[i % 2, k, channels:2 * channels, at] = form.astype(BF16)
-                s_ref[i % 2, k, 2 * channels:, at] = shift_cols(form, -1).astype(BF16)
+            b = []
+            for r in range(rows + 4):
+                v = a[:, r * width:(r + 1) * width]
+                parts = [from_left(v), v, from_right(v)]
+                if slot > 3 * latent:
+                    parts.append(jnp.zeros((slot - 3 * latent, width), F32))
+                b.append(jnp.concatenate(parts, axis=0))
+            x = []
+            for r in range(rows + 2):
+                v = jnp.concatenate(b[r:r + 3], axis=0)
+                if r <= extra:
+                    v = v * top
+                if r > extra + local_rows:
+                    v = v * bottom
+                x.append(v.astype(BF16))
+            v = gate(dot(w1_ref[:, 0:3 * slot], jnp.concatenate(x, axis=1))).astype(BF16)
+            d = [v[:, r * width:(r + 1) * width] for r in range(rows + 2)]
+            for p in range(pairs):
+                e = d[2 * p:2 * p + 4]
+                at = slice(j * span + p * width, j * span + (p + 1) * width)
+                for k, form in enumerate((e[0] - e[2], e[1] + e[2], e[2] - e[1], e[1] - e[3])):
+                    s_ref[i % 2, k, 0:channels, at] = from_left(form)
+                    s_ref[i % 2, k, channels:2 * channels, at] = form
+                    s_ref[i % 2, k, 2 * channels:, at] = from_right(form)
 
     def conv2(i, frames):
         used = len(frames) * span
         m = [dot(w2_ref[k, :, 0:3 * channels], s_ref[i % 2, k, :, 0:used]) for k in range(4)]
-        for parity, second in enumerate(((m[0] - m[1]) + m[2], (m[3] - m[1]) - m[2])):
-            x = jnp.concatenate([second.astype(BF16), silu(second).astype(BF16)], axis=0)
+        for parity, half in enumerate(((m[0] - m[1]) + m[2], (m[3] - m[1]) - m[2])):
+            x = jnp.concatenate([half.astype(BF16), gate(half).astype(BF16)], axis=0)
             z = dot(wz_ref[...], x)
             for j, f in enumerate(frames):
                 for p in range(pairs):
@@ -113,6 +143,10 @@
         if i + 1 < len(batches):
             conv1(i + 1, batches[i + 1])
         conv2(i, frames)
+
+
+def coef(ref, step, position, f):
+    return ref[step, pl.ds(position, 1), f:f + 1]
 
 
 def z_parts(z_ref, f, latent):
@@ -154,7 +188,7 @@
             z = z + z_parts(z_ref, f + 1, latent)[2]
         lo, hi = f * latent, (f + 1) * latent
         q = latents(f)[:, skip:skip + rows * width]
-        upd = keep_ref[0, position, f] * q - noise_ref[0, position, f] * z
+        upd = coef(keep_ref, 0, position, f) * q - coef(noise_ref, 0, position, f) * z
         upd_ref[lo:hi, :] = upd
         if f == 0:
             bwd_ref[0:latent, :] = z_parts(z_ref, 0, latent)[2]
@@ -224,18 +258,18 @@
                        dims, frames, prev_ref, own_ref, next_ref)
         if f == -1:
             earlier = lax.rem(level + levels - 2, levels)
-            v = fwd_in_ref[latent:, :] - noise_ref[0, earlier, last] * bwd_ref[0:latent, :]
+            v = fwd_in_ref[latent:, :] - coef(noise_ref, 0, earlier, last) * bwd_ref[0:latent, :]
             v = jnp.where(level == 1, fresh, v)
             v = jnp.where(level == 0, 0.0, v)
         elif f == 0:
-            rate = jnp.where(level == 1, 0.0, noise_ref[0, before, 0])
+            rate = jnp.where(level == 1, 0.0, coef(noise_ref, 0, before, 0))
             v = upd_ref[0:latent, :] - rate * fwd_in_ref[0:latent, :]
             v = jnp.where(level == 0, fresh, v)
         elif f == last:
-            v = upd_ref[last * latent:, :] - noise_ref[0, before, last] * bwd_in_ref[0:latent, :]
+            v = upd_ref[last * latent:, :] - coef(noise_ref, 0, before, last) * bwd_in_ref[0:latent, :]
             v = jnp.where(level == 0, fresh, v)
         else:
-            rate = jnp.where(level == 0, 0.0, noise_ref[0, level, 0])
+            rate = jnp.where(level == 0, 0.0, coef(noise_ref, 0, level, 0))
             v = bwd_in_ref[latent:, :] - rate * fwd_ref[0:latent, :]
             v = jnp.where(level == levels - 1, 0.0, v)
         v = inside(v, dims, tile, tiles)
@@ -258,8 +292,9 @@
     for f in range(frames):
         z = parts(f)[0] + parts(f - 1)[1] + parts(f + 1)[2]
         q = edge_ref[slots[f]] if f in slots else lat_ref[f - 1]
-        out = keep_ref[1, level, f] * q - noise_ref[1, level, f] * z
-        out_ref[f * latent:(f + 1) * latent, :] = out.astype(BF16)
+        out = coef(keep_ref, 1, level, f) * q - coef(noise_ref, 1, level, f) * z
+        cut = [out[:, None, r * width:(r + 1) * width] for r in range(local_rows)]
+        out_ref[f * latent:(f + 1) * latent] = jnp.concatenate(cut, axis=1).astype(BF16)
 
 
 def per_device(
@@ -276,18 +311,17 @@
     dims = (latent, rows, width, channels)
     slot = slot_of(latent)
 
-    smem = pl.BlockSpec(memory_space=pltpu.SMEM)
     vmem = pl.BlockSpec(memory_space=pltpu.VMEM)
 
     def shape(*dims_and_type):
         return jax.ShapeDtypeStruct(dims_and_type[:-1], dims_and_type[-1])
 
-    def call(body, operands, scalars, outs, scratch, row_frames, grant):
+    def call(body, operands, outs, scratch, row_frames, grant, space=vmem):
         flops = 2 * row_frames * width * channels * 8 * channels
         return pl.pallas_call(
             body,
             out_shape=tuple(outs),
-            in_specs=[smem] * scalars + [vmem] * (len(operands) - scalars),
+            in_specs=[space] * len(operands),
             out_specs=(vmem,) * len(outs),
             scratch_shapes=scratch,
             compiler_params=pltpu.CompilerParams(vmem_limit_bytes=grant * MIB),
@@ -296,6 +330,9 @@
             ),
         )(*operands)
 
+    def in_hbm(x):
+        return pltpu.with_memory_space_constraint(x, pltpu.HBM)
+
     def permute(x, dl, dt):
         pairs = [
             (l * tiles + t, ((l + dl) % levels) * tiles + t + dt)
@@ -310,18 +347,18 @@
     prev = permute(pack, 2, 1)
     nxt = permute(pack, 2, -1)
 
+    second = conv_second.reshape(9, channels, channels)
+    first = jnp.transpose(conv_first, (0, 1, 3, 2)).reshape(9, latent, channels)
     w1, w2, wz = call(
         prep_kernel,
-        (
-            conv_first.reshape(9, channels, latent), conv_second.reshape(9, channels, channels),
-            time_weight, out_proj,
-        ),
-        0,
+        tuple(in_hbm(x) for x in (first, second, time_weight, out_proj)),
         [
             shape(channels, lanes(3 * slot), BF16), shape(4, channels, lanes(3 * channels), BF16),
             shape(4 * latent, 2 * channels, BF16),
         ],
-        [], 4, 16,
+        [pltpu.VMEM(x.shape, BF16) for x in (first, second, time_weight, out_proj)]
+        + [pltpu.SemaphoreType.DMA((9,)), pltpu.SemaphoreType.DMA((3,))],
+        4, 16, pl.BlockSpec(memory_space=pltpu.HBM),
     )
     weights = (w1, w2, wz)
     coefs = (keep_coef, noise_coef)
@@ -333,7 +370,7 @@
     place = (dims, frames, levels, tiles)
     upd, fwd, bwd = call(
         functools.partial(step0_kernel, *place),
-        coefs + around + weights, 2,
+        coefs + around + weights,
         [shape(flat, n_wide, F32)] + [shape(2 * latent, n_wide, F32)] * 2,
         [spare(rows // 2 + 2), pltpu.VMEM((frames, 4 * latent, n_wide), F32)],
         frames * (rows + 4), 32,
@@ -342,14 +379,14 @@
     bwd_in = lax.ppermute(bwd, "level", [(l, (l - 1) % levels) for l in range(levels)])
     lat, zin = call(
         functools.partial(inner_kernel, *place),
-        around + (upd,) + weights, 0,
+        around + (upd,) + weights,
         [shape(frames - 2, latent, n_out, F32), shape(frames - 2, 4 * latent, n_out, F32)],
         [spare(rows)], (frames - 2) * rows, 32,
     )
     (out,) = call(
         functools.partial(outer_kernel, *place),
-        coefs + around + (upd, fwd, bwd, fwd_in, bwd_in, lat, zin) + weights, 2,
-        [shape(flat, n_out, BF16)],
+        coefs + around + (upd, fwd, bwd, fwd_in, bwd_in, lat, zin) + weights,
+        [shape(flat, rows, width, BF16)],
         [
             spare(rows), pltpu.VMEM((4, 4 * latent, n_out), F32),
             pltpu.VMEM((4, latent, n_out), F32),

time: 40.3 us -> 34.5 us (0.86)
  the two profiles are of different devices: /device:TPU:13 before, /device:TPU:17 now
where the time goes in v3:
time: 34.5 us; the launch traced here: 34.3 us
  Pallas kernels  18.8 us (54%)
  starting transfers between devices  13.1 us (38%)
  waiting for transfers between devices  1.51 us (4%)
  other arithmetic  0.79 us (2%)
    pallas_call x4, Pallas kernels, call(): pl.pallas_call(body, out_shape=tuple(outs), in_specs=[space] * len(operan...  18.8 us
    ppermute x3, starting transfers between devices, permute(): return lax.ppermute(x, ('level', 'tile'), pairs)  7.43 us
    ppermute x1, starting transfers between devices, per_device(): lax.ppermute(fwd, 'level', [(l, l + 1) for l in range(1, levels - 1)])  5.39 us
    ppermute x1, waiting for transfers between devices, per_device(): lax.ppermute(bwd, 'level', [(l, (l - 1) % levels) for l in range(levels)])  0.9 us
    slice x1, other arithmetic, per_device(): noise[1]  0.79 us
  transfers between devices with their start and end apart: 5, of which 2 were waited for; matrix products, arithmetic and copies ran while one was open for 0% of the time, Pallas kernels for 15%

profile of v3, /device:TPU:17, one launch (start us, length us, event | category | flops | bytes accessed | tf_op | source)
XLA Modules:
  0.0 34.3 jit_solution(9679925504603447529)
XLA Ops:
  0.0 0.0 copy-start.1
  0.0 0.0 copy-start
  0.0 0.8 %fusion = (bf16[1,4,4,4,128]{4,3,2,1,0:T(4,128)(2,1)S(1)}, bf16[1,4,4,4,128]{4,3,2,1,0:T(4,128)(2,1)S(1)}) fusion(bf16[2,4,4,4,128]{4,3,2,1,0:T(4,128)(2,1)} %param.9, bf16[1,4,4,4,128]{4,3,2,1,0:T(4,128)(2,1)} %param.8, pred[]{:T(512)S(6)} %eq.3), kind=kLoop, calls=%fused_computation.3 | loop fusion | flops 8192 | bytes 81921 | tf_op jit(solution)/shard_map/slice | solution.py:345
  0.8 3.9 %collective-permute-start.2 = (bf16[32,512]{1,0:T(8,128)(2,1)S(1)}, bf16[32,512]{1,0:T(8,128)(2,1)S(1)}, u32[]{:S(2)}, u32[]{:S(2)}) collective-permute-start(bf16[32,512]{1,0:T(8,128)(2,1)S(1)} %bitcast_dynamic-update-slice_fusion), channel_id=1, source_target_pairs={{1,16},{2,17},{3,18},{4,19},{5,20},{6,21},{7,22},{9,24},{10,25},{1... | collective-permute-start | bytes 98312 | tf_op jit(solution)/shard_map/ppermute | solution.py:341
  4.8 0.3 collective-permute-start.1
  5.1 3.1 %collective-permute-start = (bf16[32,512]{1,0:T(8,128)(2,1)S(1)}, bf16[32,512]{1,0:T(8,128)(2,1)S(1)}, u32[]{:S(2)}, u32[]{:S(2)}) collective-permute-start(bf16[32,512]{1,0:T(8,128)(2,1)S(1)} %bitcast_dynamic-update-slice_fusion), channel_id=1, source_target_pairs={{0,17},{1,18},{2,19},{3,20},{4,21},{5,22},{6,23},{8,25},{9,26},{10... | collective-permute-start | bytes 98312 | tf_op jit(solution)/shard_map/ppermute | solution.py:341
  8.3 2.7 %shard_map.82 = (bf16[320,128]{1,0:T(8,128)(2,1)S(1)}, bf16[4,320,1024]{2,1,0:T(8,128)(2,1)S(1)}, bf16[16,640]{1,0:T(8,128)(2,1)S(1)}) custom-call(bf16[9,4,320]{2,1,0:T(4,128)(2,1)} %bitcast.16, bf16[9,320,320]{2,1,0:T(8,128)(2,1)} %bitcast.15, bf16[3,320,320]{2,1,0:T(8,128)(2,1)} %time_hbm.1, bf16[4,320]{1,0:T(4,128)(2,1)} %proj_hbm.1), custom_call_target="tpu_custom_call" | custom-call | flops 838860800 | bytes 2457600 | tf_op jit(solution)/shard_map/pallas_call | solution.py:321
  10.9 0.0 collective-permute-done.2.next_ref
  10.9 0.0 collective-permute-done.1.own_ref
  11.0 0.6 %collective-permute-done.prev_ref = bf16[32,512]{1,0:T(8,128)(2,1)S(1)} collective-permute-done((bf16[32,512]{1,0:T(8,128)(2,1)S(1)}, bf16[32,512]{1,0:T(8,128)(2,1)S(1)}, u32[]{:S(2)}, u32[]{:S(2)}) %collective-permute-start) | collective-permute-done | bytes 32800 | tf_op jit(solution)/shard_map/ppermute | solution.py:341
  11.6 0.0 copy-done.1
  11.6 0.0 copy-done
  11.6 8.4 %shard_map.83 = (f32[16,1024]{1,0:T(8,128)S(1)}, f32[8,1024]{1,0:T(8,128)S(1)}, f32[8,1024]{1,0:T(8,128)S(1)}) custom-call(f32[2,4,4]{2,1,0:T(4,128)S(1)} %copy-done, f32[2,4,4]{2,1,0:T(4,128)S(1)} %copy-done.1, bf16[32,512]{1,0:T(8,128)(2,1)S(1)} %collective-permute-done.prev_ref, bf16[32,512]{1,0:T(8,128)(2,1)S(1)} %collective-permute-done.1.own_ref, ...), custom_call_target="tpu_custom_call" | custom-call | flops 6710886400 | bytes 2457600 | tf_op jit(solution)/shard_map/pallas_call | solution.py:321
  20.0 5.4 %collective-permute-start.3 = (f32[8,1024]{1,0:T(8,128)S(1)}, f32[8,1024]{1,0:T(8,128)S(1)}, u32[]{:S(2)}, u32[]{:S(2)}) collective-permute-start(f32[8,1024]{1,0:T(8,128)S(1)} %get-tuple-element.17.fwd_ref), channel_id=1, source_target_pairs={{8,16},{16,24},{9,17},{17,25},{10,18},{18,26},{11,19},{19,27},{12,... | collective-permute-start | bytes 98312 | tf_op jit(solution)/shard_map/ppermute | solution.py:378
  25.4 0.2 collective-permute-start.4
  25.7 2.4 %shard_map.84 = (f32[2,4,512]{2,1,0:T(4,128)S(1)}, f32[2,16,512]{2,1,0:T(8,128)S(1)}) custom-call(bf16[32,512]{1,0:T(8,128)(2,1)S(1)} %collective-permute-done.prev_ref, bf16[32,512]{1,0:T(8,128)(2,1)S(1)} %collective-permute-done.1.own_ref, bf16[32,512]{1,0:T(8,128)(2,1)S(1)} %collective-permute-done.2.next_ref, f32[16,1024]{1,0:T(8,128)S(1)} %get-tuple-element.16.upd_ref, ...), custom_call_target="tpu_custom_call" | custom-call | flops 1677721600 | bytes 2457600 | tf_op jit(solution)/shard_map/pallas_call | solution.py:321
  28.1 0.0 collective-permute-done.3.fwd_in_ref
  28.1 0.9 %collective-permute-done.4.bwd_in_ref = f32[8,1024]{1,0:T(8,128)S(1)} collective-permute-done((f32[8,1024]{1,0:T(8,128)S(1)}, f32[8,1024]{1,0:T(8,128)S(1)}, u32[]{:S(2)}, u32[]{:S(2)}) %collective-permute-start.4) | collective-permute-done | bytes 32800 | tf_op jit(solution)/shard_map/ppermute | solution.py:379
  29.0 5.3 %shard_map.85 = bf16[16,4,128]{2,1,0:T(4,128)(2,1)} custom-call(f32[2,4,4]{2,1,0:T(4,128)S(1)} %copy-done, f32[2,4,4]{2,1,0:T(4,128)S(1)} %copy-done.1, bf16[32,512]{1,0:T(8,128)(2,1)S(1)} %collective-permute-done.prev_ref, bf16[32,512]{1,0:T(8,128)(2,1)S(1)} %collective-permute-done.1.own_ref, bf16[32,512]{1,0:T(8,128)(2,1)S(1)} %collective-permute-done.2.next_ref, ...), custom_call_target="tpu_custom_call" | custom-call | flops 3355443200 | bytes 2457600 | tf_op jit(solution)/shard_map/pallas_call | solution.py:321
  (2 shorter events, 0.0 us)
Async XLA Ops:
  0.0 11.6 %copy-start.1 = (f32[2,4,4]{2,1,0:T(4,128)S(1)}, f32[2,4,4]{2,1,0:T(4,128)}, u32[]{:S(2)}) copy-start(f32[2,4,4]{2,1,0:T(4,128)} %noise_ref.3) | copy-start | bytes 388
  0.0 11.6 %copy-start = (f32[2,4,4]{2,1,0:T(4,128)S(1)}, f32[2,4,4]{2,1,0:T(4,128)}, u32[]{:S(2)}) copy-start(f32[2,4,4]{2,1,0:T(4,128)} %keep_ref.3) | copy-start | bytes 388
  0.8 10.1 %collective-permute-start.2 = (bf16[32,512]{1,0:T(8,128)(2,1)S(1)}, bf16[32,512]{1,0:T(8,128)(2,1)S(1)}, u32[]{:S(2)}, u32[]{:S(2)}) collective-permute-start(bf16[32,512]{1,0:T(8,128)(2,1)S(1)} %bitcast_dynamic-update-slice_fusion), channel_id=1, source_target_pairs={{1,16},{2,17},{3,18},{4,19},{5,20},{6,21},{7,22},{9,24},{10,25},{1... | collective-permute-start | bytes 98312 | tf_op jit(solution)/shard_map/ppermute | solution.py:341
  4.8 6.2 %collective-permute-start.1 = (bf16[32,512]{1,0:T(8,128)(2,1)S(1)}, bf16[32,512]{1,0:T(8,128)(2,1)S(1)}, u32[]{:S(2)}, u32[]{:S(2)}) collective-permute-start(bf16[32,512]{1,0:T(8,128)(2,1)S(1)} %bitcast_dynamic-update-slice_fusion), channel_id=1, source_target_pairs={{0,16},{1,17},{2,18},{3,19},{4,20},{5,21},{6,22},{7,23},{8,24},{9,... | collective-permute-start | bytes 98312 | tf_op jit(solution)/shard_map/ppermute | solution.py:341
  5.1 6.4 %collective-permute-start = (bf16[32,512]{1,0:T(8,128)(2,1)S(1)}, bf16[32,512]{1,0:T(8,128)(2,1)S(1)}, u32[]{:S(2)}, u32[]{:S(2)}) collective-permute-start(bf16[32,512]{1,0:T(8,128)(2,1)S(1)} %bitcast_dynamic-update-slice_fusion), channel_id=1, source_target_pairs={{0,17},{1,18},{2,19},{3,20},{4,21},{5,22},{6,23},{8,25},{9,26},{10... | collective-permute-start | bytes 98312 | tf_op jit(solution)/shard_map/ppermute | solution.py:341
  20.0 8.1 %collective-permute-start.3 = (f32[8,1024]{1,0:T(8,128)S(1)}, f32[8,1024]{1,0:T(8,128)S(1)}, u32[]{:S(2)}, u32[]{:S(2)}) collective-permute-start(f32[8,1024]{1,0:T(8,128)S(1)} %get-tuple-element.17.fwd_ref), channel_id=1, source_target_pairs={{8,16},{16,24},{9,17},{17,25},{10,18},{18,26},{11,19},{19,27},{12,... | collective-permute-start | bytes 98312 | tf_op jit(solution)/shard_map/ppermute | solution.py:378
  25.4 3.6 %collective-permute-start.4 = (f32[8,1024]{1,0:T(8,128)S(1)}, f32[8,1024]{1,0:T(8,128)S(1)}, u32[]{:S(2)}, u32[]{:S(2)}) collective-permute-start(f32[8,1024]{1,0:T(8,128)S(1)} %get-tuple-element.18.bwd_ref), channel_id=1, source_target_pairs={{0,24},{8,0},{16,8},{24,16},{1,25},{9,1},{17,9},{25,17},{2,26},{10... | collective-permute-start | bytes 98312 | tf_op jit(solution)/shard_map/ppermute | solution.py:379

commit v4 on v3

--- a/solution.py
+++ b/solution.py
@@ -145,6 +145,12 @@
         conv2(i, frames)
 
 
+def neighbours(odd_ref, even_ref, tile, lo, hi):
+    odd, even = odd_ref[lo:hi, :].astype(F32), even_ref[lo:hi, :].astype(F32)
+    is_even = lax.rem(tile, 2) == 0
+    return jnp.where(is_even, odd, even), jnp.where(is_even, even, odd)
+
+
 def coef(ref, step, position, f):
     return ref[step, pl.ds(position, 1), f:f + 1]
 
@@ -154,23 +160,24 @@
 
 
 def step0_kernel(
-    dims, frames, levels, tiles, keep_ref, noise_ref, prev_ref, own_ref, next_ref,
-    w1_ref, w2_ref, wz_ref, upd_ref, fwd_ref, bwd_ref, s_ref, z_ref,
+    dims, frames, levels, tiles, keep_ref, noise_ref, odd_ref, own_ref, even_ref,
+    w1_ref, w2_ref, wz_ref, full_ref, near_ref, far_ref, s_ref, z_ref,
 ):
     latent, local_rows, width, channels = dims
     rows = local_rows + 4
-    position = lax.rem(lax.axis_index("level") + levels - 1, levels)
+    level = lax.axis_index("level")
+    position = lax.rem(level + 1, levels)
+    even = lax.rem(level, 2) == 0
+    flat = frames * latent
     tile = lax.axis_index("tile")
 
     def latents(f):
         lo, hi = f * latent, (f + 1) * latent
+        prev, after = neighbours(odd_ref, even_ref, tile, lo, hi)
+        own = own_ref[lo:hi, :].astype(F32)
         return jnp.concatenate(
-            [
-                prev_ref[lo:hi, (local_rows - 4) * width:], own_ref[lo:hi, :],
-                next_ref[lo:hi, 0:4 * width],
-            ],
-            axis=1,
-        ).astype(F32)
+            [prev[:, (local_rows - 4) * width:], own, after[:, 0:4 * width]], axis=1
+        )
 
     def store(f, row, z):
         z_ref[f, :, row * width:(row + 1) * width] = z
@@ -189,25 +196,25 @@
         lo, hi = f * latent, (f + 1) * latent
         q = latents(f)[:, skip:skip + rows * width]
         upd = coef(keep_ref, 0, position, f) * q - coef(noise_ref, 0, position, f) * z
-        upd_ref[lo:hi, :] = upd
+        full_ref[lo:hi, :] = upd
         if f == 0:
-            bwd_ref[0:latent, :] = z_parts(z_ref, 0, latent)[2]
-            bwd_ref[latent:, :] = upd
+            first = jnp.concatenate([z_parts(z_ref, 0, latent)[2], upd], axis=0)
         if f == frames - 1:
-            fwd_ref[0:latent, :] = z_parts(z_ref, f, latent)[1]
-            fwd_ref[latent:, :] = upd
-
-
-def window(f, dims, frames, prev_ref, own_ref, next_ref):
+            last = jnp.concatenate([z_parts(z_ref, f, latent)[1], upd], axis=0)
+    full_ref[flat:flat + latent, :] = last[0:latent]
+    full_ref[flat + latent:, :] = first[0:latent]
+    near_ref[...] = jnp.where(even, first, last)
+    far_ref[...] = jnp.where(even, last, first)
+
+
+def window(f, dims, frames, tile, odd_ref, own_ref, even_ref):
     latent, local_rows, width, _ = dims
     lo, hi = (frames + f) * latent, (frames + f + 1) * latent
+    prev, after = neighbours(odd_ref, even_ref, tile, lo, hi)
+    own = own_ref[lo:hi, :].astype(F32)
     return jnp.concatenate(
-        [
-            prev_ref[lo:hi, (local_rows - 2) * width:], own_ref[lo:hi, :],
-            next_ref[lo:hi, 0:2 * width],
-        ],
-        axis=1,
-    ).astype(F32)
+        [prev[:, (local_rows - 2) * width:], own, after[:, 0:2 * width]], axis=1
+    )
 
 
 def inside(v, dims, tile, tiles):
@@ -219,14 +226,14 @@
 
 
 def inner_kernel(
-    dims, frames, levels, tiles, prev_ref, own_ref, next_ref, upd_ref,
+    dims, frames, levels, tiles, odd_ref, own_ref, even_ref, upd_ref,
     w1_ref, w2_ref, wz_ref, lat_ref, zin_ref, s_ref,
 ):
     latent, local_rows, width, channels = dims
     level, tile = lax.axis_index("level"), lax.axis_index("tile")
 
     def latents(f):
-        fresh = window(f, dims, frames, prev_ref, own_ref, next_ref)
+        fresh = window(f, dims, frames, tile, odd_ref, own_ref, even_ref)
         v = jnp.where(level == 0, fresh, upd_ref[f * latent:(f + 1) * latent, :])
         v = inside(v, dims, tile, tiles)
         lat_ref[f - 1] = v[:, 2 * width:(2 + local_rows) * width]
@@ -243,34 +250,39 @@
 
 
 def outer_kernel(
-    dims, frames, levels, tiles, keep_ref, noise_ref, prev_ref, own_ref, next_ref, upd_ref,
-    fwd_ref, bwd_ref, fwd_in_ref, bwd_in_ref, lat_ref, zin_ref, w1_ref, w2_ref, wz_ref,
+    dims, frames, levels, tiles, keep_ref, noise_ref, odd_ref, own_ref, even_ref, upd_ref,
+    near_ref, far_ref, lat_ref, zin_ref, w1_ref, w2_ref, wz_ref,
     out_ref, s_ref, z_ref, edge_ref,
 ):
     latent, local_rows, width, channels = dims
     level, tile = lax.axis_index("level"), lax.axis_index("tile")
     before = lax.rem(level + levels - 1, levels)
     last = frames - 1
+    flat = frames * latent
+    even = lax.rem(level, 2) == 0
+    fwd, bwd = upd_ref[flat:flat + latent, :], upd_ref[flat + latent:, :]
+    near, far = near_ref[...], far_ref[...]
+    fwd_in, bwd_in = jnp.where(even, near, far), jnp.where(even, far, near)
     slots = {-1: 0, 0: 1, last: 2, frames: 3}
 
     def latents(f):
-        fresh = window(min(max(f, 0), last) if f >= 0 else last,
-                       dims, frames, prev_ref, own_ref, next_ref)
+        source = last if f < 0 else min(f, last)
+        fresh = window(source, dims, frames, tile, odd_ref, own_ref, even_ref)
         if f == -1:
             earlier = lax.rem(level + levels - 2, levels)
-            v = fwd_in_ref[latent:, :] - coef(noise_ref, 0, earlier, last) * bwd_ref[0:latent, :]
+            v = fwd_in[latent:] - coef(noise_ref, 0, earlier, last) * bwd
             v = jnp.where(level == 1, fresh, v)
             v = jnp.where(level == 0, 0.0, v)
         elif f == 0:
             rate = jnp.where(level == 1, 0.0, coef(noise_ref, 0, before, 0))
-            v = upd_ref[0:latent, :] - rate * fwd_in_ref[0:latent, :]
+            v = upd_ref[0:latent, :] - rate * fwd_in[0:latent]
             v = jnp.where(level == 0, fresh, v)
         elif f == last:
-            v = upd_ref[last * latent:, :] - coef(noise_ref, 0, before, last) * bwd_in_ref[0:latent, :]
+            v = upd_ref[last * latent:flat, :] - coef(noise_ref, 0, before, last) * bwd_in[0:latent]
             v = jnp.where(level == 0, fresh, v)
         else:
             rate = jnp.where(level == 0, 0.0, coef(noise_ref, 0, level, 0))
-            v = bwd_in_ref[latent:, :] - rate * fwd_ref[0:latent, :]
+            v = bwd_in[latent:] - rate * fwd
             v = jnp.where(level == levels - 1, 0.0, v)
         v = inside(v, dims, tile, tiles)
         edge_ref[slots[f]] = v[:, 2 * width:(2 + local_rows) * width]
@@ -333,19 +345,16 @@
     def in_hbm(x):
         return pltpu.with_memory_space_constraint(x, pltpu.HBM)
 
-    def permute(x, dl, dt):
-        pairs = [
-            (l * tiles + t, ((l + dl) % levels) * tiles + t + dt)
-            for l in range(levels) for t in range(tiles) if 0 <= t + dt < tiles
-        ]
-        return lax.ppermute(x, ("level", "tile"), pairs)
+    def swap(x, axis, size, partner):
+        pairs = [(i, partner(i)) for i in range(size) if 0 <= partner(i) < size]
+        return lax.ppermute(x, axis, pairs)
 
     queue = queue_init[0].reshape(flat, n_out)
     noise = noise_frames.reshape(steps, flat, n_out)
     pack = jnp.concatenate([jnp.where(level == levels - 1, noise[0], queue), noise[1]], axis=0)
-    own = permute(pack, 2, 0)
-    prev = permute(pack, 2, 1)
-    nxt = permute(pack, 2, -1)
+    own = pack
+    odd = swap(pack, "tile", tiles, lambda t: t - 1 if t % 2 == 0 else t + 1)
+    even = swap(pack, "tile", tiles, lambda t: t + 1 if t % 2 == 0 else t - 1)
 
     second = conv_second.reshape(9, channels, channels)
     first = jnp.transpose(conv_first, (0, 1, 3, 2)).reshape(9, latent, channels)
@@ -362,21 +371,22 @@
     )
     weights = (w1, w2, wz)
     coefs = (keep_coef, noise_coef)
-    around = (prev, own, nxt)
+    around = (odd, own, even)
 
     def spare(pairs_of_rows):
         return pltpu.VMEM((2, 4, 3 * channels, pairs_of_rows * width), BF16)
 
     place = (dims, frames, levels, tiles)
-    upd, fwd, bwd = call(
+    full, near, far = call(
         functools.partial(step0_kernel, *place),
         coefs + around + weights,
-        [shape(flat, n_wide, F32)] + [shape(2 * latent, n_wide, F32)] * 2,
+        [shape(flat + 2 * latent, n_wide, F32)] + [shape(2 * latent, n_wide, F32)] * 2,
         [spare(rows // 2 + 2), pltpu.VMEM((frames, 4 * latent, n_wide), F32)],
         frames * (rows + 4), 32,
     )
-    fwd_in = lax.ppermute(fwd, "level", [(l, l + 1) for l in range(1, levels - 1)])
-    bwd_in = lax.ppermute(bwd, "level", [(l, (l - 1) % levels) for l in range(levels)])
+    upd = swap(full, "level", levels, lambda d: (d + 2) % levels)
+    far = swap(far, "level", levels, lambda d: (d - 1 if d % 2 == 0 else d + 1) % levels)
+    near = swap(near, "level", levels, lambda d: d + 1 if d % 2 == 0 else d - 1)
     lat, zin = call(
         functools.partial(inner_kernel, *place),
         around + (upd,) + weights,
@@ -385,7 +395,7 @@
     )
     (out,) = call(
         functools.partial(outer_kernel, *place),
-        coefs + around + (upd, fwd, bwd, fwd_in, bwd_in, lat, zin) + weights,
+        coefs + around + (upd, near, far, lat, zin) + weights,
         [shape(flat, rows, width, BF16)],
         [
             spare(rows), pltpu.VMEM((4, 4 * latent, n_out), F32),

time: 34.5 us -> 30.7 us (0.89)
  the two profiles are of different devices: /device:TPU:17 before, /device:TPU:26 now
where the time goes in v4:
time: 30.7 us; the launch traced here: 30.5 us
  Pallas kernels  19 us (62%)
  starting transfers between devices  6.08 us (20%)
  waiting for transfers between devices  4.52 us (15%)
  other arithmetic  0.79 us (3%)
    pallas_call x4, Pallas kernels, call(): pl.pallas_call(body, out_shape=tuple(outs), in_specs=[space] * len(operan...  19 us
    ppermute x5, starting transfers between devices, swap(): return lax.ppermute(x, axis, pairs)  6.08 us
    ppermute x5, waiting for transfers between devices, swap(): return lax.ppermute(x, axis, pairs)  4.52 us
    slice x1, other arithmetic, per_device(): noise[1]  0.79 us
  transfers between devices with their start and end apart: 5, of which 2 were waited for; matrix products, arithmetic and copies ran while one was open for 0% of the time, Pallas kernels for 17%

profile of v4, /device:TPU:26, one launch (start us, length us, event | category | flops | bytes accessed | tf_op | source)
XLA Modules:
  0.0 30.5 jit_solution(9719586079871553151)
XLA Ops:
  0.0 0.0 copy-start.1
  0.0 0.0 copy-start
  0.0 0.8 %fusion = (bf16[1,4,4,4,128]{4,3,2,1,0:T(4,128)(2,1)S(1)}, bf16[1,4,4,4,128]{4,3,2,1,0:T(4,128)(2,1)S(1)}) fusion(bf16[2,4,4,4,128]{4,3,2,1,0:T(4,128)(2,1)} %param.9, bf16[1,4,4,4,128]{4,3,2,1,0:T(4,128)(2,1)} %param.8, pred[]{:T(512)S(6)} %eq.3), kind=kLoop, calls=%fused_computation.3 | loop fusion | flops 8192 | bytes 81921 | tf_op jit(solution)/shard_map/slice | solution.py:354
  0.8 1.6 %collective-permute-start.1 = (bf16[32,512]{1,0:T(8,128)(2,1)S(1)}, bf16[32,512]{1,0:T(8,128)(2,1)S(1)}, u32[]{:S(2)}, u32[]{:S(2)}) collective-permute-start(bf16[32,512]{1,0:T(8,128)(2,1)S(1)} %bitcast_dynamic-update-slice_fusion.own_ref), channel_id=1, source_target_pairs={{0,1},{1,0},{2,3},{3,2},{4,5},{5,4},{6,7},{7,6},{8,9},{9,8},{10,11... | collective-permute-start | bytes 98312 | tf_op jit(solution)/shard_map/ppermute | solution.py:350
  2.4 2.3 %collective-permute-start = (bf16[32,512]{1,0:T(8,128)(2,1)S(1)}, bf16[32,512]{1,0:T(8,128)(2,1)S(1)}, u32[]{:S(2)}, u32[]{:S(2)}) collective-permute-start(bf16[32,512]{1,0:T(8,128)(2,1)S(1)} %bitcast_dynamic-update-slice_fusion.own_ref), channel_id=1, source_target_pairs={{1,2},{2,1},{3,4},{4,3},{5,6},{6,5},{9,10},{10,9},{11,12},{12,11},... | collective-permute-start | bytes 98312 | tf_op jit(solution)/shard_map/ppermute | solution.py:350
  4.7 2.7 %shard_map.82 = (bf16[320,128]{1,0:T(8,128)(2,1)S(1)}, bf16[4,320,1024]{2,1,0:T(8,128)(2,1)S(1)}, bf16[16,640]{1,0:T(8,128)(2,1)S(1)}) custom-call(bf16[9,4,320]{2,1,0:T(4,128)(2,1)} %bitcast.16, bf16[9,320,320]{2,1,0:T(8,128)(2,1)} %bitcast.15, bf16[3,320,320]{2,1,0:T(8,128)(2,1)} %time_hbm.1, bf16[4,320]{1,0:T(4,128)(2,1)} %proj_hbm.1), custom_call_target="tpu_custom_call" | custom-call | flops 838860800 | bytes 2457600 | tf_op jit(solution)/shard_map/pallas_call | solution.py:333
  7.4 0.0 collective-permute-done.1.even_ref
  7.4 1.7 %collective-permute-done.odd_ref = bf16[32,512]{1,0:T(8,128)(2,1)S(1)} collective-permute-done((bf16[32,512]{1,0:T(8,128)(2,1)S(1)}, bf16[32,512]{1,0:T(8,128)(2,1)S(1)}, u32[]{:S(2)}, u32[]{:S(2)}) %collective-permute-start) | collective-permute-done | bytes 32800 | tf_op jit(solution)/shard_map/ppermute | solution.py:350
  9.1 0.0 copy-done.1
  9.1 0.0 copy-done
  9.1 8.4 %shard_map.83 = (f32[24,1024]{1,0:T(8,128)S(1)}, f32[8,1024]{1,0:T(8,128)S(1)}, f32[8,1024]{1,0:T(8,128)S(1)}) custom-call(f32[2,4,4]{2,1,0:T(4,128)S(1)} %copy-done, f32[2,4,4]{2,1,0:T(4,128)S(1)} %copy-done.1, bf16[32,512]{1,0:T(8,128)(2,1)S(1)} %collective-permute-done.odd_ref, bf16[32,512]{1,0:T(8,128)(2,1)S(1)} %bitcast_dynamic-update-slice_fusion.own_ref, ...), custom_call_target="tpu_custom_call" | custom-call | flops 6710886400 | bytes 2457600 | tf_op jit(solution)/shard_map/pallas_call | solution.py:333
  17.6 0.6 %collective-permute-start.2 = (f32[24,1024]{1,0:T(8,128)S(1)}, f32[24,1024]{1,0:T(8,128)S(1)}, u32[]{:S(2)}, u32[]{:S(2)}) collective-permute-start(f32[24,1024]{1,0:T(8,128)S(1)} %get-tuple-element.16), channel_id=1, source_target_pairs={{0,16},{8,24},{16,0},{24,8},{1,17},{9,25},{17,1},{25,9},{2,18},{10... | collective-permute-start | bytes 294920 | tf_op jit(solution)/shard_map/ppermute | solution.py:350
  18.2 0.0 collective-permute-start.3
  18.2 1.6 %collective-permute-start.4 = (f32[8,1024]{1,0:T(8,128)S(1)}, f32[8,1024]{1,0:T(8,128)S(1)}, u32[]{:S(2)}, u32[]{:S(2)}) collective-permute-start(f32[8,1024]{1,0:T(8,128)S(1)} %get-tuple-element.18), channel_id=1, source_target_pairs={{0,24},{8,16},{16,8},{24,0},{1,25},{9,17},{17,9},{25,1},{2,26},{10... | collective-permute-start | bytes 98312 | tf_op jit(solution)/shard_map/ppermute | solution.py:350
  19.8 2.8 %collective-permute-done.2.upd_ref = f32[24,1024]{1,0:T(8,128)S(1)} collective-permute-done((f32[24,1024]{1,0:T(8,128)S(1)}, f32[24,1024]{1,0:T(8,128)S(1)}, u32[]{:S(2)}, u32[]{:S(2)}) %collective-permute-start.2) | collective-permute-done | bytes 98336 | tf_op jit(solution)/shard_map/ppermute | solution.py:350
  22.6 2.4 %shard_map.84 = (f32[2,4,512]{2,1,0:T(4,128)S(1)}, f32[2,16,512]{2,1,0:T(8,128)S(1)}) custom-call(bf16[32,512]{1,0:T(8,128)(2,1)S(1)} %collective-permute-done.odd_ref, bf16[32,512]{1,0:T(8,128)(2,1)S(1)} %bitcast_dynamic-update-slice_fusion.own_ref, bf16[32,512]{1,0:T(8,128)(2,1)S(1)} %collective-permute-done.1.even_ref, ...), custom_call_target="tpu_custom_call" | custom-call | flops 1677721600 | bytes 2457600 | tf_op jit(solution)/shard_map/pallas_call | solution.py:333
  25.0 0.0 collective-permute-done.3.near_ref
  25.0 0.0 collective-permute-done.4.far_ref
  25.0 5.5 %shard_map.85 = bf16[16,4,128]{2,1,0:T(4,128)(2,1)} custom-call(f32[2,4,4]{2,1,0:T(4,128)S(1)} %copy-done, f32[2,4,4]{2,1,0:T(4,128)S(1)} %copy-done.1, bf16[32,512]{1,0:T(8,128)(2,1)S(1)} %collective-permute-done.odd_ref, bf16[32,512]{1,0:T(8,128)(2,1)S(1)} %bitcast_dynamic-update-slice_fusion.own_ref, bf16[32,512]{1,0:T(8,128)(2,1)S(1)} %collective-permute-done.1.even_ref, ...), custom_call_target="tpu_custom_call" | custom-call | flops 3355443200 | bytes 2457600 | tf_op jit(solution)/shard_map/pallas_call | solution.py:333
  (2 shorter events, 0.0 us)
Async XLA Ops:
  0.0 9.1 %copy-start.1 = (f32[2,4,4]{2,1,0:T(4,128)S(1)}, f32[2,4,4]{2,1,0:T(4,128)}, u32[]{:S(2)}) copy-start(f32[2,4,4]{2,1,0:T(4,128)} %noise_ref.3) | copy-start | bytes 388
  0.0 9.1 %copy-start = (f32[2,4,4]{2,1,0:T(4,128)S(1)}, f32[2,4,4]{2,1,0:T(4,128)}, u32[]{:S(2)}) copy-start(f32[2,4,4]{2,1,0:T(4,128)} %keep_ref.3) | copy-start | bytes 388
  0.8 6.5 %collective-permute-start.1 = (bf16[32,512]{1,0:T(8,128)(2,1)S(1)}, bf16[32,512]{1,0:T(8,128)(2,1)S(1)}, u32[]{:S(2)}, u32[]{:S(2)}) collective-permute-start(bf16[32,512]{1,0:T(8,128)(2,1)S(1)} %bitcast_dynamic-update-slice_fusion.own_ref), channel_id=1, source_target_pairs={{0,1},{1,0},{2,3},{3,2},{4,5},{5,4},{6,7},{7,6},{8,9},{9,8},{10,11... | collective-permute-start | bytes 98312 | tf_op jit(solution)/shard_map/ppermute | solution.py:350
  2.4 6.7 %collective-permute-start = (bf16[32,512]{1,0:T(8,128)(2,1)S(1)}, bf16[32,512]{1,0:T(8,128)(2,1)S(1)}, u32[]{:S(2)}, u32[]{:S(2)}) collective-permute-start(bf16[32,512]{1,0:T(8,128)(2,1)S(1)} %bitcast_dynamic-update-slice_fusion.own_ref), channel_id=1, source_target_pairs={{1,2},{2,1},{3,4},{4,3},{5,6},{6,5},{9,10},{10,9},{11,12},{12,11},... | collective-permute-start | bytes 98312 | tf_op jit(solution)/shard_map/ppermute | solution.py:350
  17.6 5.0 %collective-permute-start.2 = (f32[24,1024]{1,0:T(8,128)S(1)}, f32[24,1024]{1,0:T(8,128)S(1)}, u32[]{:S(2)}, u32[]{:S(2)}) collective-permute-start(f32[24,1024]{1,0:T(8,128)S(1)} %get-tuple-element.16), channel_id=1, source_target_pairs={{0,16},{8,24},{16,0},{24,8},{1,17},{9,25},{17,1},{25,9},{2,18},{10... | collective-permute-start | bytes 294920 | tf_op jit(solution)/shard_map/ppermute | solution.py:350
  18.2 6.8 %collective-permute-start.3 = (f32[8,1024]{1,0:T(8,128)S(1)}, f32[8,1024]{1,0:T(8,128)S(1)}, u32[]{:S(2)}, u32[]{:S(2)}) collective-permute-start(f32[8,1024]{1,0:T(8,128)S(1)} %get-tuple-element.17), channel_id=1, source_target_pairs={{0,8},{8,0},{16,24},{24,16},{1,9},{9,1},{17,25},{25,17},{2,10},{10... | collective-permute-start | bytes 98312 | tf_op jit(solution)/shard_map/ppermute | solution.py:350
  18.2 6.8 %collective-permute-start.4 = (f32[8,1024]{1,0:T(8,128)S(1)}, f32[8,1024]{1,0:T(8,128)S(1)}, u32[]{:S(2)}, u32[]{:S(2)}) collective-permute-start(f32[8,1024]{1,0:T(8,128)S(1)} %get-tuple-element.18), channel_id=1, source_target_pairs={{0,24},{8,16},{16,8},{24,0},{1,25},{9,17},{17,9},{25,1},{2,26},{10... | collective-permute-start | bytes 98312 | tf_op jit(solution)/shard_map/ppermute | solution.py:350

commit v5 on v4

--- a/solution.py
+++ b/solution.py
@@ -10,6 +10,8 @@
 BF16 = jnp.bfloat16
 F32 = jnp.float32
 MIB = 1024 * 1024
+AHEAD, SLOTS = 1, 2
+TILE, FORMS = 4, 6
 
 
 def dot(a, b):
@@ -25,15 +27,20 @@
 
 
 def prep_kernel(
-    first_hbm, second_hbm, time_hbm, proj_hbm, w1_ref, w2_ref, wz_ref,
+    first_hbm, second_hbm, time_hbm, proj_hbm, keep_hbm, noise_hbm,
+    w1_ref, w2_ref, wz_ref, keep_ref, noise_ref,
     first_ref, second_ref, time_ref, proj_ref, second_sem, sems,
 ):
     taps, latent, channels = first_hbm.shape
     slot = slot_of(latent)
+    main = channels // 128 * 128
     loads = [
         pltpu.make_async_copy(src, dst, sems.at[k])
         for k, (src, dst) in enumerate(
-            ((first_hbm, first_ref), (proj_hbm, proj_ref), (time_hbm, time_ref))
+            (
+                (first_hbm, first_ref), (proj_hbm, proj_ref), (time_hbm, time_ref),
+                (keep_hbm, keep_ref), (noise_hbm, noise_ref),
+            )
         )
     ]
     slabs = [
@@ -45,18 +52,36 @@
             slabs[3 * a + b].start()
     for load in loads:
         load.start()
-    spare = w2_ref.shape[2] - 3 * channels
+    full_blocks, tail = main // 128, channels - main
+    blocks = w2_ref.shape[1]
+    spare = blocks * 128 - 3 * channels
     if spare:
-        w2_ref[:, :, 3 * channels:] = jnp.zeros((4, channels, spare), BF16)
+        w2_ref[:, blocks - 1, :, 128 - spare:] = jnp.zeros((FORMS, channels, spare), BF16)
     for b in range(3):
         for a in range(3):
             slabs[3 * a + b].wait()
-        g = [0.5 * second_ref[3 * a + b].astype(F32) for a in range(3)]
-        outer = 0.5 * (g[0] + g[2])
-        middle = 0.5 * g[1]
-        forms = [g[0], -outer - middle, outer - middle, -g[2]]
-        for k in range(4):
-            w2_ref[k, :, b * channels:(b + 1) * channels] = forms[k].astype(BF16)
+        for lo in range(0, channels, 32):
+            at = slice(lo, min(lo + 32, channels))
+            g = [second_ref[3 * a + b, at].astype(F32) for a in range(3)]
+            ends = g[0] + g[2]
+            far_ends, middle = g[0] + 4.0 * g[2], 2.0 * g[1]
+            forms = [
+                0.125 * g[0], (1.0 / 12.0) * (ends + g[1]), (-1.0 / 24.0) * (ends - g[1]),
+                (-1.0 / 48.0) * (far_ends + middle), (1.0 / 96.0) * (far_ends - middle),
+                0.5 * g[2],
+            ]
+            for k, form in enumerate(forms):
+                form = form.astype(BF16)
+                for t in range(full_blocks):
+                    w2_ref[k, b * full_blocks + t, at] = form[:, t * 128:(t + 1) * 128]
+                start = 0
+                while start < tail:
+                    lane = b * tail + start
+                    size = min(tail - start, 128 - lane % 128)
+                    w2_ref[k, 3 * full_blocks + lane // 128, at, lane % 128:lane % 128 + size] = (
+                        form[:, main + start:main + start + size]
+                    )
+                    start += size
     for load in loads:
         load.wait()
     pad = jnp.zeros((slot - 3 * latent, channels), F32)
@@ -77,6 +102,27 @@
     wz_ref[:, channels:] = right.astype(BF16)
 
 
+def row_forms(d):
+    low = 4.0 * d[1]
+    even1, odd1 = d[4] - 4.0 * d[2], d[3] - low
+    even2, odd2 = d[4] - d[2], 2.0 * (d[3] - d[1])
+    return (
+        4.0 * d[0] + (even1 - d[2]), even1 + odd1, even1 - odd1, even2 + odd2, even2 - odd2,
+        low + (d[5] - 5.0 * d[3]),
+    )
+
+
+def row_sums(product, put):
+    n, h = product(1), 2.0 * product(2)
+    even1, odd1 = n - h, n + h
+    n, h = product(3), 2.0 * product(4)
+    even2, odd2 = n - h, n + h
+    put(1, -2.0 * odd2 - odd1)
+    put(2, -4.0 * even2 - even1)
+    put(0, (product(0) - even1) - even2)
+    put(3, (product(5) - odd1) - 8.0 * odd2)
+
+
 def gate(half):
     return half * jnp.tanh(half) + half
 
@@ -84,9 +130,10 @@
 def convolve(batches, latents, dims, rows, tile, tiles, w1_ref, w2_ref, wz_ref, s_ref, store):
     latent, local_rows, width, channels = dims
     slot = slot_of(latent)
-    pairs = rows // 2
+    parts_per = rows // TILE
+    main = channels // 128 * 128
     extra = (rows - local_rows) // 2
-    span = pairs * width
+    span = parts_per * width
     column = lax.broadcasted_iota(jnp.int32, (1, width), 1)
     not_first = jnp.where(column == 0, 0.0, 1.0)
     not_last = jnp.where(column == width - 1, 0.0, 1.0)
@@ -117,32 +164,50 @@
                 if r > extra + local_rows:
                     v = v * bottom
                 x.append(v.astype(BF16))
-            v = gate(dot(w1_ref[:, 0:3 * slot], jnp.concatenate(x, axis=1))).astype(BF16)
+            v = gate(dot(w1_ref[:, 0:3 * slot], jnp.concatenate(x, axis=1)))
             d = [v[:, r * width:(r + 1) * width] for r in range(rows + 2)]
-            for p in range(pairs):
-                e = d[2 * p:2 * p + 4]
-                at = slice(j * span + p * width, j * span + (p + 1) * width)
-                for k, form in enumerate((e[0] - e[2], e[1] + e[2], e[2] - e[1], e[1] - e[3])):
-                    s_ref[i % 2, k, 0:channels, at] = from_left(form)
-                    s_ref[i % 2, k, channels:2 * channels, at] = form
-                    s_ref[i % 2, k, 2 * channels:, at] = from_right(form)
+            for p in range(parts_per):
+                at = j * parts_per + p
+                for k, form in enumerate(row_forms(d[TILE * p:TILE * p + FORMS])):
+                    form = form.astype(BF16)
+                    for c, v in enumerate((from_left(form), form, from_right(form))):
+                        tail = 3 * main + c * (channels - main)
+                        s_ref[i % SLOTS, k, at, c * main:(c + 1) * main, :] = v[0:main]
+                        if main < channels:
+                            s_ref[i % SLOTS, k, at, tail:tail + channels - main, :] = v[main:]
 
     def conv2(i, frames):
-        used = len(frames) * span
-        m = [dot(w2_ref[k, :, 0:3 * channels], s_ref[i % 2, k, :, 0:used]) for k in range(4)]
-        for parity, half in enumerate(((m[0] - m[1]) + m[2], (m[3] - m[1]) - m[2])):
-            x = jnp.concatenate([half.astype(BF16), gate(half).astype(BF16)], axis=0)
+        def product(k):
+            x = [s_ref[i % SLOTS, k, p] for p in range(len(frames) * parts_per)]
+            w = jnp.concatenate([w2_ref[k, t] for t in range(w2_ref.shape[1])], axis=1)
+            return dot(w[:, 0:3 * channels], jnp.concatenate(x, axis=1))
+
+        ready = {}
+
+        def put(r, half):
+            ready[r] = jnp.concatenate([half.astype(BF16), gate(half).astype(BF16)], axis=0)
+
+        row_sums(product, put)
+        return ready
+
+    def project(frames, ready):
+        for r, x in ready.items():
             z = dot(wz_ref[...], x)
             for j, f in enumerate(frames):
-                for p in range(pairs):
-                    at = (j * pairs + p) * width
-                    store(f, 2 * p + parity, z[:, at:at + width])
-
-    conv1(0, batches[0])
-    for i, frames in enumerate(batches):
-        if i + 1 < len(batches):
+                for p in range(parts_per):
+                    at = (j * parts_per + p) * width
+                    store(f, TILE * p + r, z[:, at:at + width])
+
+    count = len(batches)
+    for i in range(min(AHEAD, count)):
+        conv1(i, batches[i])
+    for i in range(count):
+        if AHEAD == 1 and i + 1 < count:
             conv1(i + 1, batches[i + 1])
-        conv2(i, frames)
+        ready = conv2(i, batches[i])
+        if AHEAD == 2 and i + 2 < count:
+            conv1(i + 2, batches[i + 2])
+        project(batches[i], ready)
 
 
 def neighbours(odd_ref, even_ref, tile, lo, hi):
@@ -314,10 +379,10 @@
 ):
     steps = noise_frames.shape[0]
     _, frames, latent, rows, width = queue_init.shape
-    assert steps == 2 and rows >= 4 and rows % 2 == 0
     channels = conv_second.shape[2]
     levels, tiles = lax.axis_size("level"), lax.axis_size("tile")
     level = lax.axis_index("level")
+    assert steps == 2 and rows % TILE == 0 and levels % 4 == 0
     flat = frames * latent
     n_out, n_wide = rows * width, (rows + 4) * width
     dims = (latent, rows, width, channels)
@@ -358,30 +423,34 @@
 
     second = conv_second.reshape(9, channels, channels)
     first = jnp.transpose(conv_first, (0, 1, 3, 2)).reshape(9, latent, channels)
-    w1, w2, wz = call(
+    w1, w2, wz, keep, rate = call(
         prep_kernel,
-        tuple(in_hbm(x) for x in (first, second, time_weight, out_proj)),
+        tuple(
+            in_hbm(x)
+            for x in (first, second, time_weight, out_proj, keep_coef, noise_coef)
+        ),
         [
-            shape(channels, lanes(3 * slot), BF16), shape(4, channels, lanes(3 * channels), BF16),
+            shape(channels, lanes(3 * slot), BF16), shape(FORMS, lanes(3 * channels) // 128, channels, 128, BF16),
             shape(4 * latent, 2 * channels, BF16),
+            shape(*keep_coef.shape, F32), shape(*noise_coef.shape, F32),
         ],
         [pltpu.VMEM(x.shape, BF16) for x in (first, second, time_weight, out_proj)]
-        + [pltpu.SemaphoreType.DMA((9,)), pltpu.SemaphoreType.DMA((3,))],
+        + [pltpu.SemaphoreType.DMA((9,)), pltpu.SemaphoreType.DMA((5,))],
         4, 16, pl.BlockSpec(memory_space=pltpu.HBM),
     )
     weights = (w1, w2, wz)
-    coefs = (keep_coef, noise_coef)
+    coefs = (keep, rate)
     around = (odd, own, even)
 
-    def spare(pairs_of_rows):
-        return pltpu.VMEM((2, 4, 3 * channels, pairs_of_rows * width), BF16)
+    def spare(row_tiles):
+        return [pltpu.VMEM((SLOTS, FORMS, row_tiles, 3 * channels, width), BF16)]
 
     place = (dims, frames, levels, tiles)
     full, near, far = call(
         functools.partial(step0_kernel, *place),
         coefs + around + weights,
         [shape(flat + 2 * latent, n_wide, F32)] + [shape(2 * latent, n_wide, F32)] * 2,
-        [spare(rows // 2 + 2), pltpu.VMEM((frames, 4 * latent, n_wide), F32)],
+        spare(rows // TILE + 1) + [pltpu.VMEM((frames, 4 * latent, n_wide), F32)],
         frames * (rows + 4), 32,
     )
     upd = swap(full, "level", levels, lambda d: (d + 2) % levels)
@@ -391,15 +460,14 @@
         functools.partial(inner_kernel, *place),
         around + (upd,) + weights,
         [shape(frames - 2, latent, n_out, F32), shape(frames - 2, 4 * latent, n_out, F32)],
-        [spare(rows)], (frames - 2) * rows, 32,
+        spare(2 * rows // TILE), (frames - 2) * rows, 32,
     )
     (out,) = call(
         functools.partial(outer_kernel, *place),
         coefs + around + (upd, near, far, lat, zin) + weights,
         [shape(flat, rows, width, BF16)],
-        [
-            spare(rows), pltpu.VMEM((4, 4 * latent, n_out), F32),
-            pltpu.VMEM((4, latent, n_out), F32),
+        spare(2 * rows // TILE) + [
+            pltpu.VMEM((4, 4 * latent, n_out), F32), pltpu.VMEM((4, latent, n_out), F32),
         ],
         4 * rows, 32,
     )

time: 30.7 us -> 28.7 us (0.935)
  Pallas kernels: 19 us -> 17.1 us
    pallas_call x4, Pallas kernels: 19 us -> 17.1 us  [call(): pl.pallas_call(body, out_shape=tuple(outs), in_specs=[space] * len(operan...]
  transfers between devices with their start and end apart: 5 -> 5, of which waited for: 2 -> 2; matrix products, arithmetic and copies ran while one was open for 0% -> 0% of each run, Pallas kernels for 17% -> 18%
where the time goes in v5:
time: 28.7 us; the launch traced here: 28.3 us
  Pallas kernels  17.1 us (60%)
  starting transfers between devices  6.08 us (21%)
  waiting for transfers between devices  4.32 us (15%)
  other arithmetic  0.77 us (3%)
    pallas_call x4, Pallas kernels, call(): pl.pallas_call(body, out_shape=tuple(outs), in_specs=[space] * len(operan...  17.1 us
    ppermute x5, starting transfers between devices, swap(): return lax.ppermute(x, axis, pairs)  6.08 us
    ppermute x5, waiting for transfers between devices, swap(): return lax.ppermute(x, axis, pairs)  4.32 us
    slice x1, other arithmetic, per_device(): noise[1]  0.77 us
  transfers between devices with their start and end apart: 5, of which 2 were waited for; matrix products, arithmetic and copies ran while one was open for 0% of the time, Pallas kernels for 18%

profile of v5, /device:TPU:26, one launch (start us, length us, event | category | flops | bytes accessed | tf_op | source)
XLA Modules:
  0.0 28.3 jit_solution(12710167215053344214)
XLA Ops:
  0.0 0.8 %fusion = (bf16[1,4,4,4,128]{4,3,2,1,0:T(4,128)(2,1)S(1)}, bf16[1,4,4,4,128]{4,3,2,1,0:T(4,128)(2,1)S(1)}) fusion(bf16[2,4,4,4,128]{4,3,2,1,0:T(4,128)(2,1)} %param.9, bf16[1,4,4,4,128]{4,3,2,1,0:T(4,128)(2,1)} %param.8, pred[]{:T(512)S(6)} %eq.3), kind=kLoop, calls=%fused_computation.3 | loop fusion | flops 8192 | bytes 81921 | tf_op jit(solution)/shard_map/slice | solution.py:419
  0.8 1.6 %collective-permute-start.1 = (bf16[32,512]{1,0:T(8,128)(2,1)S(1)}, bf16[32,512]{1,0:T(8,128)(2,1)S(1)}, u32[]{:S(2)}, u32[]{:S(2)}) collective-permute-start(bf16[32,512]{1,0:T(8,128)(2,1)S(1)} %bitcast_dynamic-update-slice_fusion.own_ref), channel_id=1, source_target_pairs={{0,1},{1,0},{2,3},{3,2},{4,5},{5,4},{6,7},{7,6},{8,9},{9,8},{10,11... | collective-permute-start | bytes 98312 | tf_op jit(solution)/shard_map/ppermute | solution.py:415
  2.4 2.3 %collective-permute-start = (bf16[32,512]{1,0:T(8,128)(2,1)S(1)}, bf16[32,512]{1,0:T(8,128)(2,1)S(1)}, u32[]{:S(2)}, u32[]{:S(2)}) collective-permute-start(bf16[32,512]{1,0:T(8,128)(2,1)S(1)} %bitcast_dynamic-update-slice_fusion.own_ref), channel_id=1, source_target_pairs={{1,2},{2,1},{3,4},{4,3},{5,6},{6,5},{9,10},{10,9},{11,12},{12,11},... | collective-permute-start | bytes 98312 | tf_op jit(solution)/shard_map/ppermute | solution.py:415
  4.7 2.9 %shard_map.82 = (bf16[320,128]{1,0:T(8,128)(2,1)S(1)}, bf16[6,8,320,128]{3,2,1,0:T(8,128)(2,1)S(1)}, bf16[16,640]{1,0:T(8,128)(2,1)S(1)}, f32[2,4,4]{2,1,0:T(4,128)S(1)}, f32[2,4,4]{2,1,0:T(4,128)S(1)}) custom-call(bf16[9,4,320]{2,1,0:T(4,128)(2,1)} %bitcast.16, bf16[9,320,320]{2,1,0:T(8,128)(2,1)} %bitcast.15, bf16[3,320,320]{2,1,0:T(8,128)(2,1)} %time_hbm.1, ...), custom_call_target="tpu_custom_call" | custom-call | flops 838860800 | bytes 2457600 | tf_op jit(solution)/shard_map/pallas_call | solution.py:398
  7.6 0.0 collective-permute-done.1.even_ref
  7.6 1.5 %collective-permute-done.odd_ref = bf16[32,512]{1,0:T(8,128)(2,1)S(1)} collective-permute-done((bf16[32,512]{1,0:T(8,128)(2,1)S(1)}, bf16[32,512]{1,0:T(8,128)(2,1)S(1)}, u32[]{:S(2)}, u32[]{:S(2)}) %collective-permute-start) | collective-permute-done | bytes 32800 | tf_op jit(solution)/shard_map/ppermute | solution.py:415
  9.1 7.4 %shard_map.83 = (f32[24,1024]{1,0:T(8,128)S(1)}, f32[8,1024]{1,0:T(8,128)S(1)}, f32[8,1024]{1,0:T(8,128)S(1)}) custom-call(f32[2,4,4]{2,1,0:T(4,128)S(1)} %get-tuple-element.15.keep_ref, f32[2,4,4]{2,1,0:T(4,128)S(1)} %get-tuple-element.16.noise_ref, bf16[32,512]{1,0:T(8,128)(2,1)S(1)} %collective-permute-done.odd_ref, ...), custom_call_target="tpu_custom_call" | custom-call | flops 6710886400 | bytes 2457600 | tf_op jit(solution)/shard_map/pallas_call | solution.py:398
  16.5 0.6 %collective-permute-start.2 = (f32[24,1024]{1,0:T(8,128)S(1)}, f32[24,1024]{1,0:T(8,128)S(1)}, u32[]{:S(2)}, u32[]{:S(2)}) collective-permute-start(f32[24,1024]{1,0:T(8,128)S(1)} %get-tuple-element.20), channel_id=1, source_target_pairs={{0,16},{8,24},{16,0},{24,8},{1,17},{9,25},{17,1},{25,9},{2,18},{10... | collective-permute-start | bytes 294920 | tf_op jit(solution)/shard_map/ppermute | solution.py:415
  17.1 0.0 collective-permute-start.3
  17.1 1.6 %collective-permute-start.4 = (f32[8,1024]{1,0:T(8,128)S(1)}, f32[8,1024]{1,0:T(8,128)S(1)}, u32[]{:S(2)}, u32[]{:S(2)}) collective-permute-start(f32[8,1024]{1,0:T(8,128)S(1)} %get-tuple-element.22), channel_id=1, source_target_pairs={{0,24},{8,16},{16,8},{24,0},{1,25},{9,17},{17,9},{25,1},{2,26},{10... | collective-permute-start | bytes 98312 | tf_op jit(solution)/shard_map/ppermute | solution.py:415
  18.7 2.8 %collective-permute-done.2.upd_ref = f32[24,1024]{1,0:T(8,128)S(1)} collective-permute-done((f32[24,1024]{1,0:T(8,128)S(1)}, f32[24,1024]{1,0:T(8,128)S(1)}, u32[]{:S(2)}, u32[]{:S(2)}) %collective-permute-start.2) | collective-permute-done | bytes 98336 | tf_op jit(solution)/shard_map/ppermute | solution.py:415
  21.5 2.1 %shard_map.84 = (f32[2,4,512]{2,1,0:T(4,128)S(1)}, f32[2,16,512]{2,1,0:T(8,128)S(1)}) custom-call(bf16[32,512]{1,0:T(8,128)(2,1)S(1)} %collective-permute-done.odd_ref, bf16[32,512]{1,0:T(8,128)(2,1)S(1)} %bitcast_dynamic-update-slice_fusion.own_ref, bf16[32,512]{1,0:T(8,128)(2,1)S(1)} %collective-permute-done.1.even_ref, ...), custom_call_target="tpu_custom_call" | custom-call | flops 1677721600 | bytes 2457600 | tf_op jit(solution)/shard_map/pallas_call | solution.py:398
  23.6 0.0 collective-permute-done.3.near_ref
  23.7 0.0 collective-permute-done.4.far_ref
  23.7 4.7 %shard_map.85 = bf16[16,4,128]{2,1,0:T(4,128)(2,1)} custom-call(f32[2,4,4]{2,1,0:T(4,128)S(1)} %get-tuple-element.15.keep_ref, f32[2,4,4]{2,1,0:T(4,128)S(1)} %get-tuple-element.16.noise_ref, bf16[32,512]{1,0:T(8,128)(2,1)S(1)} %collective-permute-done.odd_ref, bf16[32,512]{1,0:T(8,128)(2,1)S(1)} %bitcast_dynamic-update-slice_fusion.own_ref, ...), custom_call_target="tpu_custom_call" | custom-call | flops 3355443200 | bytes 2457600 | tf_op jit(solution)/shard_map/pallas_call | solution.py:398
  (2 shorter events, 0.0 us)
Async XLA Ops:
  0.8 6.8 %collective-permute-start.1 = (bf16[32,512]{1,0:T(8,128)(2,1)S(1)}, bf16[32,512]{1,0:T(8,128)(2,1)S(1)}, u32[]{:S(2)}, u32[]{:S(2)}) collective-permute-start(bf16[32,512]{1,0:T(8,128)(2,1)S(1)} %bitcast_dynamic-update-slice_fusion.own_ref), channel_id=1, source_target_pairs={{0,1},{1,0},{2,3},{3,2},{4,5},{5,4},{6,7},{7,6},{8,9},{9,8},{10,11... | collective-permute-start | bytes 98312 | tf_op jit(solution)/shard_map/ppermute | solution.py:415
  2.4 6.7 %collective-permute-start = (bf16[32,512]{1,0:T(8,128)(2,1)S(1)}, bf16[32,512]{1,0:T(8,128)(2,1)S(1)}, u32[]{:S(2)}, u32[]{:S(2)}) collective-permute-start(bf16[32,512]{1,0:T(8,128)(2,1)S(1)} %bitcast_dynamic-update-slice_fusion.own_ref), channel_id=1, source_target_pairs={{1,2},{2,1},{3,4},{4,3},{5,6},{6,5},{9,10},{10,9},{11,12},{12,11},... | collective-permute-start | bytes 98312 | tf_op jit(solution)/shard_map/ppermute | solution.py:415
  16.5 5.0 %collective-permute-start.2 = (f32[24,1024]{1,0:T(8,128)S(1)}, f32[24,1024]{1,0:T(8,128)S(1)}, u32[]{:S(2)}, u32[]{:S(2)}) collective-permute-start(f32[24,1024]{1,0:T(8,128)S(1)} %get-tuple-element.20), channel_id=1, source_target_pairs={{0,16},{8,24},{16,0},{24,8},{1,17},{9,25},{17,1},{25,9},{2,18},{10... | collective-permute-start | bytes 294920 | tf_op jit(solution)/shard_map/ppermute | solution.py:415
  17.1 6.5 %collective-permute-start.3 = (f32[8,1024]{1,0:T(8,128)S(1)}, f32[8,1024]{1,0:T(8,128)S(1)}, u32[]{:S(2)}, u32[]{:S(2)}) collective-permute-start(f32[8,1024]{1,0:T(8,128)S(1)} %get-tuple-element.21), channel_id=1, source_target_pairs={{0,8},{8,0},{16,24},{24,16},{1,9},{9,1},{17,25},{25,17},{2,10},{10... | collective-permute-start | bytes 98312 | tf_op jit(solution)/shard_map/ppermute | solution.py:415
  17.1 6.5 %collective-permute-start.4 = (f32[8,1024]{1,0:T(8,128)S(1)}, f32[8,1024]{1,0:T(8,128)S(1)}, u32[]{:S(2)}, u32[]{:S(2)}) collective-permute-start(f32[8,1024]{1,0:T(8,128)S(1)} %get-tuple-element.22), channel_id=1, source_target_pairs={{0,24},{8,16},{16,8},{24,0},{1,25},{9,17},{17,9},{25,1},{2,26},{10... | collective-permute-start | bytes 98312 | tf_op jit(solution)/shard_map/ppermute | solution.py:415

commit v6 on v5

--- a/solution.py
+++ b/solution.py
@@ -210,6 +210,10 @@
         project(batches[i], ready)
 
 
+def narrow(v):
+    return v.astype(BF16).astype(F32)
+
+
 def neighbours(odd_ref, even_ref, tile, lo, hi):
     odd, even = odd_ref[lo:hi, :].astype(F32), even_ref[lo:hi, :].astype(F32)
     is_even = lax.rem(tile, 2) == 0
@@ -251,7 +255,7 @@
         [(f,) for f in range(frames)], latents, dims, rows, tile, tiles,
         w1_ref, w2_ref, wz_ref, s_ref, store,
     )
-    skip = 2 * width
+    skip, updates = 2 * width, []
     for f in range(frames):
         z = z_parts(z_ref, f, latent)[0]
         if f > 0:
@@ -261,15 +265,16 @@
         lo, hi = f * latent, (f + 1) * latent
         q = latents(f)[:, skip:skip + rows * width]
         upd = coef(keep_ref, 0, position, f) * q - coef(noise_ref, 0, position, f) * z
-        full_ref[lo:hi, :] = upd
-        if f == 0:
-            first = jnp.concatenate([z_parts(z_ref, 0, latent)[2], upd], axis=0)
-        if f == frames - 1:
-            last = jnp.concatenate([z_parts(z_ref, f, latent)[1], upd], axis=0)
-    full_ref[flat:flat + latent, :] = last[0:latent]
-    full_ref[flat + latent:, :] = first[0:latent]
-    near_ref[...] = jnp.where(even, first, last)
-    far_ref[...] = jnp.where(even, last, first)
+        updates.append(upd)
+    z_first, z_last = z_parts(z_ref, 0, latent)[2], z_parts(z_ref, frames - 1, latent)[1]
+    first, last = updates[0], updates[-1]
+    low_first, low_last = first - narrow(first), last - narrow(last)
+    everything = updates + [z_last, z_first, low_first, low_last]
+    full_ref[...] = jnp.concatenate(everything, axis=0).astype(BF16)
+    backward = jnp.concatenate([z_first, first, low_first], axis=0)
+    forward = jnp.concatenate([z_last, last, low_last], axis=0)
+    near_ref[...] = jnp.where(even, backward, forward).astype(BF16)
+    far_ref[...] = jnp.where(even, forward, backward).astype(BF16)
 
 
 def window(f, dims, frames, tile, odd_ref, own_ref, even_ref):
@@ -296,10 +301,11 @@
 ):
     latent, local_rows, width, channels = dims
     level, tile = lax.axis_index("level"), lax.axis_index("tile")
+    update = upd_ref[...].astype(F32)
 
     def latents(f):
         fresh = window(f, dims, frames, tile, odd_ref, own_ref, even_ref)
-        v = jnp.where(level == 0, fresh, upd_ref[f * latent:(f + 1) * latent, :])
+        v = jnp.where(level == 0, fresh, update[f * latent:(f + 1) * latent])
         v = inside(v, dims, tile, tiles)
         lat_ref[f - 1] = v[:, 2 * width:(2 + local_rows) * width]
         return v
@@ -325,9 +331,12 @@
     last = frames - 1
     flat = frames * latent
     even = lax.rem(level, 2) == 0
-    fwd, bwd = upd_ref[flat:flat + latent, :], upd_ref[flat + latent:, :]
-    near, far = near_ref[...], far_ref[...]
+    update = upd_ref[...].astype(F32)
+    near, far = near_ref[...].astype(F32), far_ref[...].astype(F32)
     fwd_in, bwd_in = jnp.where(even, near, far), jnp.where(even, far, near)
+    fwd, bwd, low_first, low_last = (
+        update[flat + k * latent:flat + (k + 1) * latent] for k in range(4)
+    )
     slots = {-1: 0, 0: 1, last: 2, frames: 3}
 
     def latents(f):
@@ -335,19 +344,20 @@
         fresh = window(source, dims, frames, tile, odd_ref, own_ref, even_ref)
         if f == -1:
             earlier = lax.rem(level + levels - 2, levels)
-            v = fwd_in[latent:] - coef(noise_ref, 0, earlier, last) * bwd
+            v = fwd_in[latent:2 * latent] + fwd_in[2 * latent:] - coef(noise_ref, 0, earlier, last) * bwd
             v = jnp.where(level == 1, fresh, v)
             v = jnp.where(level == 0, 0.0, v)
         elif f == 0:
             rate = jnp.where(level == 1, 0.0, coef(noise_ref, 0, before, 0))
-            v = upd_ref[0:latent, :] - rate * fwd_in[0:latent]
+            v = update[0:latent] + low_first - rate * fwd_in[0:latent]
             v = jnp.where(level == 0, fresh, v)
         elif f == last:
-            v = upd_ref[last * latent:flat, :] - coef(noise_ref, 0, before, last) * bwd_in[0:latent]
+            v = update[last * latent:flat] + low_last
+            v = v - coef(noise_ref, 0, before, last) * bwd_in[0:latent]
             v = jnp.where(level == 0, fresh, v)
         else:
             rate = jnp.where(level == 0, 0.0, coef(noise_ref, 0, level, 0))
-            v = bwd_in[latent:] - rate * fwd
+            v = bwd_in[latent:2 * latent] + bwd_in[2 * latent:] - rate * fwd
             v = jnp.where(level == levels - 1, 0.0, v)
         v = inside(v, dims, tile, tiles)
         edge_ref[slots[f]] = v[:, 2 * width:(2 + local_rows) * width]
@@ -449,7 +459,7 @@
     full, near, far = call(
         functools.partial(step0_kernel, *place),
         coefs + around + weights,
-        [shape(flat + 2 * latent, n_wide, F32)] + [shape(2 * latent, n_wide, F32)] * 2,
+        [shape(flat + 4 * latent, n_wide, BF16)] + [shape(3 * latent, n_wide, BF16)] * 2,
         spare(rows // TILE + 1) + [pltpu.VMEM((frames, 4 * latent, n_wide), F32)],
         frames * (rows + 4), 32,
     )

time: 28.7 us -> 28.3 us (0.986)
  waiting for transfers between devices: 4.32 us -> 3.97 us
    ppermute x5, waiting for transfers between devices: 4.32 us -> 3.97 us  [swap(): return lax.ppermute(x, axis, pairs)]
where the time goes in v6:
time: 28.3 us; the launch traced here: 28 us
  Pallas kernels  17.1 us (60%)
  starting transfers between devices  6.08 us (21%)
  waiting for transfers between devices  3.97 us (14%)
  other arithmetic  0.77 us (3%)
    pallas_call x4, Pallas kernels, call(): pl.pallas_call(body, out_shape=tuple(outs), in_specs=[space] * len(operan...  17.1 us
    ppermute x5, starting transfers between devices, swap(): return lax.ppermute(x, axis, pairs)  6.08 us
    ppermute x5, waiting for transfers between devices, swap(): return lax.ppermute(x, axis, pairs)  3.97 us
    slice x1, other arithmetic, per_device(): noise[1]  0.77 us
  transfers between devices with their start and end apart: 5, of which 2 were waited for; matrix products, arithmetic and copies ran while one was open for 0% of the time, Pallas kernels for 18%

profile of v6, /device:TPU:26, one launch (start us, length us, event | category | flops | bytes accessed | tf_op | source)
XLA Modules:
  0.0 28.0 jit_solution(7490340849590692632)
XLA Ops:
  0.0 0.8 %fusion = (bf16[1,4,4,4,128]{4,3,2,1,0:T(4,128)(2,1)S(1)}, bf16[1,4,4,4,128]{4,3,2,1,0:T(4,128)(2,1)S(1)}) fusion(bf16[2,4,4,4,128]{4,3,2,1,0:T(4,128)(2,1)} %param.9, bf16[1,4,4,4,128]{4,3,2,1,0:T(4,128)(2,1)} %param.8, pred[]{:T(512)S(6)} %eq.3), kind=kLoop, calls=%fused_computation.3 | loop fusion | flops 8192 | bytes 81921 | tf_op jit(solution)/shard_map/slice | solution.py:429
  0.8 1.6 %collective-permute-start.1 = (bf16[32,512]{1,0:T(8,128)(2,1)S(1)}, bf16[32,512]{1,0:T(8,128)(2,1)S(1)}, u32[]{:S(2)}, u32[]{:S(2)}) collective-permute-start(bf16[32,512]{1,0:T(8,128)(2,1)S(1)} %bitcast_dynamic-update-slice_fusion.own_ref), channel_id=1, source_target_pairs={{0,1},{1,0},{2,3},{3,2},{4,5},{5,4},{6,7},{7,6},{8,9},{9,8},{10,11... | collective-permute-start | bytes 98312 | tf_op jit(solution)/shard_map/ppermute | solution.py:425
  2.4 2.3 %collective-permute-start = (bf16[32,512]{1,0:T(8,128)(2,1)S(1)}, bf16[32,512]{1,0:T(8,128)(2,1)S(1)}, u32[]{:S(2)}, u32[]{:S(2)}) collective-permute-start(bf16[32,512]{1,0:T(8,128)(2,1)S(1)} %bitcast_dynamic-update-slice_fusion.own_ref), channel_id=1, source_target_pairs={{1,2},{2,1},{3,4},{4,3},{5,6},{6,5},{9,10},{10,9},{11,12},{12,11},... | collective-permute-start | bytes 98312 | tf_op jit(solution)/shard_map/ppermute | solution.py:425
  4.7 2.9 %shard_map.82 = (bf16[320,128]{1,0:T(8,128)(2,1)S(1)}, bf16[6,8,320,128]{3,2,1,0:T(8,128)(2,1)S(1)}, bf16[16,640]{1,0:T(8,128)(2,1)S(1)}, f32[2,4,4]{2,1,0:T(4,128)S(1)}, f32[2,4,4]{2,1,0:T(4,128)S(1)}) custom-call(bf16[9,4,320]{2,1,0:T(4,128)(2,1)} %bitcast.16, bf16[9,320,320]{2,1,0:T(8,128)(2,1)} %bitcast.15, bf16[3,320,320]{2,1,0:T(8,128)(2,1)} %time_hbm.1, ...), custom_call_target="tpu_custom_call" | custom-call | flops 838860800 | bytes 2457600 | tf_op jit(solution)/shard_map/pallas_call | solution.py:408
  7.6 0.0 collective-permute-done.1.even_ref
  7.6 1.5 %collective-permute-done.odd_ref = bf16[32,512]{1,0:T(8,128)(2,1)S(1)} collective-permute-done((bf16[32,512]{1,0:T(8,128)(2,1)S(1)}, bf16[32,512]{1,0:T(8,128)(2,1)S(1)}, u32[]{:S(2)}, u32[]{:S(2)}) %collective-permute-start) | collective-permute-done | bytes 32800 | tf_op jit(solution)/shard_map/ppermute | solution.py:425
  9.1 7.4 %shard_map.83 = (bf16[32,1024]{1,0:T(8,128)(2,1)S(1)}, bf16[12,1024]{1,0:T(8,128)(2,1)S(1)}, bf16[12,1024]{1,0:T(8,128)(2,1)S(1)}) custom-call(f32[2,4,4]{2,1,0:T(4,128)S(1)} %get-tuple-element.15.keep_ref, f32[2,4,4]{2,1,0:T(4,128)S(1)} %get-tuple-element.16.noise_ref, bf16[32,512]{1,0:T(8,128)(2,1)S(1)} %collective-permute-done.odd_ref, ...), custom_call_target="tpu_custom_call" | custom-call | flops 6710886400 | bytes 2457600 | tf_op jit(solution)/shard_map/pallas_call | solution.py:408
  16.5 0.6 %collective-permute-start.2 = (bf16[32,1024]{1,0:T(8,128)(2,1)S(1)}, bf16[32,1024]{1,0:T(8,128)(2,1)S(1)}, u32[]{:S(2)}, u32[]{:S(2)}) collective-permute-start(bf16[32,1024]{1,0:T(8,128)(2,1)S(1)} %get-tuple-element.20), channel_id=1, source_target_pairs={{0,16},{8,24},{16,0},{24,8},{1,17},{9,25},{17,1},{25,9},{2,18},{10... | collective-permute-start | bytes 196616 | tf_op jit(solution)/shard_map/ppermute | solution.py:425
  17.1 0.0 collective-permute-start.3
  17.1 1.6 %collective-permute-start.4 = (bf16[12,1024]{1,0:T(8,128)(2,1)S(1)}, bf16[12,1024]{1,0:T(8,128)(2,1)S(1)}, u32[]{:S(2)}, u32[]{:S(2)}) collective-permute-start(bf16[12,1024]{1,0:T(8,128)(2,1)S(1)} %get-tuple-element.22), channel_id=1, source_target_pairs={{0,24},{8,16},{16,8},{24,0},{1,25},{9,17},{17,9},{25,1},{2,26},{10... | collective-permute-start | bytes 73736 | tf_op jit(solution)/shard_map/ppermute | solution.py:425
  18.7 2.4 %collective-permute-done.2.upd_ref = bf16[32,1024]{1,0:T(8,128)(2,1)S(1)} collective-permute-done((bf16[32,1024]{1,0:T(8,128)(2,1)S(1)}, bf16[32,1024]{1,0:T(8,128)(2,1)S(1)}, u32[]{:S(2)}, u32[]{:S(2)}) %collective-permute-start.2) | collective-permute-done | bytes 65568 | tf_op jit(solution)/shard_map/ppermute | solution.py:425
  21.1 2.1 %shard_map.84 = (f32[2,4,512]{2,1,0:T(4,128)S(1)}, f32[2,16,512]{2,1,0:T(8,128)S(1)}) custom-call(bf16[32,512]{1,0:T(8,128)(2,1)S(1)} %collective-permute-done.odd_ref, bf16[32,512]{1,0:T(8,128)(2,1)S(1)} %bitcast_dynamic-update-slice_fusion.own_ref, bf16[32,512]{1,0:T(8,128)(2,1)S(1)} %collective-permute-done.1.even_ref, ...), custom_call_target="tpu_custom_call" | custom-call | flops 1677721600 | bytes 2457600 | tf_op jit(solution)/shard_map/pallas_call | solution.py:408
  23.3 0.0 collective-permute-done.3.near_ref
  23.3 0.0 collective-permute-done.4.far_ref
  23.3 4.7 %shard_map.85 = bf16[16,4,128]{2,1,0:T(4,128)(2,1)} custom-call(f32[2,4,4]{2,1,0:T(4,128)S(1)} %get-tuple-element.15.keep_ref, f32[2,4,4]{2,1,0:T(4,128)S(1)} %get-tuple-element.16.noise_ref, bf16[32,512]{1,0:T(8,128)(2,1)S(1)} %collective-permute-done.odd_ref, bf16[32,512]{1,0:T(8,128)(2,1)S(1)} %bitcast_dynamic-update-slice_fusion.own_ref, ...), custom_call_target="tpu_custom_call" | custom-call | flops 3355443200 | bytes 2457600 | tf_op jit(solution)/shard_map/pallas_call | solution.py:408
  (2 shorter events, 0.0 us)
Async XLA Ops:
  0.8 6.8 %collective-permute-start.1 = (bf16[32,512]{1,0:T(8,128)(2,1)S(1)}, bf16[32,512]{1,0:T(8,128)(2,1)S(1)}, u32[]{:S(2)}, u32[]{:S(2)}) collective-permute-start(bf16[32,512]{1,0:T(8,128)(2,1)S(1)} %bitcast_dynamic-update-slice_fusion.own_ref), channel_id=1, source_target_pairs={{0,1},{1,0},{2,3},{3,2},{4,5},{5,4},{6,7},{7,6},{8,9},{9,8},{10,11... | collective-permute-start | bytes 98312 | tf_op jit(solution)/shard_map/ppermute | solution.py:425
  2.4 6.7 %collective-permute-start = (bf16[32,512]{1,0:T(8,128)(2,1)S(1)}, bf16[32,512]{1,0:T(8,128)(2,1)S(1)}, u32[]{:S(2)}, u32[]{:S(2)}) collective-permute-start(bf16[32,512]{1,0:T(8,128)(2,1)S(1)} %bitcast_dynamic-update-slice_fusion.own_ref), channel_id=1, source_target_pairs={{1,2},{2,1},{3,4},{4,3},{5,6},{6,5},{9,10},{10,9},{11,12},{12,11},... | collective-permute-start | bytes 98312 | tf_op jit(solution)/shard_map/ppermute | solution.py:425
  16.5 4.7 %collective-permute-start.2 = (bf16[32,1024]{1,0:T(8,128)(2,1)S(1)}, bf16[32,1024]{1,0:T(8,128)(2,1)S(1)}, u32[]{:S(2)}, u32[]{:S(2)}) collective-permute-start(bf16[32,1024]{1,0:T(8,128)(2,1)S(1)} %get-tuple-element.20), channel_id=1, source_target_pairs={{0,16},{8,24},{16,0},{24,8},{1,17},{9,25},{17,1},{25,9},{2,18},{10... | collective-permute-start | bytes 196616 | tf_op jit(solution)/shard_map/ppermute | solution.py:425
  17.1 6.2 %collective-permute-start.3 = (bf16[12,1024]{1,0:T(8,128)(2,1)S(1)}, bf16[12,1024]{1,0:T(8,128)(2,1)S(1)}, u32[]{:S(2)}, u32[]{:S(2)}) collective-permute-start(bf16[12,1024]{1,0:T(8,128)(2,1)S(1)} %get-tuple-element.21), channel_id=1, source_target_pairs={{0,8},{8,0},{16,24},{24,16},{1,9},{9,1},{17,25},{25,17},{2,10},{10... | collective-permute-start | bytes 73736 | tf_op jit(solution)/shard_map/ppermute | solution.py:425
  17.1 6.2 %collective-permute-start.4 = (bf16[12,1024]{1,0:T(8,128)(2,1)S(1)}, bf16[12,1024]{1,0:T(8,128)(2,1)S(1)}, u32[]{:S(2)}, u32[]{:S(2)}) collective-permute-start(bf16[12,1024]{1,0:T(8,128)(2,1)S(1)} %get-tuple-element.22), channel_id=1, source_target_pairs={{0,24},{8,16},{16,8},{24,0},{1,25},{9,17},{17,9},{25,1},{2,26},{10... | collective-permute-start | bytes 73736 | tf_op jit(solution)/shard_map/ppermute | solution.py:425

commit v7 on v6

--- a/solution.py
+++ b/solution.py
@@ -47,17 +47,39 @@
         pltpu.make_async_copy(second_hbm.at[k], second_ref.at[k], second_sem.at[k])
         for k in range(taps)
     ]
+    for k in (0, 1, 3, 4):
+        loads[k].start()
     for b in range(3):
+        if b == 2:
+            loads[2].start()
         for a in range(3):
             slabs[3 * a + b].start()
-    for load in loads:
-        load.start()
     full_blocks, tail = main // 128, channels - main
     blocks = w2_ref.shape[1]
     spare = blocks * 128 - 3 * channels
     if spare:
         w2_ref[:, blocks - 1, :, 128 - spare:] = jnp.zeros((FORMS, channels, spare), BF16)
+    for k in (0, 1, 3, 4):
+        loads[k].wait()
+    pad = jnp.zeros((slot - 3 * latent, channels), F32)
+    pieces = []
+    for a in range(3):
+        pieces += [first_ref[3 * a + b].astype(F32) for b in range(3)]
+        if slot > 3 * latent:
+            pieces.append(pad)
+    w1 = 0.5 * jnp.concatenate(pieces, axis=0)
+    w1 = jnp.pad(w1, ((0, w1_ref.shape[1] - 3 * slot), (0, lanes(channels) - channels)))
+    w1_ref[...] = w1.T[0:channels].astype(BF16)
     for b in range(3):
+        if b == 2:
+            loads[2].wait()
+            proj = proj_ref[...]
+            zero = jnp.zeros((latent, channels), F32)
+            pt = [dot(proj, time_ref[k]) for k in range(3)]
+            left = jnp.concatenate([2.0 * proj.astype(F32), zero, zero, zero], axis=0)
+            right = jnp.concatenate([pt[1], pt[0], pt[2], zero], axis=0)
+            wz_ref[:, 0:channels] = left.astype(BF16)
+            wz_ref[:, channels:] = right.astype(BF16)
         for a in range(3):
             slabs[3 * a + b].wait()
         for lo in range(0, channels, 32):
@@ -82,24 +104,6 @@
                         form[:, main + start:main + start + size]
                     )
                     start += size
-    for load in loads:
-        load.wait()
-    pad = jnp.zeros((slot - 3 * latent, channels), F32)
-    pieces = []
-    for a in range(3):
-        pieces += [first_ref[3 * a + b].astype(F32) for b in range(3)]
-        if slot > 3 * latent:
-            pieces.append(pad)
-    w1 = 0.5 * jnp.concatenate(pieces, axis=0)
-    w1 = jnp.pad(w1, ((0, w1_ref.shape[1] - 3 * slot), (0, lanes(channels) - channels)))
-    w1_ref[...] = w1.T[0:channels].astype(BF16)
-    proj = proj_ref[...]
-    zero = jnp.zeros((latent, channels), F32)
-    pt = [dot(proj, time_ref[k]) for k in range(3)]
-    left = jnp.concatenate([2.0 * proj.astype(F32), zero, zero, zero], axis=0)
-    right = jnp.concatenate([pt[1], pt[0], pt[2], zero], axis=0)
-    wz_ref[:, 0:channels] = left.astype(BF16)
-    wz_ref[:, channels:] = right.astype(BF16)
 
 
 def row_forms(d):

time: 28.3 us -> 28.3 us (level)
  Pallas kernels: 17.1 us -> 17.4 us
  transfers between devices with their start and end apart: 5 -> 5, of which waited for: 2 -> 2; matrix products, arithmetic and copies ran while one was open for 0% -> 0% of each run, Pallas kernels for 18% -> 19%
where the time goes in v7:
time: 28.3 us; the launch traced here: 28 us
  Pallas kernels  17.4 us (61%)
  starting transfers between devices  6.08 us (21%)
  waiting for transfers between devices  3.71 us (13%)
  other arithmetic  0.77 us (3%)
    pallas_call x4, Pallas kernels, call(): pl.pallas_call(body, out_shape=tuple(outs), in_specs=[space] * len(operan...  17.4 us
    ppermute x5, starting transfers between devices, swap(): return lax.ppermute(x, axis, pairs)  6.08 us
    ppermute x5, waiting for transfers between devices, swap(): return lax.ppermute(x, axis, pairs)  3.71 us
    slice x1, other arithmetic, per_device(): noise[1]  0.77 us
  transfers between devices with their start and end apart: 5, of which 2 were waited for; matrix products, arithmetic and copies ran while one was open for 0% of the time, Pallas kernels for 19%

profile of v7, /device:TPU:26, one launch (start us, length us, event | category | flops | bytes accessed | tf_op | source)
XLA Modules:
  0.0 28.0 jit_solution(8784181161355143654)
XLA Ops:
  0.0 0.8 %fusion = (bf16[1,4,4,4,128]{4,3,2,1,0:T(4,128)(2,1)S(1)}, bf16[1,4,4,4,128]{4,3,2,1,0:T(4,128)(2,1)S(1)}) fusion(bf16[2,4,4,4,128]{4,3,2,1,0:T(4,128)(2,1)} %param.9, bf16[1,4,4,4,128]{4,3,2,1,0:T(4,128)(2,1)} %param.8, pred[]{:T(512)S(6)} %eq.3), kind=kLoop, calls=%fused_computation.3 | loop fusion | flops 8192 | bytes 81921 | tf_op jit(solution)/shard_map/slice | solution.py:433
  0.8 1.6 %collective-permute-start.1 = (bf16[32,512]{1,0:T(8,128)(2,1)S(1)}, bf16[32,512]{1,0:T(8,128)(2,1)S(1)}, u32[]{:S(2)}, u32[]{:S(2)}) collective-permute-start(bf16[32,512]{1,0:T(8,128)(2,1)S(1)} %bitcast_dynamic-update-slice_fusion.own_ref), channel_id=1, source_target_pairs={{0,1},{1,0},{2,3},{3,2},{4,5},{5,4},{6,7},{7,6},{8,9},{9,8},{10,11... | collective-permute-start | bytes 98312 | tf_op jit(solution)/shard_map/ppermute | solution.py:429
  2.4 2.3 %collective-permute-start = (bf16[32,512]{1,0:T(8,128)(2,1)S(1)}, bf16[32,512]{1,0:T(8,128)(2,1)S(1)}, u32[]{:S(2)}, u32[]{:S(2)}) collective-permute-start(bf16[32,512]{1,0:T(8,128)(2,1)S(1)} %bitcast_dynamic-update-slice_fusion.own_ref), channel_id=1, source_target_pairs={{1,2},{2,1},{3,4},{4,3},{5,6},{6,5},{9,10},{10,9},{11,12},{12,11},... | collective-permute-start | bytes 98312 | tf_op jit(solution)/shard_map/ppermute | solution.py:429
  4.7 3.1 %shard_map.82 = (bf16[320,128]{1,0:T(8,128)(2,1)S(1)}, bf16[6,8,320,128]{3,2,1,0:T(8,128)(2,1)S(1)}, bf16[16,640]{1,0:T(8,128)(2,1)S(1)}, f32[2,4,4]{2,1,0:T(4,128)S(1)}, f32[2,4,4]{2,1,0:T(4,128)S(1)}) custom-call(bf16[9,4,320]{2,1,0:T(4,128)(2,1)} %bitcast.16, bf16[9,320,320]{2,1,0:T(8,128)(2,1)} %bitcast.15, bf16[3,320,320]{2,1,0:T(8,128)(2,1)} %time_hbm.1, ...), custom_call_target="tpu_custom_call" | custom-call | flops 838860800 | bytes 2457600 | tf_op jit(solution)/shard_map/pallas_call | solution.py:412
  7.8 0.0 collective-permute-done.1.even_ref
  7.8 1.3 %collective-permute-done.odd_ref = bf16[32,512]{1,0:T(8,128)(2,1)S(1)} collective-permute-done((bf16[32,512]{1,0:T(8,128)(2,1)S(1)}, bf16[32,512]{1,0:T(8,128)(2,1)S(1)}, u32[]{:S(2)}, u32[]{:S(2)}) %collective-permute-start) | collective-permute-done | bytes 32800 | tf_op jit(solution)/shard_map/ppermute | solution.py:429
  9.1 7.4 %shard_map.83 = (bf16[32,1024]{1,0:T(8,128)(2,1)S(1)}, bf16[12,1024]{1,0:T(8,128)(2,1)S(1)}, bf16[12,1024]{1,0:T(8,128)(2,1)S(1)}) custom-call(f32[2,4,4]{2,1,0:T(4,128)S(1)} %get-tuple-element.15.keep_ref, f32[2,4,4]{2,1,0:T(4,128)S(1)} %get-tuple-element.16.noise_ref, bf16[32,512]{1,0:T(8,128)(2,1)S(1)} %collective-permute-done.odd_ref, ...), custom_call_target="tpu_custom_call" | custom-call | flops 6710886400 | bytes 2457600 | tf_op jit(solution)/shard_map/pallas_call | solution.py:412
  16.5 0.6 %collective-permute-start.2 = (bf16[32,1024]{1,0:T(8,128)(2,1)S(1)}, bf16[32,1024]{1,0:T(8,128)(2,1)S(1)}, u32[]{:S(2)}, u32[]{:S(2)}) collective-permute-start(bf16[32,1024]{1,0:T(8,128)(2,1)S(1)} %get-tuple-element.20), channel_id=1, source_target_pairs={{0,16},{8,24},{16,0},{24,8},{1,17},{9,25},{17,1},{25,9},{2,18},{10... | collective-permute-start | bytes 196616 | tf_op jit(solution)/shard_map/ppermute | solution.py:429
  17.1 0.0 collective-permute-start.3
  17.1 1.6 %collective-permute-start.4 = (bf16[12,1024]{1,0:T(8,128)(2,1)S(1)}, bf16[12,1024]{1,0:T(8,128)(2,1)S(1)}, u32[]{:S(2)}, u32[]{:S(2)}) collective-permute-start(bf16[12,1024]{1,0:T(8,128)(2,1)S(1)} %get-tuple-element.22), channel_id=1, source_target_pairs={{0,24},{8,16},{16,8},{24,0},{1,25},{9,17},{17,9},{25,1},{2,26},{10... | collective-permute-start | bytes 73736 | tf_op jit(solution)/shard_map/ppermute | solution.py:429
  18.7 2.4 %collective-permute-done.2.upd_ref = bf16[32,1024]{1,0:T(8,128)(2,1)S(1)} collective-permute-done((bf16[32,1024]{1,0:T(8,128)(2,1)S(1)}, bf16[32,1024]{1,0:T(8,128)(2,1)S(1)}, u32[]{:S(2)}, u32[]{:S(2)}) %collective-permute-start.2) | collective-permute-done | bytes 65568 | tf_op jit(solution)/shard_map/ppermute | solution.py:429
  21.1 2.1 %shard_map.84 = (f32[2,4,512]{2,1,0:T(4,128)S(1)}, f32[2,16,512]{2,1,0:T(8,128)S(1)}) custom-call(bf16[32,512]{1,0:T(8,128)(2,1)S(1)} %collective-permute-done.odd_ref, bf16[32,512]{1,0:T(8,128)(2,1)S(1)} %bitcast_dynamic-update-slice_fusion.own_ref, bf16[32,512]{1,0:T(8,128)(2,1)S(1)} %collective-permute-done.1.even_ref, ...), custom_call_target="tpu_custom_call" | custom-call | flops 1677721600 | bytes 2457600 | tf_op jit(solution)/shard_map/pallas_call | solution.py:412
  23.3 0.0 collective-permute-done.3.near_ref
  23.3 0.0 collective-permute-done.4.far_ref
  23.3 4.7 %shard_map.85 = bf16[16,4,128]{2,1,0:T(4,128)(2,1)} custom-call(f32[2,4,4]{2,1,0:T(4,128)S(1)} %get-tuple-element.15.keep_ref, f32[2,4,4]{2,1,0:T(4,128)S(1)} %get-tuple-element.16.noise_ref, bf16[32,512]{1,0:T(8,128)(2,1)S(1)} %collective-permute-done.odd_ref, bf16[32,512]{1,0:T(8,128)(2,1)S(1)} %bitcast_dynamic-update-slice_fusion.own_ref, ...), custom_call_target="tpu_custom_call" | custom-call | flops 3355443200 | bytes 2457600 | tf_op jit(solution)/shard_map/pallas_call | solution.py:412
  (2 shorter events, 0.0 us)
Async XLA Ops:
  0.8 7.0 %collective-permute-start.1 = (bf16[32,512]{1,0:T(8,128)(2,1)S(1)}, bf16[32,512]{1,0:T(8,128)(2,1)S(1)}, u32[]{:S(2)}, u32[]{:S(2)}) collective-permute-start(bf16[32,512]{1,0:T(8,128)(2,1)S(1)} %bitcast_dynamic-update-slice_fusion.own_ref), channel_id=1, source_target_pairs={{0,1},{1,0},{2,3},{3,2},{4,5},{5,4},{6,7},{7,6},{8,9},{9,8},{10,11... | collective-permute-start | bytes 98312 | tf_op jit(solution)/shard_map/ppermute | solution.py:429
  2.4 6.7 %collective-permute-start = (bf16[32,512]{1,0:T(8,128)(2,1)S(1)}, bf16[32,512]{1,0:T(8,128)(2,1)S(1)}, u32[]{:S(2)}, u32[]{:S(2)}) collective-permute-start(bf16[32,512]{1,0:T(8,128)(2,1)S(1)} %bitcast_dynamic-update-slice_fusion.own_ref), channel_id=1, source_target_pairs={{1,2},{2,1},{3,4},{4,3},{5,6},{6,5},{9,10},{10,9},{11,12},{12,11},... | collective-permute-start | bytes 98312 | tf_op jit(solution)/shard_map/ppermute | solution.py:429
  16.5 4.7 %collective-permute-start.2 = (bf16[32,1024]{1,0:T(8,128)(2,1)S(1)}, bf16[32,1024]{1,0:T(8,128)(2,1)S(1)}, u32[]{:S(2)}, u32[]{:S(2)}) collective-permute-start(bf16[32,1024]{1,0:T(8,128)(2,1)S(1)} %get-tuple-element.20), channel_id=1, source_target_pairs={{0,16},{8,24},{16,0},{24,8},{1,17},{9,25},{17,1},{25,9},{2,18},{10... | collective-permute-start | bytes 196616 | tf_op jit(solution)/shard_map/ppermute | solution.py:429
  17.1 6.2 %collective-permute-start.3 = (bf16[12,1024]{1,0:T(8,128)(2,1)S(1)}, bf16[12,1024]{1,0:T(8,128)(2,1)S(1)}, u32[]{:S(2)}, u32[]{:S(2)}) collective-permute-start(bf16[12,1024]{1,0:T(8,128)(2,1)S(1)} %get-tuple-element.21), channel_id=1, source_target_pairs={{0,8},{8,0},{16,24},{24,16},{1,9},{9,1},{17,25},{25,17},{2,10},{10... | collective-permute-start | bytes 73736 | tf_op jit(solution)/shard_map/ppermute | solution.py:429
  17.1 6.2 %collective-permute-start.4 = (bf16[12,1024]{1,0:T(8,128)(2,1)S(1)}, bf16[12,1024]{1,0:T(8,128)(2,1)S(1)}, u32[]{:S(2)}, u32[]{:S(2)}) collective-permute-start(bf16[12,1024]{1,0:T(8,128)(2,1)S(1)} %get-tuple-element.22), channel_id=1, source_target_pairs={{0,24},{8,16},{16,8},{24,0},{1,25},{9,17},{17,9},{25,1},{2,26},{10... | collective-permute-start | bytes 73736 | tf_op jit(solution)/shard_map/ppermute | solution.py:429
